TPU v7x, 32 devices: a whole 2x2x4 slice. The times are simulated.
32 devices in a mesh: dp: 4 (over y, x), ctx: 2 (over core), tensor: 4 (over z).
Axes of the slice: x: 2, y: 2, z: 4, core: 2. Of those that a mesh axis runs over, the one named last changes fastest.
Arguments:
- block_in: bfloat16 [2048, 4, 1536], P(('ctx', 'tensor'), 'dp'), may hold values from -6 to 6
- cotangent: bfloat16 [2048, 4, 1536], P(('ctx', 'tensor'), 'dp'), may hold values from -6 to 6
- segments: int32 [4, 2048], P('dp', 'ctx'), may hold values from 0 to 7, never falling along the last dimension, each value on 1 to 1024 neighbouring positions
- norm_gain: float32 [1536], replicated, may hold values from 0.5 to 1.5
- inward_weight: float32 [1536, 2, 3072], P(('dp', 'ctx'), None, 'tensor'), may hold values from -0.15625 to 0.15625
- shared_weight: float32 [1536, 304], replicated, may hold values from -0.15625 to 0.15625
- conv_filter: float32 [5, 3328], replicated, may hold values from -3 to 3
- head_params: float32 [3, 48], replicated, may hold values from -12 to 1.5, as said below
- gated_gain: float32 [3072], replicated, may hold values from 0.5 to 1.5
- exit_weight: float32 [1536, 3072], P(('dp', 'ctx'), 'tensor'), may hold values from -0.109375 to 0.109375
- norm_first: float32 [1536], replicated, may hold values from -56 to 56
- norm_second: float32 [1536], replicated, may hold values from 262.144 to 4177.92
- entry_first: float32 [1536, 2, 3072], P(('dp', 'ctx'), None, 'tensor'), may hold values from -56 to 56
- entry_second: float32 [1536, 2, 3072], P(('dp', 'ctx'), None, 'tensor'), may hold values from 262.144 to 4177.92
- shared_first: float32 [1536, 304], replicated, may hold values from -64 to 64
- shared_second: float32 [1536, 304], replicated, may hold values from 311.296 to 4997.12
- filter_first: float32 [5, 3328], replicated, may hold values from -48 to 48
- filter_second: float32 [5, 3328], replicated, may hold values from 180.224 to 2949.12
- head_first: float32 [3, 48], replicated, may hold values from -128 to 128
- head_second: float32 [3, 48], replicated, may hold values from 1638.4 to 26214.4
- gated_first: float32 [3072], replicated, may hold values from -64 to 64
- gated_second: float32 [3072], replicated, may hold values from 425.984 to 6799.36
- exit_first: float32 [1536, 3072], P(('dp', 'ctx'), 'tensor'), may hold values from -112 to 112
- exit_second: float32 [1536, 3072], P(('dp', 'ctx'), 'tensor'), may hold values from 1064.96 to 17203.2
Outputs:
- block_output: bfloat16 [2048, 4, 1536], P(('ctx', 'tensor'), 'dp')
- input_grad: float32 [2048, 4, 1536], P(('ctx', 'tensor'), 'dp')
- norm_grad: float32 [1536], replicated
- norm_new: float32 [1536], replicated
- norm_first_new: float32 [1536], replicated
- norm_second_new: float32 [1536], replicated
- entry_grad: float32 [1536, 2, 3072], P(('dp', 'ctx'), None, 'tensor')
- entry_new: float32 [1536, 2, 3072], P(('dp', 'ctx'), None, 'tensor')
- entry_first_new: float32 [1536, 2, 3072], P(('dp', 'ctx'), None, 'tensor')
- entry_second_new: float32 [1536, 2, 3072], P(('dp', 'ctx'), None, 'tensor')
- shared_grad: float32 [1536, 304], replicated
- shared_new: float32 [1536, 304], replicated
- shared_first_new: float32 [1536, 304], replicated
- shared_second_new: float32 [1536, 304], replicated
- filter_grad: float32 [5, 3328], replicated
- filter_new: float32 [5, 3328], replicated
- filter_first_new: float32 [5, 3328], replicated
- filter_second_new: float32 [5, 3328], replicated
- head_grad: float32 [3, 48], replicated
- head_new: float32 [3, 48], replicated
- head_first_new: float32 [3, 48], replicated
- head_second_new: float32 [3, 48], replicated
- gated_grad: float32 [3072], replicated
- gated_new: float32 [3072], replicated
- gated_first_new: float32 [3072], replicated
- gated_second_new: float32 [3072], replicated
- exit_grad: float32 [1536, 3072], P(('dp', 'ctx'), 'tensor')
- exit_new: float32 [1536, 3072], P(('dp', 'ctx'), 'tensor')
- exit_first_new: float32 [1536, 3072], P(('dp', 'ctx'), 'tensor')
- exit_second_new: float32 [1536, 3072], P(('dp', 'ctx'), 'tensor')
Inputs may be any that keep to these rules, and one draw needn't show every extreme that they name: `segments`: along a sequence the document numbers never fall; a document has 1 to 1024 tokens. `head_params`: row 0 holds each head's step size bias, from -1.5 to 0.5; row 1 the logarithm of its decay rate, from log(0.1 / 2048) to -2.7; row 2 its skip gain, from 0.5 to 1.5.
All inputs are finite; a program needn't handle non-finite values.
Results may differ from a plain program's by a relative error of at most 0.0035.
The roundings to bfloat16 on the way count: a program that leaves them out, or rounds other values in their place, can miss the bound.
Values may be sent and summed in bfloat16 or wider, within the bound.
A program may use at most 256 MiB of HBM per device.

v0:
```python
from functools import partial

import jax
import jax.numpy as jnp
from jax import lax
from jax.sharding import PartitionSpec as P

HEADS = 48
HEAD_DIM = 64
STATE = 128
CONV = 4
SPAN = 256
STEP = 2
DI = 3072


norm_eps = 1e-05
beta_first = 0.9
beta_second = 0.95
adam_eps = 1e-08
rate_matrix = 0.01
rate_vector = 0.4
decay_matrix = 0.1
topmost_precision = lax.Precision.HIGHEST


def from_behind(block, axis, distance):
    devices = range(lax.axis_size(axis))
    route = [(i - distance, i) for i in devices if i - distance in devices]
    return lax.ppermute(block, axis, route)


def entering(value, axis, join, neutral):
    count, mine = (lax.axis_size(axis), lax.axis_index(axis))
    pieces = jax.tree.map(lambda part: lax.all_gather(part, axis), value)
    so_far = jax.tree.map(
        lambda part, zero: jnp.full_like(part, 0) + jnp.asarray(zero, part.dtype), value, neutral
    )

    def entering_step(position, so_far):
        longer = join(so_far, jax.tree.map(lambda part: part[position], pieces))
        return jax.tree.map(lambda new, old: jnp.where(position < mine, new, old), longer, so_far)

    return lax.fori_loop(0, count - 1, entering_step, so_far)


def prefix(array, axis, combine, identity):
    count, position = (lax.axis_size(axis), lax.axis_index(axis))
    everything = jax.tree.map(
        lambda part, kind: lax.all_gather(part.astype(kind), axis),
        array,
        jax.tree.map(lambda a: jnp.bfloat16 if a.dtype == jnp.float32 else a.dtype, array),
    )
    start = jax.tree.map(
        lambda part, zero: jnp.broadcast_to(jnp.asarray(zero, part.dtype), part.shape),
        array,
        identity,
    )

    def prefix_step(k, before):
        at = count - 1 - k
        reached = at > position
        new = combine(
            before, jax.tree.map(lambda part, own: part[at].astype(own.dtype), everything, array)
        )
        return jax.tree.map(lambda a, b: jnp.where(reached, a, b), new, before)

    return lax.fori_loop(0, count, prefix_step, start)


def conv_apply(padded, seg_pad, taps, bias):
    length = padded.shape[0] - (CONV - 1)
    seg_ids = seg_pad[CONV - 1 :]
    total = bias
    for offset in range(CONV):
        same = (seg_pad[offset : offset + length] == seg_ids).astype(jnp.float32)[..., None]
        total = total + taps[offset] * padded[offset : offset + length] * same
    return jax.nn.silu(total)


def span_step(state, pieces):
    values, b_proj, c_proj, delta, logdec, seg_ids, prev_id = pieces
    cumulative = jnp.cumsum(logdec, axis=0)
    length = seg_ids.shape[0]
    order = jnp.arange(length)
    allowed = ((seg_ids[:, None] == seg_ids[None, :]) & (order[:, None] >= order[None, :])).astype(
        jnp.float32
    )
    spread = cumulative[:, None, :] - cumulative[None, :, :]
    kernel = jnp.exp(jnp.where(allowed[..., None] > 0, spread, 0.0)) * allowed[..., None]
    scores = jnp.dot(c_proj, b_proj.T, precision=topmost_precision)
    mixing = scores[..., None] * kernel * delta[None]
    outputs = jnp.einsum("tsh,shp->thp", mixing, values, precision=topmost_precision)
    inflow = (seg_ids == prev_id).astype(jnp.float32)[:, None]
    outputs = (
        outputs
        + jnp.einsum("tn,hpn->thp", c_proj, state, precision=topmost_precision)
        * (jnp.exp(cumulative) * inflow)[..., None]
    )
    keeping = (seg_ids == seg_ids[-1]).astype(jnp.float32)[:, None]
    tail = jnp.exp(cumulative[-1][None] - cumulative) * keeping * delta
    carry_on = jnp.exp(cumulative[-1]) * (seg_ids[-1] == prev_id).astype(jnp.float32)
    new_state = carry_on[:, None, None] * state + jnp.einsum(
        "sh,shp,sn->hpn", tail, values, b_proj, precision=topmost_precision
    )
    return (new_state, outputs)


def local_ssd(values, b_proj, c_proj, delta, logdec, seg_ids, prev_id):
    count = seg_ids.shape[0] // SPAN

    def split(array):
        return array.reshape((count, SPAN) + array.shape[1:])

    seg_blocks = split(seg_ids)
    prev_ids = jnp.concatenate([prev_id[None], seg_blocks[:-1, -1]])
    start = jnp.zeros((values.shape[1], HEAD_DIM, STATE), jnp.float32)
    final, outputs = lax.scan(
        span_step,
        start,
        (
            split(values),
            split(b_proj),
            split(c_proj),
            split(delta),
            split(logdec),
            seg_blocks,
            prev_ids,
        ),
    )
    cumulative = jnp.cumsum(logdec, axis=0)
    through = jnp.exp(cumulative[-1]) * (seg_ids[-1] == prev_id).astype(jnp.float32)
    return (outputs.reshape(values.shape), final, through, cumulative)


def mix_local(seg_pad, padded, delta_raw, conv_own, head_own):
    per_group = delta_raw.shape[-1]
    inner_width = padded.shape[-1] - 2 * STATE
    activated = conv_apply(padded, seg_pad, conv_own[:CONV], conv_own[CONV])
    values = activated[..., :inner_width].reshape(activated.shape[:2] + (per_group, HEAD_DIM))
    b_proj = activated[..., inner_width : inner_width + STATE]
    c_proj = activated[..., inner_width + STATE :]
    delta = jax.nn.softplus(delta_raw + head_own[0])
    logdec = -jnp.exp(head_own[1]) * delta
    scanned = jax.vmap(local_ssd, in_axes=(1, 1, 1, 1, 1, 1, 0), out_axes=(1, 0, 0, 1))
    outputs, final, through, cumulative = scanned(
        values, b_proj, c_proj, delta, logdec, seg_pad[CONV - 1 :], seg_pad[CONV - 2]
    )
    mixed_heads = outputs + head_own[2][:, None] * values
    return (mixed_heads, final, through, c_proj, cumulative)


def carried_part(seg_pad, c_proj, cumulative, incoming):
    inflow = (seg_pad[CONV - 1 :] == seg_pad[CONV - 2][None]).astype(jnp.float32)
    ramp = jnp.exp(cumulative) * inflow[..., None]
    return (
        jnp.einsum("rsn,shpn->rshp", c_proj, incoming, precision=topmost_precision)
        * ramp[..., None]
    )


def chain_combine(earlier, later):
    return (earlier[0] * later[0], later[0][..., None, None] * earlier[1] + later[1])


def silu_slope(value):
    sigma = jax.nn.sigmoid(value)
    return sigma * (1.0 + value * (1.0 - sigma))


def adamw(weight, grad, first, second, rate, decay):
    first_new = beta_first * first + (1.0 - beta_first) * grad
    second_new = beta_second * second + (1.0 - beta_second) * grad * grad
    first_hat = first_new / (1.0 - beta_first**STEP)
    second_hat = second_new / (1.0 - beta_second**STEP)
    weight_new = weight - rate * (first_hat / (jnp.sqrt(second_hat) + adam_eps) + decay * weight)
    return (grad, weight_new, first_new, second_new)


def local(
    block_in,
    cotangent,
    segments,
    norm_gain,
    inward_weight,
    shared_weight,
    conv_filter,
    head_params,
    gated_gain,
    exit_weight,
    norm_first,
    norm_second,
    entry_first,
    entry_second,
    shared_first,
    shared_second,
    filter_first,
    filter_second,
    head_first,
    head_second,
    gated_first,
    gated_second,
    exit_first,
    exit_second,
):
    group = lax.axis_index("tensor")
    groups = lax.axis_size("tensor")
    per_group = HEADS // groups
    inner_width = DI // groups
    inputs = block_in.astype(jnp.float32)
    scale_in = lax.rsqrt(jnp.mean(inputs * inputs, axis=-1, keepdims=True) + norm_eps)
    normalized_input = (inputs * scale_in * norm_gain).astype(jnp.bfloat16)
    entry_complete_matrix, exit_full = (
        lax.all_gather(inward_weight.astype(jnp.bfloat16), ("dp", "ctx"), axis=0, tiled=True),
        lax.all_gather(exit_weight.astype(jnp.bfloat16), ("dp", "ctx"), axis=0, tiled=True),
    )
    normalized_gathered = lax.all_gather(normalized_input, "tensor", axis=0, tiled=True)
    piece_rows = normalized_gathered.shape[0]
    seq_count = normalized_gathered.shape[1]
    inward_projection = jnp.einsum(
        "fon,nmk->fomk",
        normalized_gathered,
        entry_complete_matrix,
        preferred_element_type=jnp.float32,
    )
    gate_in = inward_projection[:, :, 0]
    inner = inward_projection[:, :, 1].astype(jnp.bfloat16)
    shared_bf = shared_weight.astype(jnp.bfloat16)
    shared = jnp.einsum(
        "rsd,dk->rsk", normalized_gathered, shared_bf, preferred_element_type=jnp.float32
    )
    conv_in = jnp.concatenate([inner, shared[..., : 2 * STATE].astype(jnp.bfloat16)], axis=-1)
    delta_raw = lax.dynamic_slice_in_dim(shared[..., 2 * STATE :], group * per_group, per_group, 2)
    seg_rows = segments.T
    edge = piece_rows - (CONV - 1)
    prev_rows, prev_ids = from_behind((conv_in[edge:], seg_rows[edge:]), "ctx", 1)
    padded = jnp.concatenate([prev_rows, conv_in], axis=0).astype(jnp.float32)
    seg_pad = jnp.concatenate([prev_ids, seg_rows], axis=0)
    conv_own = jnp.concatenate(
        [
            lax.dynamic_slice_in_dim(conv_filter[:, :DI], group * inner_width, inner_width, 1),
            conv_filter[:, DI:],
        ],
        axis=1,
    )
    head_own = lax.dynamic_slice_in_dim(head_params, group * per_group, per_group, 1)
    mixer_out, mixer_pull = jax.vjp(
        partial(mix_local, seg_pad), padded, delta_raw, conv_own, head_own
    )
    mixed_local, final, through, c_proj, cumulative = mixer_out
    identity = (jnp.ones_like(through), jnp.zeros_like(final))
    unused_rate, incoming = entering((through, final), "ctx", chain_combine, identity)
    carried, carried_pull = jax.vjp(partial(carried_part, seg_pad), c_proj, cumulative, incoming)
    mixed_heads = (mixed_local + carried).reshape(piece_rows, seq_count, inner_width)
    gate_act = jax.nn.silu(gate_in)
    gated = mixed_heads * gate_act
    total_sq = lax.psum(jnp.sum(gated * gated, axis=-1), "tensor")
    gate_scale = lax.rsqrt(total_sq / DI + norm_eps)[..., None]
    gain_own = lax.dynamic_slice_in_dim(gated_gain, group * inner_width, inner_width)
    gnorm = (gated * gate_scale * gain_own).astype(jnp.bfloat16)
    block_rows = gnorm
    mixed = lax.psum_scatter(
        jnp.einsum("rsi,di->rsd", block_rows, exit_full, preferred_element_type=jnp.float32),
        "tensor",
        scatter_dimension=0,
        tiled=True,
    )
    block_output = (inputs + mixed).astype(jnp.bfloat16)
    entry_pullback_result, exit_back = (
        lax.all_gather(inward_weight.astype(jnp.bfloat16), ("dp", "ctx"), axis=0, tiled=True),
        lax.all_gather(exit_weight.astype(jnp.bfloat16), ("dp", "ctx"), axis=0, tiled=True),
    )
    piece = lax.all_gather(cotangent, "tensor", axis=0, tiled=True)
    block_rows = gnorm
    grad_exit = jnp.einsum("rsd,rsi->di", piece, block_rows, preferred_element_type=jnp.float32)
    grad_rows = jnp.einsum("rsd,di->rsi", piece, exit_back, preferred_element_type=jnp.float32)
    gain_part = jnp.sum(grad_rows * gated * gate_scale, axis=(0, 1))
    weighted = grad_rows * gain_own
    total_dot = lax.psum(jnp.sum(weighted * gated, axis=-1), "tensor")
    d_gated = gate_scale * weighted - gated * gate_scale**3 * (total_dot / DI)[..., None]
    d_mixed = (d_gated * gate_act).reshape(mixed_local.shape)
    d_gate = (d_gated * mixed_heads * silu_slope(gate_in)).astype(jnp.bfloat16)
    d_c_carried, d_cumulative_carried, d_incoming = carried_pull(d_mixed)
    unused_back, state_grad = prefix((through, d_incoming), "ctx", chain_combine, identity)
    d_through = jnp.sum(state_grad * incoming, axis=(2, 3))
    d_padded, d_delta_raw, d_conv_own, d_head_own = mixer_pull(
        (d_mixed, state_grad, d_through, d_c_carried, d_cumulative_carried)
    )
    from_next = from_behind(d_padded[: CONV - 1], "ctx", -1)
    d_conv_in = d_padded[CONV - 1 :]
    d_conv_in = jnp.concatenate([d_conv_in[:edge], d_conv_in[edge:] + from_next], axis=0)
    entry_weight_gradient = jnp.stack(
        [d_gate, d_conv_in[..., :inner_width].astype(jnp.bfloat16)], axis=2
    )
    d_delta_full = lax.dynamic_update_slice_in_dim(
        jnp.zeros((piece_rows, seq_count, HEADS), jnp.float32), d_delta_raw, group * per_group, 2
    )
    d_shared = jnp.concatenate(
        [d_conv_in[..., inner_width:].astype(jnp.bfloat16), d_delta_full.astype(jnp.bfloat16)],
        axis=-1,
    )
    first_term = jnp.einsum(
        "lbxa,jxa->lbj",
        entry_weight_gradient,
        entry_pullback_result,
        preferred_element_type=jnp.float32,
    )
    d_normed = lax.psum_scatter(
        first_term
        + jnp.einsum("rsk,dk->rsd", d_shared, shared_bf, preferred_element_type=jnp.float32),
        "tensor",
        scatter_dimension=0,
        tiled=True,
    )
    entry_part = jnp.einsum(
        "umw,umtg->wtg",
        normalized_gathered,
        entry_weight_gradient,
        preferred_element_type=jnp.float32,
    )
    shared_part = jnp.einsum(
        "rsd,rsk->dk", normalized_gathered, d_shared, preferred_element_type=jnp.float32
    )
    entry_grad, exit_grad = (
        lax.psum_scatter(entry_part, ("dp", "ctx"), scatter_dimension=0, tiled=True),
        lax.psum_scatter(grad_exit, ("dp", "ctx"), scatter_dimension=0, tiled=True),
    )
    d_scaled = d_normed * norm_gain
    norm_part = jnp.sum(d_normed * inputs * scale_in, axis=(0, 1))
    input_grad = (
        cotangent.astype(jnp.float32)
        + scale_in * d_scaled
        - inputs * scale_in**3 * jnp.mean(d_scaled * inputs, axis=-1, keepdims=True)
    )
    filter_inner = lax.dynamic_update_slice_in_dim(
        jnp.zeros((CONV + 1, DI), jnp.float32), d_conv_own[:, :inner_width], group * inner_width, 1
    )
    filter_part = jnp.concatenate([filter_inner, d_conv_own[:, inner_width:]], axis=1)
    head_part = lax.dynamic_update_slice_in_dim(
        jnp.zeros((3, HEADS), jnp.float32), d_head_own, group * per_group, 1
    )
    gated_part = lax.dynamic_update_slice_in_dim(
        jnp.zeros((DI,), jnp.float32), gain_part, group * inner_width, 0
    )
    shared_grad, norm_grad, filter_grad, head_grad, gated_grad = lax.psum(
        (shared_part, norm_part, filter_part, head_part, gated_part), ("dp", "ctx", "tensor")
    )
    norm_set = adamw(norm_gain, norm_grad, norm_first, norm_second, rate_vector, 0.0)
    entry_set = adamw(
        inward_weight, entry_grad, entry_first, entry_second, rate_matrix, decay_matrix
    )
    shared_set = adamw(
        shared_weight, shared_grad, shared_first, shared_second, rate_matrix, decay_matrix
    )
    filter_set = adamw(conv_filter, filter_grad, filter_first, filter_second, rate_vector, 0.0)
    head_set = adamw(head_params, head_grad, head_first, head_second, rate_vector, 0.0)
    gated_set = adamw(gated_gain, gated_grad, gated_first, gated_second, rate_vector, 0.0)
    exit_set = adamw(exit_weight, exit_grad, exit_first, exit_second, rate_matrix, decay_matrix)
    return (
        block_output,
        input_grad,
        norm_set[0],
        norm_set[1],
        norm_set[2],
        norm_set[3],
        entry_set[0],
        entry_set[1],
        entry_set[2],
        entry_set[3],
        shared_set[0],
        shared_set[1],
        shared_set[2],
        shared_set[3],
        filter_set[0],
        filter_set[1],
        filter_set[2],
        filter_set[3],
        head_set[0],
        head_set[1],
        head_set[2],
        head_set[3],
        gated_set[0],
        gated_set[1],
        gated_set[2],
        gated_set[3],
        exit_set[0],
        exit_set[1],
        exit_set[2],
        exit_set[3],
    )


def solution(mesh):
    placed = (
        P(("ctx", "tensor"), "dp", None),
        P(("ctx", "tensor"), "dp", None),
        P("dp", "ctx"),
        P(),
        P(("dp", "ctx"), None, "tensor"),
        P(),
        P(),
        P(),
        P(),
        P(("dp", "ctx"), "tensor"),
        P(),
        P(),
        P(("dp", "ctx"), None, "tensor"),
        P(("dp", "ctx"), None, "tensor"),
        P(),
        P(),
        P(),
        P(),
        P(),
        P(),
        P(),
        P(),
        P(("dp", "ctx"), "tensor"),
        P(("dp", "ctx"), "tensor"),
    )
    return jax.shard_map(
        local,
        mesh=mesh,
        in_specs=placed,
        out_specs=(
            P(("ctx", "tensor"), "dp", None),
            P(("ctx", "tensor"), "dp", None),
            P(),
            P(),
            P(),
            P(),
            P(("dp", "ctx"), None, "tensor"),
            P(("dp", "ctx"), None, "tensor"),
            P(("dp", "ctx"), None, "tensor"),
            P(("dp", "ctx"), None, "tensor"),
            P(),
            P(),
            P(),
            P(),
            P(),
            P(),
            P(),
            P(),
            P(),
            P(),
            P(),
            P(),
            P(),
            P(),
            P(),
            P(),
            P(("dp", "ctx"), "tensor"),
            P(("dp", "ctx"), "tensor"),
            P(("dp", "ctx"), "tensor"),
            P(("dp", "ctx"), "tensor"),
        ),
        check_vma=False,
    )
```

profile of v0, /device:TPU:0, one launch (start us, length us, event | category | flops | bytes accessed | tf_op | source)
XLA Modules:
  0.0 1414.1 jit_solution(14947445549004261948)
XLA Ops:
  28.0 50.5 %all-gather.7.cloned.1.call-done = bf16[1024,1,1536]{2,0,1:T(8,128)(2,1)} async-done(((bf16[256,1,1536]{2,0,1:T(8,128)(2,1)}), bf16[1024,1,1536]{2,0,1:T(8,128)(2,1)}) %all-gather.7.cloned.1.call-update) | async-done | bytes 3145744 | tf_op jit(solution)/shard_map/all_gather | solution.py:217
  82.1 3.4 reduce-window.56
  92.3 26.1 %all-gather.9.cloned.1.call-done = bf16[1536,2,768]{2,0,1:T(8,128)(2,1)} async-done(((bf16[192,2,768]{2,0,1:T(8,128)(2,1)}), bf16[1536,2,768]{2,0,1:T(8,128)(2,1)}) %all-gather.9.cloned.1.call-update) | async-done | bytes 4718608 | tf_op jit(solution)/shard_map/all_gather | solution.py:214
  118.5 8.0 fusion.171
  143.1 4.7 fusion.143
  166.1 307.4 %while.106 = (s32[]{:T(128)}, f32[1,12,64,128]{3,2,1,0:T(8,128)S(1)}, f32[4,1,256,12,64]{2,0,4,3,1:T(4,128)}, pred[4,1,256,256,12]{3,2,4,1,0:T(32,128)(4,1)}, f3...) while((s32[]{:T(128)}, ...), condition=%wide.region_4.5_spmd.clone.clone, body=%wide.region_1.4_spmd.clone.clone.sunk | while | flops 1318765568 | bytes 31186160 | solution.py:118
  189.1 5.3 multiply_dynamic-update-slice_fusion.2
  197.0 4.8 fusion.331
  203.5 17.9 %dynamic_update_slice.296 = f32[4,1,256,12,64]{2,0,4,3,1:T(4,128)} dynamic-update-slice(f32[4,1,256,12,64]{2,0,4,3,1:T(4,128)} %get-tuple-element.2975, f32[1,1,256,12,64]{2,0,4,3,1:T(1,128)} %copy.816, s32[]{:T(128)} %get-tuple-element.2973, s32[]{:T(128)} %constant.322.clone.1..sunk.2, s32[]{:T(128)} %constant.322.clone.1..sunk.2, s32[]{:T(128)} %constant.322.clone.1..sunk.2, ...) | dynamic-update-slice | bytes 1572868 | tf_op jit(solution)/shard_map/jvp(vmap())/while/body/jit(dynamic_update_index_in_dim)/dynamic_update_slice | solution.py:118
  266.0 5.1 multiply_dynamic-update-slice_fusion.2
  273.7 4.8 fusion.331
  280.2 17.9 %dynamic_update_slice.296 = f32[4,1,256,12,64]{2,0,4,3,1:T(4,128)} dynamic-update-slice(f32[4,1,256,12,64]{2,0,4,3,1:T(4,128)} %get-tuple-element.2975, f32[1,1,256,12,64]{2,0,4,3,1:T(1,128)} %copy.816, s32[]{:T(128)} %get-tuple-element.2973, s32[]{:T(128)} %constant.322.clone.1..sunk.2, s32[]{:T(128)} %constant.322.clone.1..sunk.2, s32[]{:T(128)} %constant.322.clone.1..sunk.2, ...) | dynamic-update-slice | bytes 1572868 | tf_op jit(solution)/shard_map/jvp(vmap())/while/body/jit(dynamic_update_index_in_dim)/dynamic_update_slice | solution.py:118
  342.7 5.3 multiply_dynamic-update-slice_fusion.2
  350.6 4.8 fusion.331
  357.1 17.9 %dynamic_update_slice.296 = f32[4,1,256,12,64]{2,0,4,3,1:T(4,128)} dynamic-update-slice(f32[4,1,256,12,64]{2,0,4,3,1:T(4,128)} %get-tuple-element.2975, f32[1,1,256,12,64]{2,0,4,3,1:T(1,128)} %copy.816, s32[]{:T(128)} %get-tuple-element.2973, s32[]{:T(128)} %constant.322.clone.1..sunk.2, s32[]{:T(128)} %constant.322.clone.1..sunk.2, s32[]{:T(128)} %constant.322.clone.1..sunk.2, ...) | dynamic-update-slice | bytes 1572868 | tf_op jit(solution)/shard_map/jvp(vmap())/while/body/jit(dynamic_update_index_in_dim)/dynamic_update_slice | solution.py:118
  419.6 5.1 multiply_dynamic-update-slice_fusion.2
  427.3 4.8 fusion.331
  433.8 17.9 %dynamic_update_slice.296 = f32[4,1,256,12,64]{2,0,4,3,1:T(4,128)} dynamic-update-slice(f32[4,1,256,12,64]{2,0,4,3,1:T(4,128)} %get-tuple-element.2975, f32[1,1,256,12,64]{2,0,4,3,1:T(1,128)} %copy.816, s32[]{:T(128)} %get-tuple-element.2973, s32[]{:T(128)} %constant.322.clone.1..sunk.2, s32[]{:T(128)} %constant.322.clone.1..sunk.2, s32[]{:T(128)} %constant.322.clone.1..sunk.2, ...) | dynamic-update-slice | bytes 1572868 | tf_op jit(solution)/shard_map/jvp(vmap())/while/body/jit(dynamic_update_index_in_dim)/dynamic_update_slice | solution.py:118
  473.5 5.7 transpose.198
  481.6 7.9 multiply_reduce_fusion.7
  491.9 12.1 psum.49
  504.1 8.8 convolution_bitcast_fusion.6
  512.8 6.1 copy.636
  519.0 51.1 %reduce-scatter.13.cloned.1.call-done = f32[192,768]{1,0:T(8,128)} async-done(((f32[1536,768]{1,0:T(8,128)}), f32[192,768]{1,0:T(8,128)}) %reduce-scatter.13.cloned.1.call-update) | async-done | bytes 589840
  570.1 3.5 multiply_subtract_fusion.3
  580.2 22.4 %all-gather.11.cloned.1.call-done = bf16[1536,768]{1,0:T(8,128)(2,1)} async-done(((bf16[192,768]{1,0:T(8,128)(2,1)}), bf16[1536,768]{1,0:T(8,128)(2,1)}) %all-gather.11.cloned.1.call-update) | async-done | bytes 2359312 | tf_op jit(solution)/shard_map/all_gather | solution.py:215
  602.6 9.9 multiply_reduce_fusion.5
  612.5 12.2 psum.50
  625.5 6.2 fusion.144
  634.1 3.4 transpose_reshape.3
  637.5 3.7 fusion.209
  648.9 229.3 %while.104 = (s32[]{:T(128)}, f32[1,12,64,128]{3,2,1,0:T(8,128)S(1)}, f32[4,1,256,12,64]{2,0,4,3,1:T(4,128)}, f32[4,1,256,128]{3,2,1,0:T(8,128)}, f32[4,1,256,12...) while((s32[]{:T(128)}, ...), condition=%wide.region_24.25_spmd, body=%wide.region_14.24_spmd.sunk | while | flops 2628295680 | bytes 34666104 | solution.py:118
  653.6 7.1 fusion.319
  672.9 4.0 fusion.318
  677.7 17.9 %dynamic_update_slice.281 = f32[4,1,256,12,64]{2,0,4,3,1:T(4,128)} dynamic-update-slice(f32[4,1,256,12,64]{2,0,4,3,1:T(4,128)} %get-tuple-element.3107, f32[1,1,256,12,64]{2,0,4,3,1:T(1,128)S(1)} %copy.804, s32[]{:T(128)S(6)} %sub.250, s32[]{:T(128)} %constant.322.clone.1..sunk, s32[]{:T(128)} %constant.322.clone.1..sunk, s32[]{:T(128)} %constant.322.clone.1..sunk, s32[]{:T(128)} %constant.322.clone.1..sunk) | dynamic-update-slice | bytes 1572868 | tf_op jit(solution)/shard_map/transpose(jvp(vmap()))/while/body/jit(dynamic_update_index_in_dim)/dynamic_update_slice | solution.py:118
  701.4 3.2 fusion.320
  710.7 7.1 fusion.319
  730.0 4.0 fusion.318
  734.8 17.9 %dynamic_update_slice.281 = f32[4,1,256,12,64]{2,0,4,3,1:T(4,128)} dynamic-update-slice(f32[4,1,256,12,64]{2,0,4,3,1:T(4,128)} %get-tuple-element.3107, f32[1,1,256,12,64]{2,0,4,3,1:T(1,128)S(1)} %copy.804, s32[]{:T(128)S(6)} %sub.250, s32[]{:T(128)} %constant.322.clone.1..sunk, s32[]{:T(128)} %constant.322.clone.1..sunk, s32[]{:T(128)} %constant.322.clone.1..sunk, s32[]{:T(128)} %constant.322.clone.1..sunk) | dynamic-update-slice | bytes 1572868 | tf_op jit(solution)/shard_map/transpose(jvp(vmap()))/while/body/jit(dynamic_update_index_in_dim)/dynamic_update_slice | solution.py:118
  758.6 3.2 fusion.320
  767.9 7.1 fusion.319
  787.2 4.0 fusion.318
  792.0 17.9 %dynamic_update_slice.281 = f32[4,1,256,12,64]{2,0,4,3,1:T(4,128)} dynamic-update-slice(f32[4,1,256,12,64]{2,0,4,3,1:T(4,128)} %get-tuple-element.3107, f32[1,1,256,12,64]{2,0,4,3,1:T(1,128)S(1)} %copy.804, s32[]{:T(128)S(6)} %sub.250, s32[]{:T(128)} %constant.322.clone.1..sunk, s32[]{:T(128)} %constant.322.clone.1..sunk, s32[]{:T(128)} %constant.322.clone.1..sunk, s32[]{:T(128)} %constant.322.clone.1..sunk) | dynamic-update-slice | bytes 1572868 | tf_op jit(solution)/shard_map/transpose(jvp(vmap()))/while/body/jit(dynamic_update_index_in_dim)/dynamic_update_slice | solution.py:118
  815.7 3.2 fusion.320
  825.1 7.1 fusion.319
  844.4 4.0 fusion.318
  849.2 17.9 %dynamic_update_slice.281 = f32[4,1,256,12,64]{2,0,4,3,1:T(4,128)} dynamic-update-slice(f32[4,1,256,12,64]{2,0,4,3,1:T(4,128)} %get-tuple-element.3107, f32[1,1,256,12,64]{2,0,4,3,1:T(1,128)S(1)} %copy.804, s32[]{:T(128)S(6)} %sub.250, s32[]{:T(128)} %constant.322.clone.1..sunk, s32[]{:T(128)} %constant.322.clone.1..sunk, s32[]{:T(128)} %constant.322.clone.1..sunk, s32[]{:T(128)} %constant.322.clone.1..sunk) | dynamic-update-slice | bytes 1572868 | tf_op jit(solution)/shard_map/transpose(jvp(vmap()))/while/body/jit(dynamic_update_index_in_dim)/dynamic_update_slice | solution.py:118
  878.2 8.1 fusion.204
  888.8 3.7 copy.605
  897.1 4.8 multiply_reduce_fusion.4
  904.8 8.7 pad_add_fusion
  917.6 4.3 fusion.194
  924.5 4.1 pad_add_fusion.1
  928.9 14.9 %reduce-window.58 = f32[12,1,8,128]{3,2,1,0:T(8,128)S(1)} reduce-window(f32[12,1,8,128]{3,2,1,0:T(8,128)S(1)} %copy.608, f32[]{:T(128)} %constant.323.clone.1), window={size=1x1x1x128 pad=0_0x0_0x0_0x0_127}, to_apply=%region_27.28 | reduce-window | flops 1560576 | bytes 98308 | tf_op jit(solution)/shard_map/reduce-window.6
  955.2 8.0 fusion.174
  963.2 4.4 fusion.140
  969.6 6.6 convolution_bitcast_fusion.5
  978.1 9.5 fusion.161
  989.7 97.3 %all-reduce.23.cloned.1.call-done = (f32[1536,304]{0,1:T(8,128)}, f32[5,3328]{1,0:T(8,128)}) async-done(((f32[1536,304]{0,1:T(8,128)}, f32[5,3328]{1,0:T(8,128)}), (f32[1536,304]{0,1:T(8,128)}, f32[5,3328]{1,0:T(8,128)})) %all-reduce.23.cloned.1.call-update) | async-done | bytes 1934352 | tf_op jit(solution)/shard_map/psum | solution.py:345
  1087.1 6.2 multiply_subtract_fusion.1
  1094.1 105.9 %reduce-scatter.9.cloned.1.call-done = f32[256,1,1536]{2,0,1:T(8,128)} async-done(((f32[1024,1,1536]{2,0,1:T(8,128)}), f32[256,1,1536]{2,0,1:T(8,128)}) %reduce-scatter.9.cloned.1.call-update) | async-done | bytes 1572880 | tf_op jit(solution)/shard_map/reduce_scatter | solution.py:308
  1201.9 111.6 %reduce-scatter.7.cloned.1.call-done = f32[256,1,1536]{2,0,1:T(8,128)} async-done(((f32[1024,1,1536]{2,0,1:T(8,128)}), f32[256,1,1536]{2,0,1:T(8,128)}) %reduce-scatter.7.cloned.1.call-update) | async-done | bytes 1572880 | tf_op jit(solution)/shard_map/reduce_scatter | solution.py:262
  1319.3 41.8 %all-reduce.19 = (f32[1536]{0:T(1024)S(1)}, f32[3,48]{1,0:T(4,128)S(1)}, f32[3072]{0:T(1024)S(1)}) all-reduce(f32[1536]{0:T(1024)S(1)} %get-tuple-element.2173, f32[3,48]{1,0:T(4,128)S(1)} %dynamic_update_slice.188, f32[3072]{0:T(1024)S(1)} %dynamic_update_slice.189), channel_id=1, replica_groups=mesh['dp'=4,'ctx'=2,'tensor'=4] {'dp','ctx','tensor'}, use_global_device_ids=true, to_apply=%region_32.33 | all-reduce | flops 4752 | bytes 38016 | tf_op jit(solution)/shard_map/psum | solution.py:345
  1363.0 32.0 %reduce-scatter.11.cloned.1.call-done = f32[192,2,768]{2,0,1:T(8,128)} async-done(((f32[1536,2,768]{2,0,1:T(8,128)}), f32[192,2,768]{2,0,1:T(8,128)}) %reduce-scatter.11.cloned.1.call-update) | async-done | bytes 1179664 | tf_op jit(solution)/shard_map/reduce_scatter | solution.py:325
  (809 shorter events, 436.3 us)
Async XLA Ops:
  7.2 13.3 slice-start.3
  7.2 10.6 copy-start.98
  7.2 71.3 %all-gather.7.cloned.1.call-start = ((), (), s32[]{:S(2)}) async-start(), calls=%async_computation.4 | async-start | bytes 3932160 | tf_op jit(solution)/shard_map/all_gather | solution.py:217
  8.7 13.2 slice-start.4
  8.8 69.8 %copy-start.27 = (f32[1536,304]{0,1:T(8,128)S(1)}, f32[1536,304]{0,1:T(8,128)}, u32[]{:S(2)}) copy-start(f32[1536,304]{0,1:T(8,128)} %param.35) | copy-start | bytes 5603332
  12.2 106.3 %all-gather.9.cloned.1.call-start = ((), (), s32[]{:S(2)}) async-start(), calls=%async_computation.5 | async-start | bytes 5308416 | tf_op jit(solution)/shard_map/all_gather | solution.py:214
  13.2 490.9 %all-gather.13.cloned.1.call-start = ((), (), s32[]{:S(2)}) async-start(), calls=%async_computation.8 | async-start | bytes 3932160 | tf_op jit(solution)/shard_map/all_gather | solution.py:273
  14.0 8.6 collective-permute-start
  16.4 553.7 %reduce-scatter.13.cloned.1.call-start = ((), (), s32[]{:S(2)}) async-start(), calls=%async_computation.11 | async-start | bytes 5308416
  18.5 63.4 %copy-start.101 = (f32[12]{0:T(128)}, f32[12]{0:T(128)S(1)}, u32[]{:S(2)}) copy-start(f32[12]{0:T(128)S(1)} %get-tuple-element.2416) | copy-start | bytes 148
  18.5 63.4 %copy-start.103 = (f32[12]{0:T(128)}, f32[12]{0:T(128)S(1)}, u32[]{:S(2)}) copy-start(f32[12]{0:T(128)S(1)} %get-tuple-element.2417) | copy-start | bytes 148
  22.5 120.4 %copy-start.77 = (f32[1,1024]{1,0:T(1,128)}, f32[1,1024]{1,0:T(1,128)S(1)}, u32[]{:S(2)}) copy-start(f32[1,1024]{1,0:T(1,128)S(1)} %get-tuple-element.2408) | copy-start | bytes 12292
  24.5 61.7 %copy-start.75 = (f32[1,1024]{1,0:T(1,128)}, f32[1,1024]{1,0:T(1,128)S(1)}, u32[]{:S(2)}) copy-start(f32[1,1024]{1,0:T(1,128)S(1)} %compare_convert_fusion.4) | copy-start | bytes 12292
  28.0 115.0 %copy-start.68 = (f32[1024,1]{0,1:T(1,128)}, f32[1024,1]{0,1:T(1,128)S(1)}, u32[]{:S(2)}) copy-start(f32[1024,1]{0,1:T(1,128)S(1)} %get-tuple-element.2412) | copy-start | bytes 12292
  28.0 115.0 %copy-start.70 = (f32[1024,1]{0,1:T(1,128)}, f32[1024,1]{0,1:T(1,128)S(1)}, u32[]{:S(2)}) copy-start(f32[1024,1]{0,1:T(1,128)S(1)} %get-tuple-element.2413) | copy-start | bytes 12292
  28.0 115.0 %copy-start.72 = (f32[1024,1]{0,1:T(1,128)}, f32[1024,1]{0,1:T(1,128)S(1)}, u32[]{:S(2)}) copy-start(f32[1024,1]{0,1:T(1,128)S(1)} %get-tuple-element.2414) | copy-start | bytes 12292
  81.9 47.3 %copy-start.31 = (bf16[1024,1,256]{2,0,1:T(8,128)(2,1)}, bf16[1024,1,256]{2,0,1:T(8,128)(2,1)S(1)}, u32[]{:S(2)}) copy-start(bf16[1024,1,256]{2,0,1:T(8,128)(2,1)S(1)} %copy.571) | copy-start | bytes 1572868
  82.1 52.9 %copy-start.55 = (f32[1024,1,12]{0,2,1:T(8,128)}, f32[1024,1,12]{0,2,1:T(8,128)S(1)}, u32[]{:S(2)}) copy-start(f32[1024,1,12]{0,2,1:T(8,128)S(1)} %get-tuple-element.2368) | copy-start | bytes 147460
  131.0 9.7 collective-permute-start.1
  201.8 19.6 %copy-start.36 = (f32[1,1,256,12]{2,3,1,0:T(8,128)S(1)}, f32[1,1,256,12]{2,3,1,0:T(8,128)}, u32[]{:S(2)}) copy-start(f32[1,1,256,12]{2,3,1,0:T(8,128)} %copy-done.35) | copy-start | bytes 36868 | tf_op jit(solution)/shard_map/jvp(vmap())/while
  222.2 12.7 copy-start.52
  278.5 19.6 %copy-start.36 = (f32[1,1,256,12]{2,3,1,0:T(8,128)S(1)}, f32[1,1,256,12]{2,3,1,0:T(8,128)}, u32[]{:S(2)}) copy-start(f32[1,1,256,12]{2,3,1,0:T(8,128)} %copy-done.35) | copy-start | bytes 36868 | tf_op jit(solution)/shard_map/jvp(vmap())/while
  298.9 12.6 copy-start.52
  355.4 19.6 %copy-start.36 = (f32[1,1,256,12]{2,3,1,0:T(8,128)S(1)}, f32[1,1,256,12]{2,3,1,0:T(8,128)}, u32[]{:S(2)}) copy-start(f32[1,1,256,12]{2,3,1,0:T(8,128)} %copy-done.35) | copy-start | bytes 36868 | tf_op jit(solution)/shard_map/jvp(vmap())/while
  375.8 12.6 copy-start.52
  432.2 19.6 %copy-start.36 = (f32[1,1,256,12]{2,3,1,0:T(8,128)S(1)}, f32[1,1,256,12]{2,3,1,0:T(8,128)}, u32[]{:S(2)}) copy-start(f32[1,1,256,12]{2,3,1,0:T(8,128)} %copy-done.35) | copy-start | bytes 36868 | tf_op jit(solution)/shard_map/jvp(vmap())/while
  452.5 12.6 copy-start.52
  489.5 14.6 %copy-start.85 = (f32[768]{0:T(1024)S(1)}, f32[768]{0:T(1024)}, u32[]{:S(2)}) copy-start(f32[768]{0:T(1024)} %dynamic_slice.339) | copy-start | bytes 9220
  518.9 83.7 %all-gather.11.cloned.1.call-start = ((), (), s32[]{:S(2)}) async-start(), calls=%async_computation.6 | async-start | bytes 2654208 | tf_op jit(solution)/shard_map/all_gather | solution.py:215
  573.6 513.4 %all-reduce.23.cloned.1.call-start = ((), (), s32[]{:S(2)}) async-start(), calls=%async_computation.12 | async-start | bytes 3948544 | tf_op jit(solution)/shard_map/psum | solution.py:345
  612.5 19.2 %copy-start.18 = (f32[1024,768]{1,0:T(8,128)}, f32[1024,768]{1,0:T(8,128)S(1)}, u32[]{:S(2)}) copy-start(f32[1024,768]{1,0:T(8,128)S(1)} %get-tuple-element.2358) | copy-start | bytes 9437188
  648.8 229.3 %copy-start.54 = (f32[1024,12]{0,1:T(8,128)S(1)}, f32[1024,12]{0,1:T(8,128)}, u32[]{:S(2)}) copy-start(f32[1024,12]{0,1:T(8,128)} %copy.584) | copy-start | bytes 147460
  648.8 229.3 %copy-start.112 = (f32[12]{0:T(128)S(1)}, f32[12]{0:T(128)}, u32[]{:S(2)}) copy-start(f32[12]{0:T(128)} %fusion.241) | copy-start | bytes 148
  878.1 10.6 copy-start.61
  878.1 10.6 copy-start.63
  922.0 27.3 %collective-permute-start.2 = (f32[3,1,1024]{2,0,1:T(4,128)S(1)}, f32[3,1,1024]{2,0,1:T(4,128)S(1)}, u32[]{:S(2)}, u32[]{:S(2)}) collective-permute-start(f32[3,1,1024]{2,0,1:T(4,128)S(1)} %pad_add_fusion.2), channel_id=1, source_target_pairs={{4,0},{5,1},{6,2},{7,3},{12,8},{13,9},{14,10},{15,11},{20,16},{21,... | collective-permute-start | bytes 36872 | tf_op jit(solution)/shard_map/ppermute | solution.py:30
  923.4 20.7 %copy-start.64 = (f32[4,1,256,12]{2,0,1,3:T(4,128)S(1)}, f32[4,1,256,12]{2,0,1,3:T(4,128)}, u32[]{:S(2)}) copy-start(f32[4,1,256,12]{2,0,1,3:T(4,128)} %copy-done.63) | copy-start | bytes 147460
  924.2 19.9 %copy-start.62 = (f32[4,1,256,12]{2,0,3,1:T(4,128)S(1)}, f32[4,1,256,12]{2,0,3,1:T(4,128)}, u32[]{:S(2)}) copy-start(f32[4,1,256,12]{2,0,3,1:T(4,128)} %copy-done.61) | copy-start | bytes 147460
  924.3 20.6 %copy-start.56 = (f32[1024,1,12]{0,2,1:T(8,128)S(1)}, f32[1024,1,12]{0,2,1:T(8,128)}, u32[]{:S(2)}) copy-start(f32[1024,1,12]{0,2,1:T(8,128)} %copy-done.55) | copy-start | bytes 147460
  924.3 20.6 %copy-start.102 = (f32[12]{0:T(128)S(1)}, f32[12]{0:T(128)}, u32[]{:S(2)}) copy-start(f32[12]{0:T(128)} %copy-done.101) | copy-start | bytes 148
  924.3 20.6 %copy-start.104 = (f32[12]{0:T(128)S(1)}, f32[12]{0:T(128)}, u32[]{:S(2)}) copy-start(f32[12]{0:T(128)} %copy-done.103) | copy-start | bytes 148
  955.1 244.8 %reduce-scatter.9.cloned.1.call-start = ((), (), s32[]{:S(2)}) async-start(), calls=%async_computation.9 | async-start | bytes 7864320 | tf_op jit(solution)/shard_map/reduce_scatter | solution.py:308
  967.7 345.9 %reduce-scatter.7.cloned.1.call-start = ((), (), s32[]{:S(2)}) async-start(), calls=%async_computation.7 | async-start | bytes 7864320 | tf_op jit(solution)/shard_map/reduce_scatter | solution.py:262
  976.2 418.7 %reduce-scatter.11.cloned.1.call-start = ((), (), s32[]{:S(2)}) async-start(), calls=%async_computation.10 | async-start | bytes 10616832 | tf_op jit(solution)/shard_map/reduce_scatter | solution.py:325
  987.6 99.4 %copy-start.29 = (f32[1536,304]{0,1:T(8,128)S(1)}, f32[1536,304]{0,1:T(8,128)}, u32[]{:S(2)}) copy-start(f32[1536,304]{0,1:T(8,128)} %param.35) | copy-start | bytes 5603332
  1087.0 112.9 %copy-start.24 = (bf16[256,1,1536]{2,0,1:T(8,128)(2,1)S(1)}, bf16[256,1,1536]{2,0,1:T(8,128)(2,1)}, u32[]{:S(2)}) copy-start(bf16[256,1,1536]{2,0,1:T(8,128)(2,1)} %param.30) | copy-start | bytes 2359300
  1087.0 112.9 %copy-start.65 = (f32[1536]{0:T(1024)S(1)}, f32[1536]{0:T(1024)}, u32[]{:S(2)}) copy-start(f32[1536]{0:T(1024)} %param.33) | copy-start | bytes 18436
  1087.0 112.9 %copy-start.91 = (f32[256]{0:T(256)S(1)}, f32[256]{0:T(256)}, u32[]{:S(2)}) copy-start(f32[256]{0:T(256)} %copy-done.90) | copy-start | bytes 3076
  1087.1 226.5 %copy-start.105 = (f32[256]{0:T(256)S(1)}, f32[256]{0:T(256)}, u32[]{:S(2)}) copy-start(f32[256]{0:T(256)} %get-tuple-element.2418) | copy-start | bytes 3076
  1093.3 220.3 %copy-start.37 = (bf16[256,1,1536]{2,0,1:T(8,128)(2,1)S(1)}, bf16[256,1,1536]{2,0,1:T(8,128)(2,1)}, u32[]{:S(2)}) copy-start(bf16[256,1,1536]{2,0,1:T(8,128)(2,1)} %param.31) | copy-start | bytes 2359300
  1200.0 113.6 %copy-start.30 = (f32[256,1,1536]{2,0,1:T(8,128)S(1)}, f32[256,1,1536]{2,0,1:T(8,128)}, u32[]{:S(2)}) copy-start(f32[256,1,1536]{2,0,1:T(8,128)} %reduce-scatter.9.cloned.1.call-done) | copy-start | bytes 4718596
  1316.4 44.7 %copy-start.99 = (f32[3,48]{1,0:T(4,128)S(1)}, f32[3,48]{1,0:T(4,128)}, u32[]{:S(2)}) copy-start(f32[3,48]{1,0:T(4,128)} %param.37) | copy-start | bytes 1732
  1316.4 44.7 %copy-start.107 = (f32[3,48]{1,0:T(4,128)S(1)}, f32[3,48]{1,0:T(4,128)}, u32[]{:S(2)}) copy-start(f32[3,48]{1,0:T(4,128)} %param.48) | copy-start | bytes 1732
  1316.4 44.7 %copy-start.108 = (f32[3,48]{1,0:T(4,128)S(1)}, f32[3,48]{1,0:T(4,128)}, u32[]{:S(2)}) copy-start(f32[3,48]{1,0:T(4,128)} %param.49) | copy-start | bytes 1732
  1316.4 45.3 %copy-start.95 = (f32[1536]{0:T(1024)S(1)}, f32[1536]{0:T(1024)}, u32[]{:S(2)}) copy-start(f32[1536]{0:T(1024)} %param.40) | copy-start | bytes 18436
  1316.4 45.3 %copy-start.96 = (f32[1536]{0:T(1024)S(1)}, f32[1536]{0:T(1024)}, u32[]{:S(2)}) copy-start(f32[1536]{0:T(1024)} %param.41) | copy-start | bytes 18436
  1316.5 45.9 %copy-start.86 = (f32[3072]{0:T(1024)S(1)}, f32[3072]{0:T(1024)}, u32[]{:S(2)}) copy-start(f32[3072]{0:T(1024)} %param.38) | copy-start | bytes 36868
  1316.5 45.9 %copy-start.92 = (f32[3072]{0:T(1024)S(1)}, f32[3072]{0:T(1024)}, u32[]{:S(2)}) copy-start(f32[3072]{0:T(1024)} %param.50) | copy-start | bytes 36868
  1316.5 45.9 %copy-start.93 = (f32[3072]{0:T(1024)S(1)}, f32[3072]{0:T(1024)}, u32[]{:S(2)}) copy-start(f32[3072]{0:T(1024)} %param.51) | copy-start | bytes 36868
  1316.5 78.5 %copy-start.33 = (f32[192,2,768]{2,1,0:T(2,128)S(1)}, f32[192,2,768]{2,1,0:T(2,128)}, u32[]{:S(2)}) copy-start(f32[192,2,768]{2,1,0:T(2,128)} %param.34) | copy-start | bytes 3538948
  1316.5 78.5 %copy-start.53 = (f32[192,2,768]{2,1,0:T(2,128)S(1)}, f32[192,2,768]{2,1,0:T(2,128)}, u32[]{:S(2)}) copy-start(f32[192,2,768]{2,1,0:T(2,128)} %param.42) | copy-start | bytes 3538948
  1361.1 36.4 %copy-start.94 = (f32[3072]{0:T(1024)}, f32[3072]{0:T(1024)S(1)}, u32[]{:S(2)}) copy-start(f32[3072]{0:T(1024)S(1)} %get-tuple-element.3203) | copy-start | bytes 36868
  1361.1 36.4 %copy-start.97 = (f32[1536]{0:T(1024)}, f32[1536]{0:T(1024)S(1)}, u32[]{:S(2)}) copy-start(f32[1536]{0:T(1024)S(1)} %get-tuple-element.3183) | copy-start | bytes 18436
  1361.1 36.4 %copy-start.109 = (f32[3,48]{1,0:T(4,128)}, f32[3,48]{1,0:T(4,128)S(1)}, u32[]{:S(2)}) copy-start(f32[3,48]{1,0:T(4,128)S(1)} %get-tuple-element.3199) | copy-start | bytes 1732
  (105 other events, 497.7 us)
Sparse Core Ops, SparseCore 0:
  12.3 66.1 all-gather.6
  81.0 37.4 all-gather.8
  120.0 63.4 all-gather.12
  519.0 51.0 reduce-scatter.12
  573.7 28.8 all-gather.10
  955.3 131.6 all-reduce.22
  1089.3 110.5 reduce-scatter.8
  1202.2 111.2 reduce-scatter.6
  1317.1 77.8 reduce-scatter.10
where the time goes:
time: 1430 us; the launch traced here: 1410 us
  waiting for transfers between devices  497 us (35%)
  local copies, waits for them, and re-layouts  390 us (27%)
  matrix products  215 us (15%)
  other arithmetic  206 us (14%)
  blocking collectives  75.2 us (5%)
  between operations  17.2 us (1%)
    dynamic_update_slice x72, local copies, waits for them, and re-layouts, local_ssd(): lax.scan(span_step, start, (split(values), split(b_proj), split(c_proj),...  218 us
    reduce_scatter x1, waiting for transfers between devices, local(): lax.psum_scatter(jnp.einsum('rsi,di->rsd', block_rows, exit_full, preferr...  112 us
    reduce_scatter x1, waiting for transfers between devices, local(): lax.psum_scatter(first_term + jnp.einsum('rsk,dk->rsd', d_shared, shared_...  106 us
    psum x1, waiting for transfers between devices, local(): lax.psum((shared_part, norm_part, filter_part, head_part, gated_part), ('...  97.3 us
    dot_general x12, matrix products, span_step(): jnp.einsum('tsh,shp->thp', mixing, values, precision=topmost_precision)  63.5 us
    unnamed x10, waiting for transfers between devices  51.3 us
    all_gather x1, waiting for transfers between devices, local(): lax.all_gather(normalized_input, 'tensor', axis=0, tiled=True)  50.5 us
    unnamed x228, local copies, waits for them, and re-layouts  43.8 us
  transfers between devices with their start and end apart: 12, of which 8 were waited for; matrix products, arithmetic and copies ran while one was open for 32% of the time, Pallas kernels for 0%

commit v1 on v0

v1 whole, which is shorter than its diff:
```python
import functools

import jax
import jax.numpy as jnp
from jax import lax
from jax.experimental import pallas as pl
from jax.experimental.pallas import tpu as pltpu
from jax.sharding import PartitionSpec as P

HEADS = 48
HEAD_DIM = 64
STATE = 128
CONV = 4
STEP = 2
DI = 3072
CHUNK = 128
LANES = 128

norm_eps = 1e-05
beta_first = 0.9
beta_second = 0.95
adam_eps = 1e-08
rate_matrix = 0.01
rate_vector = 0.4
decay_matrix = 0.1

MESH = pl.DeviceIdType.MESH
f32 = jnp.float32
bf16 = jnp.bfloat16
NT = (((1,), (1,)), ((), ()))
NEG = -1e30


def pick(index, table):
    out = jnp.int32(table[0])
    for i, v in enumerate(table[1:], 1):
        out = jnp.where(index == i, jnp.int32(v), out)
    return out


def gather_kernel(n_dp, n_ctx, n_z, ring, zc, n_ref, w_ref, nf, wf, halo, *sems):
    z_send, z_recv, d_send, d_recv, c_send, c_recv, h_sem, l_sem = sems
    z, d, c = lax.axis_index("tensor"), lax.axis_index("dp"), lax.axis_index("ctx")
    pos = pick(d, [ring.index(i) for i in range(n_dp)])
    nxt = pick(lax.rem(pos + 1, n_dp), ring)
    prv = pick(lax.rem(pos + n_dp - 1, n_dp), ring)
    c_next, c_prev = lax.rem(c + 1, n_ctx), lax.rem(c + n_ctx - 1, n_ctx)
    rows, wr = n_ref.shape[0], w_ref.shape[0]
    half, zr = wr // 2, rows // zc
    bar = pltpu.get_barrier_semaphore()

    @pl.when(z > 0)
    def _():
        pl.semaphore_signal(bar, device_id={"tensor": z - 1}, device_id_type=MESH)

    @pl.when(z < n_z - 1)
    def _():
        pl.semaphore_signal(bar, device_id={"tensor": z + 1}, device_id_type=MESH)

    pl.semaphore_signal(bar, device_id={"dp": nxt}, device_id_type=MESH)
    pl.semaphore_signal(bar, device_id={"dp": prv}, device_id_type=MESH)
    pl.semaphore_signal(bar, device_id={"ctx": c_prev}, device_id_type=MESH)
    if n_ctx > 2:
        pl.semaphore_signal(bar, device_id={"ctx": c_next}, device_id_type=MESH)
    extra = 3 if n_ctx == 2 else 4

    @pl.when((z > 0) & (z < n_z - 1))
    def _():
        pl.semaphore_wait(bar, extra + 2)

    @pl.when((z == 0) | (z == n_z - 1))
    def _():
        pl.semaphore_wait(bar, extra + 1)

    def zcopy(src, k, to, first, way):
        here = nf.at[pl.ds(src * rows + k * zr, zr)]
        return pltpu.make_async_remote_copy(
            n_ref.at[pl.ds(k * zr, zr)] if first else here,
            here,
            z_send.at[way, src, k],
            z_recv.at[src, k],
            device_id={"tensor": to},
            device_id_type=MESH,
        )

    def wpart(cc, dd, h):
        return wf.at[pl.ds((dd * n_ctx + cc) * wr + h * half, half)]

    def dcopy(sp, h, first):
        here = wpart(c, pick(sp, ring), h)
        return pltpu.make_async_remote_copy(
            w_ref.at[pl.ds(h * half, half)] if first else here,
            here,
            d_send.at[sp, h],
            d_recv.at[sp, h],
            device_id={"dp": nxt if h == 0 else prv},
            device_id_type=MESH,
        )

    def ccopy(cc, dd, h, first):
        here = wpart(cc, dd, h)
        return pltpu.make_async_remote_copy(
            w_ref.at[pl.ds(h * half, half)] if first else here,
            here,
            c_send.at[cc, dd, h],
            c_recv.at[cc, dd, h],
            device_id={"ctx": c_next},
            device_id_type=MESH,
        )

    def ring_pos(dist, h):
        return lax.rem(pos + (n_dp - dist if h == 0 else dist), n_dp)

    for k in range(zc):

        @pl.when(z < n_z - 1)
        def _(k=k):
            zcopy(z, k, z + 1, True, 0).start()

        @pl.when(z > 0)
        def _(k=k):
            zcopy(z, k, z - 1, True, 1).start()

        if k == 0:
            for h in range(2):
                dcopy(pos, h, True).start()
            for h in range(2):
                ccopy(c, d, h, True).start()
            own_w = pltpu.make_async_copy(
                w_ref, wf.at[pl.ds((d * n_ctx + c) * wr, wr)], l_sem.at[0]
            )
            own_n = pltpu.make_async_copy(n_ref, nf.at[pl.ds(z * rows, rows)], l_sem.at[1])
            own_w.start()
            own_n.start()
    for dist in range(1, max(n_z, n_dp)):
        for k in range(zc):
            if dist < n_z:

                @pl.when(z >= dist)
                def _(k=k, dist=dist):
                    zcopy(z - dist, k, z, False, 0).wait_recv()

                    @pl.when(z < n_z - 1)
                    def _():
                        zcopy(z - dist, k, z + 1, False, 0).start()

                @pl.when(z + dist < n_z)
                def _(k=k, dist=dist):
                    zcopy(z + dist, k, z, False, 1).wait_recv()

                    @pl.when(z > 0)
                    def _():
                        zcopy(z + dist, k, z - 1, False, 1).start()

            if k == 0 and dist < n_dp:
                for h in range(2):
                    sp = ring_pos(dist, h)
                    dcopy(sp, h, False).wait_recv()
                    if dist < n_dp - 1:
                        dcopy(sp, h, False).start()
                    ccopy(c, pick(sp, ring), h, False).start()
    own_n.wait()
    own_w.wait()
    edge = pltpu.make_async_remote_copy(
        nf.at[pl.ds(n_z * rows - halo.shape[0], halo.shape[0])],
        halo,
        h_sem.at[0],
        h_sem.at[1],
        device_id={"ctx": c_next},
        device_id_type=MESH,
    )
    edge.start()
    for step in range(1, n_ctx):
        cc = lax.rem(c + n_ctx - step, n_ctx)
        for dist in range(n_dp):
            for h in range(2):
                dd = pick(ring_pos(dist, h), ring)
                ccopy(cc, dd, h, False).wait_recv()
                if step < n_ctx - 1:
                    ccopy(cc, dd, h, False).start()
    edge.wait()
    for k in range(zc):
        for dist in range(n_z):

            @pl.when((z >= dist) & (z < n_z - 1))
            def _(k=k, dist=dist):
                zcopy(z - dist, k, z + 1, dist == 0, 0).wait_send()

            @pl.when((z + dist < n_z) & (z > 0))
            def _(k=k, dist=dist):
                zcopy(z + dist, k, z - 1, dist == 0, 1).wait_send()

    for dist in range(n_dp):
        for h in range(2):
            sp = ring_pos(dist, h)
            if dist < n_dp - 1:
                dcopy(sp, h, dist == 0).wait_send()
            for step in range(n_ctx - 1):
                cc = lax.rem(c + n_ctx - step, n_ctx)
                ccopy(cc, pick(sp, ring), h, dist == 0 and step == 0).wait_send()


def gather_all(dims, normed, weights):
    n_dp, n_ctx, n_z, ring = dims
    rows, width = normed.shape
    wr, wc = weights.shape
    zc = 2
    dma = pltpu.SemaphoreType.DMA
    return pl.pallas_call(
        functools.partial(gather_kernel, n_dp, n_ctx, n_z, ring, zc),
        out_shape=(
            jax.ShapeDtypeStruct((rows * n_z, width), normed.dtype),
            jax.ShapeDtypeStruct((wr * n_dp * n_ctx, wc), weights.dtype),
            jax.ShapeDtypeStruct((16, width), normed.dtype),
        ),
        in_specs=[pl.BlockSpec(memory_space=pltpu.VMEM)] * 2,
        out_specs=tuple([pl.BlockSpec(memory_space=pl.ANY)] * 3),
        scratch_shapes=[
            dma((2, n_z, zc)),
            dma((n_z, zc)),
            dma((n_dp, 2)),
            dma((n_dp, 2)),
            dma((n_ctx, n_dp, 2)),
            dma((n_ctx, n_dp, 2)),
            dma((2,)),
            dma((2,)),
        ],
        compiler_params=pltpu.CompilerParams(collective_id=0, has_side_effects=True),
        name="gather_all",
    )(normed, weights)


def all_sum_kernel(n_z, x_ref, o_ref, land, send, recv):
    z = lax.axis_index("tensor")
    bar = pltpu.get_barrier_semaphore()
    for k in range(1, n_z):
        pl.semaphore_signal(
            bar, device_id={"tensor": lax.rem(z + k, n_z)}, device_id_type=MESH
        )
    pl.semaphore_wait(bar, n_z - 1)
    copies = []
    for k in range(1, n_z):
        copy = pltpu.make_async_remote_copy(
            x_ref,
            land.at[k - 1],
            send.at[k - 1],
            recv.at[k - 1],
            device_id={"tensor": lax.rem(z + k, n_z)},
            device_id_type=MESH,
        )
        copy.start()
        copies.append(copy)
    for copy in copies:
        copy.wait()
    total = x_ref[...]
    for k in range(1, n_z):
        total = total + land[k - 1]
    o_ref[...] = total


def all_sum(n_z, collective_id, x):
    return pl.pallas_call(
        functools.partial(all_sum_kernel, n_z),
        out_shape=jax.ShapeDtypeStruct(x.shape, x.dtype),
        in_specs=[pl.BlockSpec(memory_space=pltpu.VMEM)],
        out_specs=pl.BlockSpec(memory_space=pltpu.VMEM),
        scratch_shapes=[
            pltpu.VMEM((n_z - 1,) + x.shape, x.dtype),
            pltpu.SemaphoreType.DMA((n_z - 1,)),
            pltpu.SemaphoreType.DMA((n_z - 1,)),
        ],
        compiler_params=pltpu.CompilerParams(collective_id=collective_id, has_side_effects=True),
        name="all_sum",
    )(x)


def split2(a):
    hi = a.astype(bf16)
    return hi, (a - hi.astype(f32)).astype(bf16)


def split3(a):
    hi = a.astype(bf16)
    rest = a - hi.astype(f32)
    mid = rest.astype(bf16)
    return hi, mid, (rest - mid.astype(f32)).astype(bf16)


def dot(a, b):
    return jnp.dot(a, b, preferred_element_type=f32)


def dot_nt(a, b):
    return lax.dot_general(a, b, NT, preferred_element_type=f32)


def lhs3(hi, lo):
    return jnp.concatenate([hi, lo, hi], axis=1)


def rhs3(hi, lo):
    return jnp.concatenate([hi, hi, lo], axis=0)


def rhs3_nt(hi, lo):
    return jnp.concatenate([hi, hi, lo], axis=1)


def left_half(shape):
    return lax.broadcasted_iota(jnp.int32, shape, 1) < HEAD_DIM


def expand(v, j):
    shape = (v.shape[0], LANES)
    return jnp.where(
        left_half(shape),
        jnp.broadcast_to(v[:, 2 * j : 2 * j + 1], shape),
        jnp.broadcast_to(v[:, 2 * j + 1 : 2 * j + 2], shape),
    )


def halves(a):
    keep = left_half(a.shape)
    return jnp.where(keep, a, 0.0), jnp.where(keep, 0.0, a)


def column(row):
    return jnp.broadcast_to(row, (LANES, LANES)).T


def ordered(length=CHUNK):
    r = lax.broadcasted_iota(jnp.int32, (length, length), 0)
    c = lax.broadcasted_iota(jnp.int32, (length, length), 1)
    return r, c


def fold8(a):
    out = a[0:8]
    for k in range(8, a.shape[0], 8):
        out = out + a[k : k + 8]
    return out


def head_columns(j):
    r, c = ordered(LANES)
    return jnp.where(c == 2 * j + jnp.where(r < HEAD_DIM, 0, 1), 1.0, 0.0).astype(bf16)


def sigmoid(x):
    return 1.0 / (1.0 + jnp.exp(-x))


def entry_kernel(
    nc,
    n_ref,
    w_ref,
    ws_ref,
    halo_ref,
    tok_ref,
    flag_ref,
    par_ref,
    cf_ref,
    gate_ref,
    v_ref,
    u_ref,
    act_ref,
    del_ref,
    cum_ref,
    sig_ref,
    s0_ref,
    fin_ref,
    thr_ref,
    vh_ref,
    vbuf,
    state,
    total,
):
    i = pl.program_id(0)
    rows = n_ref.shape[0]
    width = gate_ref.shape[1]
    cols = v_ref.shape[1]

    @pl.when(i == 0)
    def _():
        hv = jnp.concatenate(
            [dot(halo_ref[...], w_ref[:, width:]), dot(halo_ref[...], ws_ref[:, : 2 * STATE])],
            axis=1,
        )
        hv = hv.astype(bf16).astype(f32) * par_ref[3:4, 0:1]
        vbuf[0:8] = hv[8:16]
        vh_ref[...] = hv[8:16]
        state[...] = jnp.zeros_like(state)
        total[...] = jnp.zeros_like(total)

    @pl.when(i > 0)
    def _():
        vbuf[0:8] = vbuf[rows : rows + 8]

    n = n_ref[...]
    gate_ref[...] = dot(n, w_ref[:, :width])
    vi = dot(n, w_ref[:, width:]).astype(bf16)
    v_ref[:, :width] = vi
    vbuf[8 : rows + 8, :width] = vi.astype(f32)
    sh = dot(n, ws_ref[...])
    vb = sh[:, : 2 * STATE].astype(bf16)
    v_ref[:, width:] = vb
    vbuf[8 : rows + 8, width:] = vb.astype(f32)
    raw = sh[:, 2 * STATE :] + par_ref[0:1, :]
    delta = jnp.maximum(raw, 0.0) + jnp.log1p(jnp.exp(-jnp.abs(raw)))
    del_ref[...] = delta
    sig_ref[...] = sigmoid(raw)
    logdec = par_ref[1:2, :] * delta

    masks = [jnp.broadcast_to(tok_ref[:, k : k + 1], (rows, LANES)) for k in range(3)]
    for j in range(cols // LANES):
        cs = slice(j * LANES, (j + 1) * LANES)
        u = cf_ref[4:5, cs] + cf_ref[3:4, cs] * vbuf[8 : 8 + rows, cs]
        for k in range(3):
            u = u + cf_ref[k : k + 1, cs] * vbuf[5 + k : 5 + k + rows, cs] * masks[k]
        u_ref[:, cs] = u
        act_ref[:, cs] = u * sigmoid(u)

    r, c = ordered()
    tri = jnp.where(r >= c, 1.0, 0.0).astype(bf16)
    tri3 = jnp.concatenate([tri, tri, tri], axis=1)
    for k in range(rows // CHUNK):
        ts = slice(k * CHUNK, (k + 1) * CHUNK)
        chunk = i * (rows // CHUNK) + k
        cum = dot(tri3, jnp.concatenate(split3(logdec[ts]), axis=0))
        cum_ref[ts] = cum
        last = cum[CHUNK - 1 : CHUNK]
        weight = jnp.exp(last - cum) * tok_ref[ts, 3:4] * delta[ts]
        carry = jnp.exp(last) * flag_ref[pl.ds(chunk, 1), :]
        thr_ref[pl.ds(chunk, 1), :] = jnp.exp(total[0:1]) * flag_ref[pl.ds(nc + chunk, 1), :]
        total[0:1] = total[0:1] + last
        bt = lhs3(*split2(act_ref[ts, width : width + STATE].T))
        for j in range(width // LANES):
            cs = slice(j * LANES, (j + 1) * LANES)
            s0_ref[k, :, cs] = state[:, cs]
            xw = act_ref[ts, cs] * expand(weight, j)
            state[:, cs] = state[:, cs] * expand(carry, j) + dot(bt, rhs3(*split2(xw)))

    @pl.when(i == pl.num_programs(0) - 1)
    def _():
        thr_ref[nc : nc + 8, :] = jnp.broadcast_to(
            jnp.exp(total[0:1]) * flag_ref[3 * nc : 3 * nc + 1, :], (8, LANES)
        )
        fin_ref[...] = state[...]


def run_entry(normed, weights, shared_ext, halo, tok, flags, par, cf, width):
    tokens, d = normed.shape
    rows = 256
    nc = tokens // CHUNK
    cols = width + 2 * STATE
    one = pl.Buffered(1)

    def whole(shape):
        return pl.BlockSpec(shape, lambda i: (0,) * len(shape), pipeline_mode=one)

    def by_row(w):
        return pl.BlockSpec((rows, w), lambda i: (i, 0))

    def out(shape, dt=f32):
        return jax.ShapeDtypeStruct(shape, dt)

    return pl.pallas_call(
        functools.partial(entry_kernel, nc),
        grid=(tokens // rows,),
        in_specs=[
            by_row(d),
            whole((d, 2 * width)),
            whole(shared_ext.shape),
            whole(halo.shape),
            by_row(tok.shape[1]),
            whole(flags.shape),
            whole(par.shape),
            whole(cf.shape),
        ],
        out_specs=(
            by_row(width),
            by_row(cols),
            by_row(cols),
            by_row(cols),
            by_row(LANES),
            by_row(LANES),
            by_row(LANES),
            pl.BlockSpec((rows // CHUNK, STATE, width), lambda i: (i, 0, 0)),
            whole((STATE, width)),
            whole((nc + 8, LANES)),
            whole((8, cols)),
        ),
        out_shape=(
            out((tokens, width)),
            out((tokens, cols), bf16),
            out((tokens, cols)),
            out((tokens, cols)),
            out((tokens, LANES)),
            out((tokens, LANES)),
            out((tokens, LANES)),
            out((nc, STATE, width)),
            out((STATE, width)),
            out((nc + 8, LANES)),
            out((8, cols)),
        ),
        scratch_shapes=[
            pltpu.VMEM((rows + 8, cols), f32),
            pltpu.VMEM((STATE, width), f32),
            pltpu.VMEM((8, LANES), f32),
        ],
        compiler_params=pltpu.CompilerParams(dimension_semantics=("arbitrary",)),
        name="entry",
    )(normed, weights, shared_ext, halo, tok, flags, par, cf)


def mix_kernel(
    act_ref,
    del_ref,
    cum_ref,
    tok_ref,
    segr_ref,
    s0_ref,
    sin_ref,
    thr_ref,
    gate_ref,
    gain_ref,
    mixed_ref,
    sq_ref,
):
    chunk = pl.program_id(0)
    width = gate_ref.shape[1]
    b = act_ref[:, width : width + STATE]
    c = act_ref[:, width + STATE :]
    bh, bl = split2(b)
    ch, cl = split2(c)
    c3 = lhs3(ch, cl)
    scores = dot_nt(c3, rhs3_nt(bh, bl))
    cum = cum_ref[...]
    cum_t = cum.T
    r, s = ordered()
    same = tok_ref[:, 5:6] == segr_ref[pl.ds(chunk, 1), :]
    bias = jnp.where(same & (r >= s), 0.0, NEG)
    delta = del_ref[...]
    ramp = jnp.exp(cum) * tok_ref[:, 4:5]
    thr = thr_ref[pl.ds(chunk, 1), :]
    squares = jnp.zeros((CHUNK, LANES), f32)
    for j in range(width // LANES):
        cs = slice(j * LANES, (j + 1) * LANES)
        x = act_ref[:, cs]
        his, los = [], []
        for h in (2 * j, 2 * j + 1):
            decay = jnp.exp(cum[:, h : h + 1] - cum_t[h : h + 1, :] + bias)
            hi, lo = split2(scores * decay)
            his.append(hi)
            los.append(lo)
        xh, xl = split2(x * expand(delta, j))
        zero = jnp.zeros_like(xh)
        keep = left_half(xh.shape)
        xh0, xh1 = jnp.where(keep, xh, zero), jnp.where(keep, zero, xh)
        xl0, xl1 = jnp.where(keep, xl, zero), jnp.where(keep, zero, xl)
        y = dot(
            jnp.concatenate(his + los + his, axis=1),
            jnp.concatenate([xh0, xh1, xh0, xh1, xl0, xl1], axis=0),
        )
        st = s0_ref[0, :, cs] + expand(thr, j) * sin_ref[:, cs]
        y = y + dot(c3, rhs3(*split2(st))) * expand(ramp, j)
        mixed = y + gain_ref[0:1, cs] * x
        mixed_ref[:, cs] = mixed
        g = gate_ref[:, cs]
        gated = mixed * (g * sigmoid(g))
        squares = squares + gated * gated
    ones = jnp.ones((8, 2 * LANES), bf16)
    sq_ref[pl.ds(chunk, 1), :] = dot_nt(ones, jnp.concatenate(split2(squares), axis=1))[0:1]


def run_mix(act, delta, cum, tok, segr, s0, s_in, thr, gate, gains):
    tokens, cols = act.shape
    width = gate.shape[1]
    nc = tokens // CHUNK

    def whole(shape):
        return pl.BlockSpec(shape, lambda i: (0,) * len(shape))

    def by_row(w):
        return pl.BlockSpec((CHUNK, w), lambda i: (i, 0))

    return pl.pallas_call(
        mix_kernel,
        grid=(nc,),
        in_specs=[
            by_row(cols),
            by_row(LANES),
            by_row(LANES),
            by_row(tok.shape[1]),
            whole(segr.shape),
            pl.BlockSpec((1, STATE, width), lambda i: (i, 0, 0)),
            whole(s_in.shape),
            whole(thr.shape),
            by_row(width),
            whole(gains.shape),
        ],
        out_specs=(by_row(width), whole((nc, LANES))),
        out_shape=(
            jax.ShapeDtypeStruct((tokens, width), f32),
            jax.ShapeDtypeStruct((nc, LANES), f32),
        ),
        compiler_params=pltpu.CompilerParams(dimension_semantics=("arbitrary",)),
        name="mix",
    )(act, delta, cum, tok, segr, s0, s_in, thr, gate, gains)


def exit_kernel(g_ref, mixed_ref, gate_ref, sq_ref, gain_ref, w_ref, gnorm_ref, *out_refs):
    i = pl.program_id(0)
    rows, width = mixed_ref.shape
    block = lax.rem(g_ref[0] + i, len(out_refs))
    scales = []
    for k in range(rows // CHUNK):
        tot = column(sq_ref[pl.ds(block * (rows // CHUNK) + k, 1), :])
        scales.append(lax.rsqrt(tot / DI + norm_eps))
    scale = jnp.concatenate(scales, axis=0)
    for j in range(width // LANES):
        cs = slice(j * LANES, (j + 1) * LANES)
        g = gate_ref[:, cs]
        gated = mixed_ref[:, cs] * (g * sigmoid(g))
        gnorm_ref[:, cs] = (gated * scale * gain_ref[1:2, cs]).astype(bf16)
    part = dot_nt(gnorm_ref[...], w_ref[...]).astype(bf16)
    for k, out_ref in enumerate(out_refs):

        @pl.when(i == k)
        def _(out_ref=out_ref):
            out_ref[...] = part


def run_exit(group, groups, mixed, gate, sq, gains, weights):
    tokens, width = mixed.shape
    d = weights.shape[0]
    rows = tokens // groups

    def whole(shape, where=0):
        return pl.BlockSpec(
            shape, lambda i, g: (0,) * (len(shape) - 1) + (where,), pipeline_mode=pl.Buffered(1)
        )

    def by_row(w):
        return pl.BlockSpec((rows, w), lambda i, g: (lax.rem(g[0] + i, groups), 0))

    return pl.pallas_call(
        exit_kernel,
        grid_spec=pltpu.PrefetchScalarGridSpec(
            num_scalar_prefetch=1,
            grid=(groups,),
            in_specs=[
                by_row(width),
                by_row(width),
                whole(sq.shape),
                whole(gains.shape),
                whole((d, width), 2),
            ],
            out_specs=(by_row(width),) + (whole((rows, d)),) * groups,
        ),
        out_shape=(jax.ShapeDtypeStruct((tokens, width), bf16),)
        + (jax.ShapeDtypeStruct((rows, d), bf16),) * groups,
        compiler_params=pltpu.CompilerParams(dimension_semantics=("arbitrary",)),
        name="exit",
    )(group, mixed, gate, sq, gains, weights)


def pull_exit_kernel(groups, g_ref, *refs):
    cot_refs, refs = refs[:groups], refs[groups:]
    w_ref, mixed_ref, gate_ref, gnorm_ref, gain_ref, dgn_ref, dot_ref, gw_ref, acc = refs
    i = pl.program_id(0)
    rows, width = mixed_ref.shape
    block = lax.rem(g_ref[0] + groups - i, groups)

    @pl.when(i == 0)
    def _():
        acc[...] = jnp.zeros_like(acc)

    for s, cot_ref in enumerate(cot_refs):

        @pl.when(i == s)
        def _(cot_ref=cot_ref):
            cot = cot_ref[...]
            dgn_ref[...] = dot(cot, w_ref[...])
            acc[...] = acc[...] + lax.dot_general(
                cot, gnorm_ref[...], (((0,), (0,)), ((), ())), preferred_element_type=f32
            )

    part = jnp.zeros((rows, LANES), f32)
    for j in range(width // LANES):
        cs = slice(j * LANES, (j + 1) * LANES)
        g = gate_ref[:, cs]
        gated = mixed_ref[:, cs] * (g * sigmoid(g))
        part = part + dgn_ref[:, cs] * gain_ref[1:2, cs] * gated
    ones = jnp.ones((8, 2 * LANES), bf16)
    for k in range(rows // CHUNK):
        row = dot_nt(ones, jnp.concatenate(split2(part[k * CHUNK : (k + 1) * CHUNK]), axis=1))
        dot_ref[pl.ds(block * (rows // CHUNK) + k, 1), :] = row[0:1]

    @pl.when(i == groups - 1)
    def _():
        gw_ref[...] = acc[...].astype(bf16)


def run_pull_exit(group, groups, cots, weights, mixed, gate, gnorm, gains):
    tokens, width = mixed.shape
    d = weights.shape[0]
    rows = tokens // groups
    nc = tokens // CHUNK

    def whole(shape, where=0):
        return pl.BlockSpec(
            shape, lambda i, g: (0,) * (len(shape) - 1) + (where,), pipeline_mode=pl.Buffered(1)
        )

    def by_row(w):
        return pl.BlockSpec((rows, w), lambda i, g: (lax.rem(g[0] + groups - i, groups), 0))

    return pl.pallas_call(
        functools.partial(pull_exit_kernel, groups),
        grid_spec=pltpu.PrefetchScalarGridSpec(
            num_scalar_prefetch=1,
            grid=(groups,),
            in_specs=[whole((rows, d))] * groups
            + [
                whole((d, width), 2),
                by_row(width),
                by_row(width),
                by_row(width),
                whole(gains.shape),
            ],
            out_specs=(by_row(width), whole((nc, LANES)), whole((d, width))),
            scratch_shapes=[pltpu.VMEM((d, width), f32)],
        ),
        out_shape=(
            jax.ShapeDtypeStruct((tokens, width), f32),
            jax.ShapeDtypeStruct((nc, LANES), f32),
            jax.ShapeDtypeStruct((d, width), bf16),
        ),
        compiler_params=pltpu.CompilerParams(dimension_semantics=("arbitrary",)),
        name="pull_exit",
    )(group, *cots, weights, mixed, gate, gnorm, gains)


def pull_gate_kernel(
    nc,
    mixed_ref,
    gate_ref,
    dgn_ref,
    sq_ref,
    dot_ref,
    gain_ref,
    cum_ref,
    tok_ref,
    act_ref,
    flag_ref,
    dmix_ref,
    dgate_ref,
    g0_ref,
    dinc_ref,
    suf_ref,
    gpart_ref,
    grad,
    total,
    gacc,
):
    i = pl.program_id(0)
    chunk = nc - 1 - i
    width = mixed_ref.shape[1]

    @pl.when(i == 0)
    def _():
        grad[...] = jnp.zeros_like(grad)
        total[...] = jnp.zeros_like(total)
        gacc[...] = jnp.zeros_like(gacc)

    scale = lax.rsqrt(column(sq_ref[pl.ds(chunk, 1), :]) / DI + norm_eps)
    inner = column(dot_ref[pl.ds(chunk, 1), :]) / DI * (scale * scale * scale)
    cum = cum_ref[...]
    last = cum[CHUNK - 1 : CHUNK]
    ramp = jnp.exp(cum) * tok_ref[:, 4:5]
    carry = jnp.exp(last) * flag_ref[pl.ds(chunk, 1), :]
    suf_ref[pl.ds(chunk, 1), :] = jnp.exp(total[0:1]) * flag_ref[pl.ds(2 * nc + chunk, 1), :]
    total[0:1] = total[0:1] + last
    ct = lhs3(*split2(act_ref[...].T))
    for j in range(width // LANES):
        cs = slice(j * LANES, (j + 1) * LANES)
        g = gate_ref[:, cs]
        sg = sigmoid(g)
        gact = g * sg
        mixed = mixed_ref[:, cs]
        gated = mixed * gact
        dgn = dgn_ref[:, cs]
        d_gated = scale * (dgn * gain_ref[1:2, cs]) - gated * inner
        dmix = d_gated * gact
        dmix_ref[:, cs] = dmix
        dgate_ref[:, cs] = (d_gated * mixed * (sg * (1.0 + g * (1.0 - sg)))).astype(bf16)
        gacc[:, cs] = gacc[:, cs] + fold8(dgn * gated * scale)
        g0_ref[0, :, cs] = grad[:, cs]
        dw = dmix * expand(ramp, j)
        grad[:, cs] = grad[:, cs] * expand(carry, j) + dot(ct, rhs3(*split2(dw)))

    @pl.when(i == nc - 1)
    def _():
        dinc_ref[...] = grad[...]
        gpart_ref[...] = gacc[...]


def run_pull_gate(mixed, gate, dgn, sq, dots, gains, cum, tok, act, flags):
    tokens, width = mixed.shape
    nc = tokens // CHUNK

    def whole(shape):
        return pl.BlockSpec(shape, lambda i: (0,) * len(shape))

    def by_row(w, where=0):
        return pl.BlockSpec((CHUNK, w), lambda i: (nc - 1 - i, where))

    return pl.pallas_call(
        functools.partial(pull_gate_kernel, nc),
        grid=(nc,),
        in_specs=[
            by_row(width),
            by_row(width),
            by_row(width),
            whole(sq.shape),
            whole(dots.shape),
            whole(gains.shape),
            by_row(LANES),
            by_row(tok.shape[1]),
            by_row(STATE, (width + STATE) // STATE),
            whole(flags.shape),
        ],
        out_specs=(
            by_row(width),
            by_row(width),
            pl.BlockSpec((1, STATE, width), lambda i: (nc - 1 - i, 0, 0)),
            whole((STATE, width)),
            whole((nc, LANES)),
            whole((8, width)),
        ),
        out_shape=(
            jax.ShapeDtypeStruct((tokens, width), f32),
            jax.ShapeDtypeStruct((tokens, width), bf16),
            jax.ShapeDtypeStruct((nc, STATE, width), f32),
            jax.ShapeDtypeStruct((STATE, width), f32),
            jax.ShapeDtypeStruct((nc, LANES), f32),
            jax.ShapeDtypeStruct((8, width), f32),
        ),
        scratch_shapes=[
            pltpu.VMEM((STATE, width), f32),
            pltpu.VMEM((8, LANES), f32),
            pltpu.VMEM((8, width), f32),
        ],
        compiler_params=pltpu.CompilerParams(dimension_semantics=("arbitrary",)),
        name="pull_gate",
    )(mixed, gate, dgn, sq, dots, gains, cum, tok, act, flags)


def pull_mix_kernel(
    nc,
    u_ref,
    act_ref,
    v_ref,
    vh_ref,
    dmix_ref,
    mixed_ref,
    del_ref,
    cum_ref,
    sig_ref,
    tok_ref,
    segr_ref,
    s0_ref,
    sin_ref,
    fin_ref,
    thr_ref,
    g0_ref,
    gin_ref,
    suf_ref,
    gain_ref,
    par_ref,
    cf_ref,
    dv_ref,
    ddr_ref,
    dvh_ref,
    edge_ref,
    fpart_ref,
    hpart_ref,
    spart_ref,
    du,
    q1,
    q2,
    q3,
    facc,
    hacc,
    sacc,
    send,
):
    i = pl.program_id(0)
    chunk = nc - 1 - i
    width = dmix_ref.shape[1]
    cols = u_ref.shape[1]
    shifted = (q1, q2, q3)

    @pl.when(i == 0)
    def _():
        for q in shifted:
            q[...] = jnp.zeros_like(q)
        facc[...] = jnp.zeros_like(facc)
        hacc[...] = jnp.zeros_like(hacc)
        sacc[...] = jnp.zeros_like(sacc)
        send[...] = fin_ref[...]
        for j in range(width // LANES):
            cs = slice(j * LANES, (j + 1) * LANES)
            send[:, cs] = send[:, cs] + expand(thr_ref[nc : nc + 1, :], j) * sin_ref[:, cs]

    @pl.when(i > 0)
    def _():
        for q in shifted:
            q[CHUNK + 8 : CHUNK + 16] = q[8:16]

    bh, bl = split2(act_ref[:, width : width + STATE])
    ch, cl = split2(act_ref[:, width + STATE :])
    b3 = lhs3(bh, bl)
    scores_t = dot_nt(b3, rhs3_nt(ch, cl))
    cum = cum_ref[...]
    cum_t = cum.T
    r, s = ordered()
    allowed = (tok_ref[:, 5:6] == segr_ref[pl.ds(chunk, 1), :]) & (r <= s)
    bias = jnp.where(allowed, 0.0, NEG)
    delta = del_ref[...]
    last = cum[CHUNK - 1 : CHUNK]
    ramp = jnp.exp(cum) * tok_ref[:, 4:5]
    tail = jnp.exp(last - cum) * tok_ref[:, 3:4]
    thr = thr_ref[pl.ds(chunk, 1), :]
    suf = suf_ref[pl.ds(chunk, 1), :]
    d_scores = jnp.zeros((CHUNK, CHUNK), f32)
    d_b = jnp.zeros((CHUNK, STATE), f32)
    d_c = jnp.zeros((CHUNK, STATE), f32)
    d_delta = jnp.zeros((CHUNK, LANES), f32)
    flow = jnp.zeros((CHUNK, LANES), f32)
    bound = jnp.zeros((8, LANES), f32)
    for j in range(width // LANES):
        cs = slice(j * LANES, (j + 1) * LANES)
        x = act_ref[:, cs]
        dy = dmix_ref[:, cs]
        delta_e = expand(delta, j)
        xd = x * delta_e
        dyh, dyl = split2(dy)
        zero = jnp.zeros_like(dyh)
        keep = left_half(dyh.shape)
        dyh0, dyh1 = jnp.where(keep, dyh, zero), jnp.where(keep, zero, dyh)
        dyl0, dyl1 = jnp.where(keep, dyl, zero), jnp.where(keep, zero, dyl)
        his, los, decays = [], [], []
        for h in (2 * j, 2 * j + 1):
            decay = jnp.exp(cum_t[h : h + 1, :] - cum[:, h : h + 1] + bias)
            hi, lo = split2(scores_t * decay)
            his.append(hi)
            los.append(lo)
            decays.append(decay)
        g_end = g0_ref[0, :, cs] + expand(suf, j) * gin_ref[:, cs]
        st = s0_ref[0, :, cs] + expand(thr, j) * sin_ref[:, cs]
        gh, gl = split2(g_end)
        sh, sl = split2(st)
        tail_e = expand(tail, j)
        dxd = dot(
            jnp.concatenate(his + los + his, axis=1),
            jnp.concatenate([dyh0, dyh1, dyh0, dyh1, dyl0, dyl1], axis=0),
        )
        dxd = dxd + dot(b3, rhs3(gh, gl)) * tail_e
        xdh, xdl = split2(xd)
        d_kernel = dot_nt(
            lhs3(xdh, xdl),
            jnp.concatenate(
                [rhs3_nt(dyh0, dyl0), rhs3_nt(dyh1, dyl1)],
                axis=0,
            ),
        )
        d_scores = d_scores + d_kernel[:, :CHUNK] * decays[0] + d_kernel[:, CHUNK:] * decays[1]
        d_c = d_c + dot_nt(lhs3(*split2(dy * expand(ramp, j))), rhs3_nt(sh, sl))
        d_b = d_b + dot_nt(lhs3(*split2(xd * tail_e)), rhs3_nt(gh, gl))
        skip = gain_ref[0:1, cs]
        yssm = mixed_ref[:, cs] - skip * x
        to_head = head_columns(j)
        to_head2 = jnp.concatenate([to_head, to_head], axis=0)
        d_delta = d_delta + dot(jnp.concatenate(split2(dxd * x), axis=1), to_head2)
        flow = flow + dot(jnp.concatenate(split2(dy * yssm - dxd * xd), axis=1), to_head2)
        met = fold8(g_end * send[:, cs])
        bound = bound + dot(jnp.concatenate(split2(met), axis=1), to_head2)
        send[:, cs] = st
        sacc[:, cs] = sacc[:, cs] + fold8(dy * x)
        u = u_ref[:, cs]
        sg = sigmoid(u)
        du[:, cs] = (dxd * delta_e + skip * dy) * (sg * (1.0 + u * (1.0 - sg)))
    dsh, dsl = split2(d_scores)
    d_b = d_b + dot(lhs3(dsh, dsl), rhs3(ch, cl))
    dth, dtl = split2(d_scores.T)
    d_c = d_c + dot(lhs3(dth, dtl), rhs3(bh, bl))
    for k, value in ((0, d_b), (1, d_c)):
        cs = slice(width + k * STATE, width + (k + 1) * STATE)
        u = u_ref[:, cs]
        sg = sigmoid(u)
        du[:, cs] = value * (sg * (1.0 + u * (1.0 - sg)))
    later = jnp.where(allowed, 1.0, 0.0).astype(bf16)
    later3 = jnp.concatenate([later, later, later], axis=1)
    ends = jnp.sum(bound, axis=0, keepdims=True)
    d_logdec = dot(later3, jnp.concatenate(split3(flow), axis=0)) + ends * tok_ref[:, 3:4]
    d_logdec = d_logdec * tok_ref[:, 2:3]
    ddr = (d_delta + d_logdec * par_ref[1:2, :]) * sig_ref[...]
    ddr_ref[...] = ddr.astype(bf16)
    hacc[0:8] = hacc[0:8] + fold8(ddr)
    hacc[8:16] = hacc[8:16] + fold8(d_logdec * par_ref[1:2, :] * delta)

    masks = [jnp.broadcast_to(tok_ref[:, k : k + 1], (CHUNK, LANES)) for k in (2, 1, 0)]
    for j in range(cols // LANES):
        cs = slice(j * LANES, (j + 1) * LANES)
        d = du[:, cs]
        v = v_ref[:, cs].astype(f32)
        dv = cf_ref[3:4, cs] * d
        facc[32:40, cs] = facc[32:40, cs] + fold8(d)
        facc[24:32, cs] = facc[24:32, cs] + fold8(d * v)
        for n, q in enumerate(shifted, 1):
            q[8 : 8 + CHUNK, cs] = d * masks[n - 1]
            moved = q[8 + n : 8 + n + CHUNK, cs]
            tap = CONV - 1 - n
            dv = dv + cf_ref[tap : tap + 1, cs] * moved
            at = slice(8 * tap, 8 * tap + 8)
            facc[at, cs] = facc[at, cs] + fold8(moved * v)
        dv_ref[:, cs] = dv.astype(bf16)

        @pl.when(i == 0)
        def _(cs=cs, dv=dv):
            edge_ref[:, cs] = dv[CHUNK - 16 :]

    @pl.when(i == nc - 1)
    def _():
        for j in range(cols // LANES):
            cs = slice(j * LANES, (j + 1) * LANES)
            vh = vh_ref[:, cs]
            dvh = jnp.zeros((8, LANES), f32)
            for n, q in enumerate(shifted, 1):
                moved = q[n : n + 8, cs]
                tap = CONV - 1 - n
                dvh = dvh + cf_ref[tap : tap + 1, cs] * moved
                at = slice(8 * tap, 8 * tap + 8)
                facc[at, cs] = facc[at, cs] + moved * vh
            dvh_ref[:, cs] = dvh
        fpart_ref[...] = facc[...]
        hpart_ref[...] = hacc[...]
        spart_ref[...] = sacc[...]


def run_pull_mix(
    u, act, v, vh, dmix, mixed, delta, cum, sig, tok, segr, s0, s_in, fin, thr, g0, g_in, suf,
    gains, par, cf,
):
    tokens, cols = u.shape
    width = dmix.shape[1]
    nc = tokens // CHUNK

    def whole(shape):
        return pl.BlockSpec(
            shape, lambda i: (0,) * len(shape), pipeline_mode=pl.Buffered(1)
        )

    def by_row(w):
        return pl.BlockSpec((CHUNK, w), lambda i: (nc - 1 - i, 0))

    def states():
        return pl.BlockSpec((1, STATE, width), lambda i: (nc - 1 - i, 0, 0))

    def out(shape, dt=f32):
        return jax.ShapeDtypeStruct(shape, dt)

    return pl.pallas_call(
        functools.partial(pull_mix_kernel, nc),
        grid=(nc,),
        in_specs=[
            by_row(cols),
            by_row(cols),
            by_row(cols),
            whole(vh.shape),
            by_row(width),
            by_row(width),
            by_row(LANES),
            by_row(LANES),
            by_row(LANES),
            by_row(tok.shape[1]),
            whole(segr.shape),
            states(),
            whole(s_in.shape),
            whole(fin.shape),
            whole(thr.shape),
            states(),
            whole(g_in.shape),
            whole(suf.shape),
            whole(gains.shape),
            whole(par.shape),
            whole(cf.shape),
        ],
        out_specs=(
            by_row(cols),
            by_row(LANES),
            whole((8, cols)),
            whole((16, cols)),
            whole((40, cols)),
            whole((16, LANES)),
            whole((8, width)),
        ),
        out_shape=(
            out((tokens, cols), bf16),
            out((tokens, LANES), bf16),
            out((8, cols)),
            out((16, cols)),
            out((40, cols)),
            out((16, LANES)),
            out((8, width)),
        ),
        scratch_shapes=[
            pltpu.VMEM((CHUNK, cols), f32),
            pltpu.VMEM((CHUNK + 16, cols), f32),
            pltpu.VMEM((CHUNK + 16, cols), f32),
            pltpu.VMEM((CHUNK + 16, cols), f32),
            pltpu.VMEM((40, cols), f32),
            pltpu.VMEM((16, LANES), f32),
            pltpu.VMEM((8, width), f32),
            pltpu.VMEM((STATE, width), f32),
        ],
        compiler_params=pltpu.CompilerParams(dimension_semantics=("arbitrary",)),
        name="pull_mix",
    )(
        u, act, v, vh, dmix, mixed, delta, cum, sig, tok, segr, s0, s_in, fin, thr, g0, g_in, suf,
        gains, par, cf,
    )


def scatter_kernel(n_dp, n_ctx, n_z, ring, widths, *refs):
    ng = len(widths)
    refs = list(refs)

    def take(n):
        return [refs.pop(0) for _ in range(n)]

    (dn_ref,), parts, (small_ref,) = take(1), take(ng), take(1)
    (dno_ref,), outs, (shared_ref, smalls_ref) = take(1), take(ng - 1), take(2)
    lands, qs, temps, opps, fins = take(ng), take(ng), take(ng), take(ng), take(ng)
    zsh, acc_sh, zland, zsum, sland, ssum, lo, far, near, comb = take(10)
    c_send, c_recv, o_send, o_recv, f_send, f_recv, g_send, g_recv, h_send, h_recv = take(10)
    s_send, s_recv, t_send, t_recv, x_send, x_recv, y_send, y_recv, n_send, n_recv = take(10)
    own = [zsh] + outs

    z, d, c = lax.axis_index("tensor"), lax.axis_index("dp"), lax.axis_index("ctx")
    pos = pick(d, [ring.index(i) for i in range(n_dp)])
    at = [pick(lax.rem(pos + r, n_dp), ring) for r in range(n_dp)]
    nxt, prv = at[1], at[n_dp - 1]
    n_plane = n_dp * n_ctx
    wr = parts[0].shape[0] // n_plane
    rows = dno_ref.shape[0]
    zc = lo.shape[1]
    zr = rows // zc
    step = 16
    mine = d * n_ctx + c

    def remote(src, dst, send, recv, **where):
        return pltpu.make_async_remote_copy(
            src, dst, send, recv, device_id=where, device_id_type=MESH
        )

    def z_at(k):
        return lax.rem(z + k, n_z)

    def c_at(k):
        return lax.rem(c + k, n_ctx)

    peers = [(at[r], c_at(s)) for r in range(n_dp) for s in range(n_ctx) if r or s]
    bar = pltpu.get_barrier_semaphore()
    for dd, cc in peers:
        pl.semaphore_signal(bar, device_id={"dp": dd, "ctx": cc}, device_id_type=MESH)
    for k in range(1, n_z):
        pl.semaphore_signal(bar, device_id={"tensor": z_at(k)}, device_id_type=MESH)
    pl.semaphore_wait(bar, len(peers) + n_z - 1)

    def ctx_copy(g, r, s):
        return remote(
            parts[g].at[pl.ds(pl.multiple_of((at[r] * n_ctx + c_at(s)) * wr, step), wr)],
            lands[g].at[s - 1, r],
            c_send.at[g, s - 1, r],
            c_recv.at[g, s - 1, r],
            ctx=c_at(s),
        )

    cut = [w // 2 // LANES * LANES for w in widths]

    def side(g, h):
        return pl.ds(0, cut[g]) if h == 0 else pl.ds(cut[g], widths[g] - cut[g])

    def opp_copy(g, h):
        return remote(
            qs[g].at[1, :, side(g, h)],
            opps[g].at[:, side(g, h)],
            o_send.at[g, h],
            o_recv.at[g, h],
            dp=nxt if h == 0 else prv,
        )

    def fin_copy(g, way, h):
        return remote(
            qs[g].at[2 * way, :, side(g, h)],
            fins[g].at[way, :, side(g, h)],
            f_send.at[g, way, h],
            f_recv.at[g, way, h],
            dp=nxt if way == 0 else prv,
        )

    def small_copy(i):
        dd, cc = peers[i]
        return remote(small_ref, sland.at[i], s_send.at[i], s_recv.at[i], dp=dd, ctx=cc)

    def small_z(k, src):
        return remote(
            ssum, smalls_ref.at[src], t_send.at[k - 1], t_recv.at[k - 1], tensor=z_at(k)
        )

    def shared_z(k):
        return remote(
            acc_sh.at[z_at(k)], zland.at[k - 1], x_send.at[k - 1], x_recv.at[k - 1], tensor=z_at(k)
        )

    def shared_back(k, src):
        return remote(
            zsum, shared_ref.at[mine, src], y_send.at[k - 1], y_recv.at[k - 1], tensor=z_at(k)
        )

    def shared_dp(r, src):
        return remote(
            shared_ref.at[mine],
            shared_ref.at[src * n_ctx + c],
            g_send.at[r - 1],
            g_recv.at[r - 1],
            dp=at[r],
        )

    def shared_ctx(r, s, src):
        return remote(
            shared_ref.at[at[r] * n_ctx + c],
            shared_ref.at[at[r] * n_ctx + src],
            h_send.at[r, s - 1],
            h_recv.at[r, s - 1],
            ctx=c_at(s),
        )

    outer = (z == 0) | (z == n_z - 1)
    inner = (z > 0) & (z < n_z - 1)
    mate = pick(z, [1, 0, 3, 2])
    far_mate, far_z = n_z - 1 - mate, n_z - 1 - z

    def dn_at(block, k):
        return pl.ds(pl.multiple_of(block * rows + k * zr, step), zr)

    def lo_copy(n, k):
        block = (far_z, far_mate, mate)[n]
        return remote(
            dn_ref.at[dn_at(block, k)], lo.at[n, k], n_send.at[n, k], n_recv.at[n, k], tensor=mate
        )

    def near_copy(k):
        return remote(
            dn_ref.at[dn_at(mate, k)], near.at[k], n_send.at[3, k], n_recv.at[3, k], tensor=mate
        )

    def comb_copy(n, k):
        return remote(
            comb.at[n, k],
            far.at[k],
            n_send.at[4 + n, k],
            n_recv.at[4, k],
            tensor=(far_mate, far_z)[n],
        )

    for g in range(ng):
        for s in range(1, n_ctx):
            for r in range(n_dp):
                ctx_copy(g, r, s).start()

    @pl.when(outer)
    def _():
        for n in range(3):
            for k in range(zc):
                lo_copy(n, k).start()

    @pl.when(inner)
    def _():
        for k in range(zc):
            near_copy(k).start()

    for i in range(len(peers)):
        small_copy(i).start()

    def by_rows(fn):
        def body(i, carry):
            fn(pl.multiple_of(i * step, step))
            return carry

        lax.fori_loop(0, wr // step, body, 0)

    def first(g):
        for s in range(1, n_ctx):
            for r in range(n_dp):
                ctx_copy(g, r, s).wait_recv()

        def body(row):
            for r in range(n_dp):
                base = pl.multiple_of(mine_rows[r] + row, step)
                value = parts[g][pl.ds(base, step)].astype(f32)
                for s in range(n_ctx - 1):
                    value = value + lands[g][s, r, pl.ds(row, step)].astype(f32)
                if r == 0:
                    own[g][pl.ds(row, step)] = value
                else:
                    qs[g][r - 1, pl.ds(row, step)] = value.astype(qs[g].dtype)
                if r == 1:
                    temps[g][pl.ds(row, step), : cut[g]] = value[:, : cut[g]]
                if r == n_dp - 1:
                    temps[g][pl.ds(row, step), cut[g] :] = value[:, cut[g] :]

        by_rows(body)

    mine_rows = [(at[r] * n_ctx + c) * wr for r in range(n_dp)]

    def send_first(g):
        for h in range(2):
            opp_copy(g, h).start()
        fin_copy(g, 0, 1).start()
        fin_copy(g, 1, 0).start()

    def second(g):
        for h in range(2):
            opp_copy(g, h).wait_recv()

        def body(row):
            at_rows = pl.ds(row, step)
            value = temps[g][at_rows] + opps[g][at_rows].astype(f32)
            qs[g][0, at_rows, : cut[g]] = value[:, : cut[g]].astype(qs[g].dtype)
            qs[g][2, at_rows, cut[g] :] = value[:, cut[g] :].astype(qs[g].dtype)

        by_rows(body)

    def send_second(g):
        fin_copy(g, 0, 0).start()
        fin_copy(g, 1, 1).start()

    def third(g):
        for way in range(2):
            for h in range(2):
                fin_copy(g, way, h).wait_recv()

        def body(row):
            at_rows = pl.ds(row, step)
            own[g][at_rows] = (
                own[g][at_rows] + fins[g][0, at_rows].astype(f32) + fins[g][1, at_rows].astype(f32)
            )

        by_rows(body)

    def combine(n, k):
        @pl.when(inner)
        def _():
            lo_copy(n, k).wait_recv()
            block = (far_mate, far_z)[n]
            comb[n, k] = (dn_ref[dn_at(block, k)].astype(f32) + lo[n, k].astype(f32)).astype(bf16)

    def send_combined(n, k):
        @pl.when(inner)
        def _():
            comb_copy(n, k).start()

    first(0)
    first(1)
    send_first(0)
    for i in range(len(peers)):
        small_copy(i).wait_recv()
    total = small_ref[...]
    for i in range(len(peers)):
        total = total + sland[i]
    ssum[...] = total
    smalls_ref[z] = total
    first(2)
    send_first(1)
    for k in range(1, n_z):
        small_z(k, z).start()
    first(3)
    send_first(2)
    second(0)
    send_first(3)
    combine(0, 0)
    send_second(0)
    second(1)
    send_combined(0, 0)
    combine(0, 1)
    send_second(1)
    third(0)
    quarter = wr // n_z
    for k in range(n_z):
        acc_sh[k] = zsh[k * quarter : (k + 1) * quarter]
    second(2)
    send_combined(0, 1)
    for k in range(1, n_z):
        shared_z(k).start()
    combine(1, 0)
    send_second(2)
    for k in range(1, n_z):
        shared_z(k).wait_recv()
    total = acc_sh[z]
    for k in range(1, n_z):
        total = total + zland[k - 1]
    zsum[...] = total
    shared_ref[mine, z] = total
    second(3)
    send_combined(1, 0)
    send_second(3)
    for k in range(1, n_z):
        shared_back(k, z).start()
    combine(1, 1)
    third(1)
    send_combined(1, 1)
    for k in range(1, n_z):
        shared_back(k, z_at(n_z - k)).wait_recv()
    for r in range(1, n_dp):
        shared_dp(r, d).start()
    for s in range(1, n_ctx):
        shared_ctx(0, s, c).start()
    third(2)
    for r in range(1, n_dp):
        shared_dp(r, at[n_dp - r]).wait_recv()
    for r in range(1, n_dp):
        for s in range(1, n_ctx):
            shared_ctx(r, s, c).start()
    third(3)
    for k in range(1, n_z):
        small_z(k, z_at(n_z - k)).wait_recv()
    for k in range(zc):
        at_rows = pl.ds(k * zr, zr)
        dno_ref[at_rows] = dn_ref[dn_at(z, k)].astype(f32)

        @pl.when(outer)
        def _(k=k, at_rows=at_rows):
            near_copy(k).wait_recv()
            dno_ref[at_rows] = dno_ref[at_rows] + near[k].astype(f32)

        @pl.when(inner)
        def _(k=k, at_rows=at_rows):
            lo_copy(2, k).wait_recv()
            dno_ref[at_rows] = dno_ref[at_rows] + lo[2, k].astype(f32)

        comb_copy(0, k).wait_recv()
        dno_ref[at_rows] = dno_ref[at_rows] + far[k].astype(f32)
    for r in range(n_dp):
        for s in range(1, n_ctx):
            shared_ctx(r, s, c_at(n_ctx - s)).wait_recv()

    for g in range(ng):
        for s in range(1, n_ctx):
            for r in range(n_dp):
                ctx_copy(g, r, s).wait_send()
        for h in range(2):
            opp_copy(g, h).wait_send()
            for way in range(2):
                fin_copy(g, way, h).wait_send()

    @pl.when(outer)
    def _():
        for n in range(3):
            for k in range(zc):
                lo_copy(n, k).wait_send()

    @pl.when(inner)
    def _():
        for k in range(zc):
            near_copy(k).wait_send()
            for n in range(2):
                comb_copy(n, k).wait_send()

    for i in range(len(peers)):
        small_copy(i).wait_send()
    for k in range(1, n_z):
        small_z(k, z).wait_send()
        shared_z(k).wait_send()
        shared_back(k, z).wait_send()
    for r in range(1, n_dp):
        shared_dp(r, d).wait_send()
    for r in range(n_dp):
        for s in range(1, n_ctx):
            shared_ctx(r, s, c).wait_send()


def scatter_all(dims, d_normed, parts, small):
    n_dp, n_ctx, n_z, ring = dims
    n_plane = n_dp * n_ctx
    widths = [p.shape[1] for p in parts]
    ng = len(parts)
    wr = parts[0].shape[0] // n_plane
    rows, d = d_normed.shape[0] // n_z, d_normed.shape[1]
    zc = 2
    dma = pltpu.SemaphoreType.DMA
    vmem = pltpu.VMEM
    quarter = wr // n_z

    def out(*shape):
        return jax.ShapeDtypeStruct(shape, f32)

    outs = (
        [out(rows, d)]
        + [out(wr, w) for w in widths[1:]]
        + [out(n_plane, n_z, quarter, widths[0]), out(n_z, *small.shape)]
    )
    scratch = (
        [vmem((n_ctx - 1, n_dp, wr, p.shape[1]), p.dtype) for p in parts]
        + [vmem((3, wr, p.shape[1]), p.dtype) for p in parts]
        + [vmem((wr, w), f32) for w in widths]
        + [vmem((wr, p.shape[1]), p.dtype) for p in parts]
        + [vmem((2, wr, p.shape[1]), p.dtype) for p in parts]
        + [
            vmem((wr, widths[0]), f32),
            vmem((n_z, quarter, widths[0]), f32),
            vmem((n_z - 1, quarter, widths[0]), f32),
            vmem((quarter, widths[0]), f32),
            vmem((n_plane - 1,) + small.shape, f32),
            vmem(small.shape, f32),
            vmem((3, zc, rows // zc, d), bf16),
            vmem((zc, rows // zc, d), bf16),
            vmem((zc, rows // zc, d), bf16),
            vmem((2, zc, rows // zc, d), bf16),
        ]
        + [dma((ng, n_ctx - 1, n_dp))] * 2
        + [dma((ng, 2))] * 2
        + [dma((ng, 2, 2))] * 2
        + [dma((n_dp - 1,))] * 2
        + [dma((n_dp, n_ctx - 1))] * 2
        + [dma((n_plane - 1,))] * 2
        + [dma((n_z - 1,))] * 6
        + [dma((6, zc)), dma((5, zc))]
    )
    return pl.pallas_call(
        functools.partial(scatter_kernel, n_dp, n_ctx, n_z, ring, widths),
        out_shape=tuple(outs),
        in_specs=[pl.BlockSpec(memory_space=pltpu.VMEM)] * (ng + 2),
        out_specs=tuple([pl.BlockSpec(memory_space=pltpu.VMEM)] * len(outs)),
        scratch_shapes=scratch,
        compiler_params=pltpu.CompilerParams(collective_id=3, has_side_effects=True),
        name="scatter_all",
    )(d_normed, *parts, small)


def shift(block, axis, by):
    n = lax.axis_size(axis)
    return lax.ppermute(block, axis, [(i, i + by) for i in range(n) if 0 <= i + by < n])


def turn(block, axis, by):
    n = lax.axis_size(axis)
    return lax.ppermute(block, axis, [(i, (i + by) % n) for i in range(n)])


def adamw(weight, grad, first, second, rate, decay):
    first_new = beta_first * first + (1.0 - beta_first) * grad
    second_new = beta_second * second + (1.0 - beta_second) * grad * grad
    first_hat = first_new / (1.0 - beta_first**STEP)
    second_hat = second_new / (1.0 - beta_second**STEP)
    weight_new = weight - rate * (first_hat / (jnp.sqrt(second_hat) + adam_eps) + decay * weight)
    return (grad, weight_new, first_new, second_new)


def per_lane(row):
    return jnp.repeat(row, HEAD_DIM, axis=-1)


def pad_lanes(a):
    return jnp.pad(a, ((0, 0),) * (a.ndim - 1) + ((0, LANES - a.shape[-1]),))


def state_scan(through, final, axis, reverse):
    n, mine = lax.axis_size(axis), lax.axis_index(axis)
    if n == 2:
        moved = shift(final, axis, -1 if reverse else 1)
        return moved
    finals = lax.all_gather(final, axis)
    rates = lax.all_gather(through, axis)
    acc = jnp.zeros_like(final)
    for k in range(n - 1):
        at = n - 1 - k if reverse else k
        nxt = rates[at] * acc + finals[at]
        acc = jnp.where(at > mine if reverse else at < mine, nxt, acc)
    return acc


def local(
    dims,
    block_in,
    cotangent,
    segments,
    norm_gain,
    inward_weight,
    shared_weight,
    conv_filter,
    head_params,
    gated_gain,
    exit_weight,
    norm_first,
    norm_second,
    entry_first,
    entry_second,
    shared_first,
    shared_second,
    filter_first,
    filter_second,
    head_first,
    head_second,
    gated_first,
    gated_second,
    exit_first,
    exit_second,
):
    group = lax.axis_index("tensor")
    groups = lax.axis_size("tensor")
    per_group = HEADS // groups
    width = DI // groups
    rows = block_in.shape[0]
    tokens = rows * groups
    nc = tokens // CHUNK
    inputs = block_in[:, 0].astype(f32)
    cot = cotangent[:, 0]
    scale_in = lax.rsqrt(jnp.mean(inputs * inputs, axis=-1, keepdims=True) + norm_eps)
    normed_own = (inputs * scale_in * norm_gain).astype(bf16)
    w_own = jnp.concatenate(
        [inward_weight[:, 0], inward_weight[:, 1], exit_weight], axis=1
    ).astype(bf16)

    seg = segments[0]
    prev = shift(seg[-8:], "ctx", 1)
    prev = jnp.where(lax.axis_index("ctx") > 0, prev, -1)
    seg_pad = jnp.concatenate([prev[-3:], seg])
    same = [(seg_pad[k : k + tokens] == seg).astype(f32) for k in range(3)]
    chunks = seg.reshape(nc, CHUNK)
    lasts = chunks[:, -1]
    before = jnp.concatenate([prev[-1:], lasts[:-1]])
    keep = (chunks == lasts[:, None]).astype(f32).reshape(-1)
    inflow = (chunks == before[:, None]).astype(f32).reshape(-1)
    zero = jnp.zeros_like(keep)
    tok = jnp.stack(same + [keep, inflow, seg.astype(f32), zero, zero], axis=1)
    segr = chunks.astype(f32)
    reach = (before == prev[-1]).at[0].set(True)
    flag = jnp.concatenate(
        [
            lasts == before,
            reach,
            lasts == lasts[-1],
            jnp.broadcast_to(lasts[-1] == prev[-1], (nc,)),
        ]
    ).astype(f32)
    flags = jnp.broadcast_to(flag[:, None], (4 * nc, LANES))

    head_own = lax.dynamic_slice_in_dim(head_params, group * per_group, per_group, 1)
    has_prev = jnp.broadcast_to((lax.axis_index("ctx") > 0).astype(f32), (1, LANES))
    par = jnp.concatenate(
        [
            pad_lanes(head_own[0:1]),
            pad_lanes(-jnp.exp(head_own[1:2])),
            jnp.zeros((1, LANES), f32),
            has_prev,
            jnp.zeros((4, LANES), f32),
        ]
    )
    gain_own = lax.dynamic_slice_in_dim(gated_gain, group * width, width)
    gains = jnp.concatenate(
        [per_lane(head_own[2:3]), gain_own[None], jnp.zeros((6, width), f32)]
    )
    cf = jnp.concatenate(
        [
            lax.dynamic_slice_in_dim(conv_filter[:, :DI], group * width, width, 1),
            conv_filter[:, DI:],
        ],
        axis=1,
    )
    cf = jnp.pad(cf, ((0, 3), (0, 0)))
    delta_w = lax.dynamic_slice_in_dim(shared_weight[:, 2 * STATE :], group * per_group, per_group, 1)
    shared_ext = jnp.concatenate(
        [shared_weight[:, : 2 * STATE], pad_lanes(delta_w)], axis=1
    ).astype(bf16)

    shared_bf = jnp.pad(
        shared_weight, ((0, 0), (0, -shared_weight.shape[1] % LANES))
    ).astype(bf16)

    normed, weights, halo = gather_all(dims, normed_own, w_own)

    cot_out = lax.optimization_barrier((cot, halo))[0]
    cots = [cot] + [turn(cot_out, "tensor", k) for k in range(1, groups)]

    gate, v, u, act, delta, cum, sig, s0, fin, thr, vh = run_entry(
        normed, weights, shared_ext, halo, tok, flags, par, cf, width
    )
    through = per_lane(thr[nc : nc + 1, :per_group])
    s_in = state_scan(through, fin, "ctx", False)
    mixed, sq = run_mix(act, delta, cum, tok, segr, s0, s_in, thr, gate, gains)
    sq = all_sum(groups, 1, sq)
    group_at = group.astype(jnp.int32)[None]
    gnorm, *out_parts = run_exit(group_at, groups, mixed, gate, sq, gains, weights)
    total = inputs + out_parts[0].astype(f32)
    for k in range(1, groups):
        total = total + turn(out_parts[k], "tensor", k).astype(f32)
    block_output = total.astype(bf16)[:, None]

    dgn, dots, exit_part = run_pull_exit(
        group_at, groups, cots, weights, mixed, gate, gnorm, gains
    )
    dots = all_sum(groups, 2, dots)
    dmix, d_gate, g0, d_inc, suf, gpart = run_pull_gate(
        mixed, gate, dgn, sq, dots, gains, cum, tok, act, flags
    )
    g_in = state_scan(through, d_inc, "ctx", True)
    d_v, d_raw, d_vh, edge, fpart, hpart, spart = run_pull_mix(
        u, act, v, vh, dmix, mixed, delta, cum, sig, tok, segr, s0, s_in, fin, thr, g0, g_in, suf,
        gains, par, cf,
    )
    from_next = shift(d_vh, "ctx", -1)
    edge = edge.at[8:].add(from_next).astype(bf16)
    d_v = lax.dynamic_update_slice_in_dim(d_v, edge, tokens - 16, 0)

    d_raw = lax.dynamic_update_slice_in_dim(
        jnp.zeros((tokens, LANES), bf16), d_raw[:, :per_group], group * per_group, 1
    )
    d_all = jnp.concatenate([d_gate, d_v, d_raw], axis=1)
    w_all = jnp.concatenate([weights[:, : 2 * width], shared_bf], axis=1)
    back = lax.dot_general(d_all, w_all, NT, preferred_element_type=bf16)
    w_part = lax.dot_general(
        normed, d_all, (((0,), (0,)), ((), ())), preferred_element_type=f32
    )
    norm_part = jnp.sum(w_part * w_all.astype(f32), axis=1) / norm_gain
    shared_part = w_part[:, 2 * width :]
    w_part = w_part.astype(bf16)
    small = jnp.concatenate(
        [
            jnp.sum(gpart, axis=0),
            jnp.sum(fpart[:, :width].reshape(CONV + 1, 8, width), axis=1).reshape(-1),
            pad_lanes(
                jnp.concatenate(
                    [
                        jnp.sum(hpart.reshape(2, 8, LANES), axis=1)[:, :per_group],
                        jnp.sum(spart, axis=0).reshape(1, per_group, HEAD_DIM).sum(-1),
                    ]
                )
            ).reshape(-1),
            jnp.sum(fpart[:, width:].reshape(CONV + 1, 8, 2 * STATE), axis=1).reshape(-1),
            norm_part,
        ]
    )
    n_small = small.shape[0]
    small = jnp.pad(small, (0, -n_small % (8 * LANES))).reshape(-1, LANES)
    d_normed, exit_grad, grad_gate, grad_inner, shared_sum, smalls = scatter_all(
        dims,
        back,
        [shared_part, exit_part, w_part[:, :width], w_part[:, width : 2 * width]],
        small,
    )
    entry_grad = jnp.stack([grad_gate, grad_inner], axis=1)
    shared_grad = shared_sum.reshape(w_part.shape[0], -1)[:, : 2 * STATE + HEADS]
    d_scaled = d_normed * norm_gain
    input_grad = (
        cot.astype(f32)
        + scale_in * d_scaled
        - inputs * scale_in**3 * jnp.mean(d_scaled * inputs, axis=-1, keepdims=True)
    )[:, None]
    smalls = smalls.reshape(groups, -1)
    sizes = [width, (CONV + 1) * width, 3 * LANES, (CONV + 1) * 2 * STATE, norm_gain.shape[0]]
    ends = [sum(sizes[: k + 1]) for k in range(5)]
    gated_grad, f_own, heads, f_shared, norm_grad = (
        smalls[:, e - s : e] for s, e in zip(sizes, ends, strict=True)
    )
    gated_grad = gated_grad.reshape(DI)
    f_own = f_own.reshape(groups, CONV + 1, width).transpose(1, 0, 2).reshape(CONV + 1, DI)
    filter_grad = jnp.concatenate(
        [f_own, jnp.sum(f_shared, axis=0).reshape(CONV + 1, 2 * STATE)], axis=1
    )
    head_grad = (
        heads.reshape(groups, 3, LANES)[:, :, :per_group].transpose(1, 0, 2).reshape(3, HEADS)
    )
    norm_grad = jnp.sum(norm_grad, axis=0)
    return (
        block_output,
        input_grad,
        *adamw(norm_gain, norm_grad, norm_first, norm_second, rate_vector, 0.0),
        *adamw(inward_weight, entry_grad, entry_first, entry_second, rate_matrix, decay_matrix),
        *adamw(shared_weight, shared_grad, shared_first, shared_second, rate_matrix, decay_matrix),
        *adamw(conv_filter, filter_grad, filter_first, filter_second, rate_vector, 0.0),
        *adamw(head_params, head_grad, head_first, head_second, rate_vector, 0.0),
        *adamw(gated_gain, gated_grad, gated_first, gated_second, rate_vector, 0.0),
        *adamw(exit_weight, exit_grad, exit_first, exit_second, rate_matrix, decay_matrix),
    )


def solution(mesh):
    n_dp, n_ctx, n_z = (mesh.shape[a] for a in ("dp", "ctx", "tensor"))
    ring = [0, 1, 3, 2] if n_ctx == 2 and n_dp == 4 else list(range(n_dp))
    dims = (n_dp, n_ctx, n_z, ring)
    token = P(("ctx", "tensor"), "dp", None)
    entry = P(("dp", "ctx"), None, "tensor")
    leave = P(("dp", "ctx"), "tensor")
    rep = P()
    return jax.shard_map(
        functools.partial(local, dims),
        mesh=mesh,
        in_specs=(
            token, token, P("dp", "ctx"), rep, entry, rep, rep, rep, rep, leave,
            rep, rep, entry, entry, rep, rep, rep, rep, rep, rep, rep, rep, leave, leave,
        ),
        out_specs=(token, token)
        + (rep,) * 4 + (entry,) * 4 + (rep,) * 16 + (leave,) * 4,
        check_vma=False,
    )
```

time: 1430 us -> 407 us (0.28)
  waiting for transfers between devices: 497 us -> 0.03 us
  local copies, waits for them, and re-layouts: 390 us -> 49.7 us
  Pallas kernels: 0 us -> 270 us
  matrix products: 215 us -> 22.7 us
  other arithmetic: 206 us -> 40.6 us
  blocking collectives: 75.2 us -> 0 us
    pallas_call x0 -> x10, Pallas kernels: none -> 270 us  [the longest x1 104 us: scatter_all(): pl.pallas_call(functools.partial(scatter_kernel, n_dp, n_ctx, n_z, ring,...]
    reduce_scatter x3 -> x0, waiting for transfers between devices: 249 us -> none  [the longest x1 112 us: local(): lax.psum_scatter(jnp.einsum('rsi,di->rsd', block_rows, exit_full, preferr...]
    dynamic_update_slice x75 -> x1, local copies, waits for them, and re-layouts: 220 us -> 2.49 us  [local(): lax.dynamic_update_slice_in_dim(jnp.zeros((tokens, LANES), bf16), d_raw[:...]
    dot_general x60 -> x2, matrix products: 215 us -> 22.7 us  [the longest x1 14.3 us: local(): lax.dot_general(normed, d_all, (((0,), (0,)), ((), ())), preferred_elemen...]
    all_gather x4 -> x0, waiting for transfers between devices: 99.1 us -> none  [the longest x1 50.5 us: local(): lax.all_gather(normalized_input, 'tensor', axis=0, tiled=True)]
    psum x1 -> x0, waiting for transfers between devices: 97.3 us -> none  [local(): lax.psum((shared_part, norm_part, filter_part, head_part, gated_part), ('...]
    psum x3 -> x0, blocking collectives: 66.2 us -> none  [the longest x1 41.8 us: local(): lax.psum((shared_part, norm_part, filter_part, head_part, gated_part), ('...]
    unnamed x10 -> x0, waiting for transfers between devices: 51.3 us -> none
  transfers between devices with their start and end apart: 12 -> 10, of which waited for: 8 -> 0; matrix products, arithmetic and copies ran while one was open for 32% -> 22% of each run, Pallas kernels for 0% -> 45%
where the time goes in v1:
time: 407 us; the launch traced here: 400 us
  Pallas kernels  270 us (66%)
  local copies, waits for them, and re-layouts  49.7 us (12%)
  other arithmetic  40.6 us (10%)
  matrix products  22.7 us (6%)
  starting transfers between devices  14.3 us (4%)
    pallas_call x1, Pallas kernels, scatter_all(): pl.pallas_call(functools.partial(scatter_kernel, n_dp, n_ctx, n_z, ring,...  104 us
    pallas_call x1, Pallas kernels, gather_all(): pl.pallas_call(functools.partial(gather_kernel, n_dp, n_ctx, n_z, ring, z...  59 us
    pallas_call x1, Pallas kernels, run_pull_mix(): pl.pallas_call(functools.partial(pull_mix_kernel, nc), grid=(nc,), in_spe...  28.1 us
    unnamed x105, local copies, waits for them, and re-layouts  22 us
    pallas_call x1, Pallas kernels, run_entry(): pl.pallas_call(functools.partial(entry_kernel, nc), grid=(tokens // rows,...  20.6 us
    sub x7, other arithmetic, adamw(): weight - rate * (first_hat / (jnp.sqrt(second_hat) + adam_eps) + decay *...  15.5 us
    dot_general x1, matrix products, local(): lax.dot_general(normed, d_all, (((0,), (0,)), ((), ())), preferred_elemen...  14.3 us
    pallas_call x2, Pallas kernels, all_sum(): pl.pallas_call(functools.partial(all_sum_kernel, n_z), out_shape=jax.Shap...  13.5 us
  transfers between devices with their start and end apart: 10, of which 0 were waited for; matrix products, arithmetic and copies ran while one was open for 22% of the time, Pallas kernels for 45%

profile of v1, /device:TPU:0, one launch (start us, length us, event | category | flops | bytes accessed | tf_op | source)
XLA Modules:
  0.0 400.3 jit_solution(9003225687208349777)
XLA Ops:
  0.7 1.4 copy.137
  3.7 1.1 fusion.9.n_ref
  4.9 1.0 pad_maximum_fusion.4.w_ref
  5.8 59.0 %gather_all.1 = (bf16[1024,1536]{1,0:T(8,128)(2,1)}, bf16[1536,2304]{1,0:T(8,128)(2,1)}, bf16[16,1536]{1,0:T(8,128)(2,1)}) custom-call(bf16[256,1536]{1,0:T(8,128)(2,1)} %fusion.9.n_ref, bf16[192,2304]{1,0:T(8,128)(2,1)} %pad_maximum_fusion.4.w_ref), custom_call_target="tpu_custom_call" | custom-call | tf_op jit(solution)/shard_map/gather_all/pallas_call | solution.py:209
  64.9 3.0 collective-permute-start.6
  68.0 0.8 collective-permute-start.7
  69.3 2.2 collective-permute-start
  71.6 1.3 fusion.50
  73.4 0.7 slice_reduce_fusion.2
  74.7 1.4 copy.110
  76.2 2.1 slice.184
  80.1 2.3 fusion.19.ws_ref
  84.3 2.0 broadcast_compare_fusion
  87.7 0.7 eq.73
  88.4 0.7 compare_convert_fusion
  89.1 0.9 fusion.31
  90.1 0.7 stack.41
  90.8 1.0 copy.112.tok_ref
  91.9 1.5 fusion.34
  93.5 0.7 broadcast_in_dim.53.flag_ref
  94.2 20.6 %entry.1 = (f32[1024,768]{1,0:T(8,128)}, bf16[1024,1024]{1,0:T(8,128)(2,1)}, f32[1024,1024]{1,0:T(8,128)}, f32[1024,1024]{1,0:T(8,128)}, f32[1024,128]{1,0:T(8,1...) custom-call(bf16[1024,1536]{1,0:T(8,128)(2,1)} %get-tuple-element.98, ...), custom_call_target="tpu_custom_call" | custom-call | tf_op jit(solution)/shard_map/entry/pallas_call | solution.py:467
  114.8 1.6 collective-permute-start.1
  117.4 0.7 maximum_maximum_fusion.gain_ref.refs_8_
  118.0 0.7 copy-done.12
  118.8 12.3 %mix.1 = (f32[1024,768]{1,0:T(8,128)}, f32[8,128]{1,0:T(8,128)}) custom-call(f32[1024,1024]{1,0:T(8,128)} %get-tuple-element.101.act_ref, f32[1024,128]{1,0:T(8,128)} %get-tuple-element.102.del_ref, f32[1024,128]{1,0:T(8,128)} %get-tuple-element.103.cum_ref, f32[1024,8]{1,0:T(8,128)} %copy.112.tok_ref, f32[8,128]{1,0:T(8,128)} %convert_element_type.106.segr_ref, ...), custom_call_target="tpu_custom_call" | custom-call | tf_op jit(solution)/shard_map/mix/pallas_call | solution.py:587
  131.1 6.7 %all_sum.2.sq_ref = f32[8,128]{1,0:T(8,128)} custom-call(f32[8,128]{1,0:T(8,128)} %get-tuple-element.109.x_ref), custom_call_target="tpu_custom_call" | custom-call | tf_op jit(solution)/shard_map/all_sum/pallas_call | solution.py:262
  137.9 8.7 %exit.1 = (bf16[1024,768]{1,0:T(8,128)(2,1)}, bf16[256,1536]{1,0:T(8,128)(2,1)}, bf16[256,1536]{1,0:T(8,128)(2,1)}, bf16[256,1536]{1,0:T(8,128)(2,1)}, bf16[256,1536]{1,0:T(8,128)(2,1)}) custom-call(s32[1]{0:T(128)} %bitcast.1.g_ref, f32[1024,768]{1,0:T(8,128)} %get-tuple-element.108.mixed_ref.refs_5_, f32[1024,768]{1,0:T(8,128)} %get-tuple-element.107.gate_ref.refs_6_, ...), custom_call_target="tpu_custom_call" | custom-call | tf_op jit(solution)/shard_map/exit/pallas_call | solution.py:647
  146.6 12.7 %pull_exit.1 = (f32[1024,768]{1,0:T(8,128)}, f32[8,128]{1,0:T(8,128)}, bf16[1536,768]{1,0:T(8,128)(2,1)}) custom-call(s32[1]{0:T(128)} %bitcast.1.g_ref, bf16[256,1536]{1,0:T(8,128)(2,1)} %bitcast.19.refs_0_, bf16[256,1536]{1,0:T(8,128)(2,1)} %collective-permute-done.5.refs_1_, bf16[256,1536]{1,0:T(8,128)(2,1)} %collective-permute-done.6.refs_2_, ...), custom_call_target="tpu_custom_call" | custom-call | tf_op jit(solution)/shard_map/pull_exit/pallas_call | solution.py:719
  159.3 6.7 %all_sum.3.dot_ref = f32[8,128]{1,0:T(8,128)} custom-call(f32[8,128]{1,0:T(8,128)} %get-tuple-element.117.x_ref), custom_call_target="tpu_custom_call" | custom-call | tf_op jit(solution)/shard_map/all_sum/pallas_call | solution.py:262
  166.1 11.1 %pull_gate.1 = (f32[1024,768]{1,0:T(8,128)}, bf16[1024,768]{1,0:T(8,128)(2,1)}, f32[8,128,768]{2,1,0:T(8,128)}, f32[128,768]{1,0:T(8,128)}, f32[8,128]{1,0:T(8,128)}, /*index=5*/f32[8,768]{1,0:T(8,128)}) custom-call(f32[1024,768]{1,0:T(8,128)} %get-tuple-element.108.mixed_ref.refs_5_, f32[1024,768]{1,0:T(8,128)} %get-tuple-element.107.gate_ref.refs_6_, ...), custom_call_target="tpu_custom_call" | custom-call | tf_op jit(solution)/shard_map/pull_gate/pallas_call | solution.py:819
  177.2 1.3 collective-permute-start.8
  178.5 4.8 %slice.168 = bf16[1536,1536]{1,0:T(8,128)(2,1)} slice(bf16[1536,2304]{1,0:T(8,128)(2,1)} %get-tuple-element.99.w_ref.refs_4_), slice={[0:1536], [0:1536]} | slice | bytes 9437184 | tf_op jit(solution)/shard_map/slice | solution.py:1733
  183.8 1.8 collective-permute-start.3
  185.7 1.4 collective-permute-start.4
  187.2 0.7 copy-done.15
  187.9 28.1 %pull_mix.1 = (bf16[1024,1024]{1,0:T(8,128)(2,1)}, bf16[1024,128]{1,0:T(8,128)(2,1)}, f32[8,1024]{1,0:T(8,128)}, f32[16,1024]{1,0:T(8,128)}, f32[40,1024]{1,0:T(...) custom-call(f32[1024,1024]{1,0:T(8,128)} %get-tuple-element.119.u_ref, f32[1024,1024]{1,0:T(8,128)} %get-tuple-element.101.act_ref, ...), custom_call_target="tpu_custom_call" | custom-call | tf_op jit(solution)/shard_map/pull_mix/pallas_call | solution.py:1075
  216.0 0.9 bitcast_reduce_fusion
  216.9 0.8 bitcast_reduce_fusion.1
  217.8 0.8 reduce_sum.105
  218.7 0.7 bitcast_reduce_fusion.2
  219.4 1.5 collective-permute-start.9
  221.0 2.5 dynamic_update_slice.7
  223.5 1.4 add_dynamic-update-slice_fusion
  224.9 1.4 convert_dynamic-update-slice_fusion
  226.4 14.3 %multiply_reduce_fusion = (f32[1536]{0:T(1024)S(1)}, bf16[1536,1920]{1,0:T(8,128)(2,1)}, f32[1536,1920]{1,0:T(8,128)}) fusion(bf16[1536,304]{1,0:T(8,128)(2,1)} %copy.110, bf16[1536,1536]{1,0:T(8,128)(2,1)} %slice.168, bf16[1024,1536]{1,0:T(8,128)(2,1)} %get-tuple-element.98.n_ref, bf16[1024,128]{1,0:T(8,128)(2,1)S(1)} %dynamic_update_slice.7, ...), kind=kOutput, calls=%fused_computation.1 | convolution fusion | flops 6078134784 | bytes 30431232 | tf_op jit(solution)/shard_map/dot_general | solution.py:1735
  240.8 8.4 %fusion.2.refs_0_ = bf16[1024,1536]{1,0:T(8,128)(2,1)} fusion(bf16[1536,304]{1,0:T(8,128)(2,1)S(1)} %copy-done.7, bf16[1536,1536]{1,0:T(8,128)(2,1)S(1)} %bitcast.68, bf16[1024,128]{1,0:T(8,128)(2,1)S(1)} %dynamic_update_slice.7, bf16[1024,1024]{1,0:T(8,128)(2,1)S(1)} %copy-done.42, bf16[1024,768]{1,0:T(8,128)(2,1)S(1)} %copy-done.43), kind=kOutput, calls=%fused_computation.11 | convolution fusion | flops 6069288960 | bytes 12730368 | tf_op jit(solution)/shard_map/dot_general | solution.py:1734
  249.8 4.9 %fusion.49 = (bf16[1536,768]{1,0:T(8,128)(2,1)}, bf16[1536,768]{1,0:T(8,128)(2,1)}) fusion(bf16[1536,1920]{1,0:T(8,128)(2,1)} %get-tuple-element.289), kind=kLoop, calls=%fused_computation.123 | loop fusion | bytes 9437184 | tf_op jit(solution)/shard_map/slice | solution.py:1762
  254.7 3.2 slice.190.refs_1_
  257.9 103.7 %scatter_all.1 = (f32[256,1536]{1,0:T(8,128)}, f32[192,768]{1,0:T(8,128)}, f32[192,768]{1,0:T(8,128)}, f32[192,768]{1,0:T(8,128)}, f32[8,4,48,384]{3,2,1,0:T(8,128)}, /*index=5*/f32[4,64,128]{2,1,0:T(8,128)}) custom-call(bf16[1024,1536]{1,0:T(8,128)(2,1)} %fusion.2.refs_0_, f32[1536,384]{1,0:T(8,128)} %slice.190.refs_1_, ...), custom_call_target="tpu_custom_call" | custom-call | tf_op jit(solution)/shard_map/scatter_all/pallas_call | solution.py:1543
  361.6 1.0 copy.140
  362.6 4.8 %multiply_subtract_fusion.1 = (f32[192,2,768]{2,0,1:T(8,128)}, f32[192,2,768]{2,0,1:T(8,128)}, f32[192,2,768]{2,0,1:T(8,128)}, f32[192,2,768]{2,0,1:T(8,128)}) fusion(f32[192,2,768]{2,1,0:T(2,128)} %param.32, f32[192,1,768]{2,0,1:T(8,128)} %bitcast.71, f32[192,1,768]{2,0,1:T(8,128)} %bitcast.70, f32[192,2,768]{2,1,0:T(2,128)} %param.40, f32[192,2,768]{2,1,0:T(2,128)} %param.41), kind=kLoop, calls=%fused_computation.36 | loop fusion | flops 4718592 | bytes 9437184 | tf_op jit(solution)/shard_map/sub | solution.py:1569
  367.6 3.3 copy.122
  370.9 1.9 copy.123
  372.9 1.9 copy.124
  374.8 1.9 copy.125
  376.7 2.9 copy.126
  379.7 1.8 fusion.17
  381.7 3.6 fusion.16
  385.4 2.8 copy.121
  388.2 2.9 multiply_subtract_fusion.2
  391.2 5.1 %multiply_subtract_fusion = (f32[1536,304]{0,1:T(8,128)}, f32[1536,304]{0,1:T(8,128)}, f32[1536,304]{0,1:T(8,128)}) fusion(f32[1536,304]{0,1:T(8,128)S(1)} %copy-done.1, f32[1536,304]{0,1:T(8,128)S(1)} %copy-done.2, f32[1536,304]{0,1:T(8,128)S(1)} %copy-done.11, f32[1536,304]{0,1:T(8,128)} %param.43), kind=kLoop, calls=%fused_computation.15 | loop fusion | flops 7004160 | bytes 13074432 | tf_op jit(solution)/shard_map/sub | solution.py:1569
  396.4 0.6 multiply_subtract_fusion.4
  398.3 0.8 multiply_subtract_fusion.3
  399.0 0.8 copy.151
  (168 shorter events, 11.5 us)
Async XLA Ops:
  0.7 1.5 copy-start.8
  0.7 1.7 copy-start
  2.1 1.6 copy-start.16
  3.2 0.6 copy-start.29
  4.8 63.9 %copy-start.17 = (s32[1,1024]{1,0:T(1,128)S(1)}, s32[1,1024]{1,0:T(1,128)}, u32[]{:S(2)}) copy-start(s32[1,1024]{1,0:T(1,128)} %param.30) | copy-start | bytes 12292
  4.9 69.9 %copy-start.1 = (f32[1536,304]{0,1:T(8,128)S(1)}, f32[1536,304]{0,1:T(8,128)}, u32[]{:S(2)}) copy-start(f32[1536,304]{0,1:T(8,128)} %param.33) | copy-start | bytes 5603332
  64.9 81.7 %collective-permute-start.5 = (bf16[256,1536]{1,0:T(8,128)(2,1)}, bf16[256,1536]{1,0:T(8,128)(2,1)}, u32[]{:S(2)}, u32[]{:S(2)}) collective-permute-start(bf16[256,1536]{1,0:T(8,128)(2,1)} %bitcast.19.refs_0_), channel_id=1, source_target_pairs={{0,1},{1,2},{2,3},{3,0},{4,5},{5,6},{6,7},{7,4},{8,9},{9,10},{10,1... | collective-permute-start | bytes 2359304 | tf_op jit(solution)/shard_map/ppermute | solution.py:1561
  64.9 81.7 %collective-permute-start.6 = (bf16[256,1536]{1,0:T(8,128)(2,1)}, bf16[256,1536]{1,0:T(8,128)(2,1)}, u32[]{:S(2)}, u32[]{:S(2)}) collective-permute-start(bf16[256,1536]{1,0:T(8,128)(2,1)} %bitcast.19.refs_0_), channel_id=1, source_target_pairs={{0,2},{1,3},{2,0},{3,1},{4,6},{5,7},{6,4},{7,5},{8,10},{9,11},{10,... | collective-permute-start | bytes 2359304 | tf_op jit(solution)/shard_map/ppermute | solution.py:1561
  68.0 78.7 %collective-permute-start.7 = (bf16[256,1536]{1,0:T(8,128)(2,1)}, bf16[256,1536]{1,0:T(8,128)(2,1)}, u32[]{:S(2)}, u32[]{:S(2)}) collective-permute-start(bf16[256,1536]{1,0:T(8,128)(2,1)} %bitcast.19.refs_0_), channel_id=1, source_target_pairs={{0,3},{1,0},{2,1},{3,2},{4,7},{5,4},{6,5},{7,6},{8,11},{9,8},{10,9... | collective-permute-start | bytes 2359304 | tf_op jit(solution)/shard_map/ppermute | solution.py:1561
  69.3 14.3 %collective-permute-start = (s32[8]{0:T(128)}, s32[8]{0:T(128)}, u32[]{:S(2)}, u32[]{:S(2)}) collective-permute-start(s32[8]{0:T(128)} %slice_bitcast_fusion.5), channel_id=1, source_target_pairs={{0,4},{1,5},{2,6},{3,7},{8,12},{9,13},{10,14},{11,15},{16,20},{17,... | collective-permute-start | bytes 104 | tf_op jit(solution)/shard_map/ppermute | solution.py:1556
  76.2 2.1 copy-start.33
  76.2 3.7 slice-start.2
  78.3 4.1 %slice-start.3 = ((f32[5,3328]{1,0:T(8,128)}), f32[5,3072]{1,0:T(8,128)S(1)}, s32[]{:S(2)}) async-start(f32[5,3328]{1,0:T(8,128)} %param.34), calls=%async_computation.3 | async-start | bytes 196608 | tf_op jit(solution)/shard_map/slice | solution.py:1679
  78.3 4.1 %slice-start.4 = ((f32[5,3328]{1,0:T(8,128)}), f32[5,256]{1,0:T(8,128)S(1)}, s32[]{:S(2)}) async-start(f32[5,3328]{1,0:T(8,128)} %param.34), calls=%async_computation.4 | async-start | bytes 16384 | tf_op jit(solution)/shard_map/slice | solution.py:1680
  80.1 3.0 copy-start.40
  80.1 3.0 copy-start.41
  80.1 11.8 %copy-start.18 = (s32[1,1024]{1,0:T(1,128)S(1)}, s32[1,1024]{1,0:T(1,128)}, u32[]{:S(2)}) copy-start(s32[1,1024]{1,0:T(1,128)} %param.30) | copy-start | bytes 12292
  80.1 11.8 %copy-start.26 = (s32[7,1]{1,0:T(8,128)S(1)}, s32[7,1]{1,0:T(8,128)}, u32[]{:S(2)}) copy-start(s32[7,1]{1,0:T(8,128)} %get-tuple-element.300) | copy-start | bytes 88
  94.2 22.3 %copy-start.19 = (s32[1,1024]{1,0:T(1,128)S(1)}, s32[1,1024]{1,0:T(1,128)}, u32[]{:S(2)}) copy-start(s32[1,1024]{1,0:T(1,128)} %param.30) | copy-start | bytes 12292
  94.2 22.9 %copy-start.39 = (f32[12]{0:T(128)S(1)}, f32[12]{0:T(128)}, u32[]{:S(2)}) copy-start(f32[12]{0:T(128)} %get-tuple-element.304) | copy-start | bytes 148
  94.2 23.0 %copy-start.25 = (f32[3072]{0:T(1024)S(1)}, f32[3072]{0:T(1024)}, u32[]{:S(2)}) copy-start(f32[3072]{0:T(1024)} %param.36) | copy-start | bytes 36868
  114.8 3.2 collective-permute-start.1
  118.0 0.7 copy-start.12
  177.2 10.0 %collective-permute-start.8 = (f32[128,768]{1,0:T(8,128)}, f32[128,768]{1,0:T(8,128)S(1)}, u32[]{:S(2)}, u32[]{:S(2)}) collective-permute-start(f32[128,768]{1,0:T(8,128)} %get-tuple-element.125), channel_id=1, source_target_pairs={{4,0},{5,1},{6,2},{7,3},{12,8},{13,9},{14,10},{15,11},{20,16},{21,... | collective-permute-start | bytes 1179656 | tf_op jit(solution)/shard_map/ppermute | solution.py:1556
  178.5 8.6 %copy-start.24 = (f32[8,768]{1,0:T(8,128)S(1)}, f32[8,768]{1,0:T(8,128)}, u32[]{:S(2)}) copy-start(f32[8,768]{1,0:T(8,128)} %get-tuple-element.132) | copy-start | bytes 73732
  183.2 198.3 %collective-permute-start.2 = (bf16[256,1536]{1,0:T(8,128)(2,1)}, bf16[256,1536]{1,0:T(8,128)(2,1)}, u32[]{:S(2)}, u32[]{:S(2)}) collective-permute-start(bf16[256,1536]{1,0:T(8,128)(2,1)} %get-tuple-element.111), channel_id=1, source_target_pairs={{0,1},{1,2},{2,3},{3,0},{4,5},{5,6},{6,7},{7,4},{8,9},{9,10},{10,1... | collective-permute-start | bytes 2359304 | tf_op jit(solution)/shard_map/ppermute | solution.py:1561
  183.8 197.7 %collective-permute-start.3 = (bf16[256,1536]{1,0:T(8,128)(2,1)}, bf16[256,1536]{1,0:T(8,128)(2,1)}, u32[]{:S(2)}, u32[]{:S(2)}) collective-permute-start(bf16[256,1536]{1,0:T(8,128)(2,1)} %get-tuple-element.112), channel_id=1, source_target_pairs={{0,2},{1,3},{2,0},{3,1},{4,6},{5,7},{6,4},{7,5},{8,10},{9,11},{10,... | collective-permute-start | bytes 2359304 | tf_op jit(solution)/shard_map/ppermute | solution.py:1561
  185.7 195.9 %collective-permute-start.4 = (bf16[256,1536]{1,0:T(8,128)(2,1)}, bf16[256,1536]{1,0:T(8,128)(2,1)}, u32[]{:S(2)}, u32[]{:S(2)}) collective-permute-start(bf16[256,1536]{1,0:T(8,128)(2,1)} %get-tuple-element.113), channel_id=1, source_target_pairs={{0,3},{1,0},{2,1},{3,2},{4,7},{5,4},{6,5},{7,6},{8,11},{9,8},{10,9... | collective-permute-start | bytes 2359304 | tf_op jit(solution)/shard_map/ppermute | solution.py:1561
  187.1 0.7 copy-start.15
  219.4 4.1 %collective-permute-start.9 = (f32[8,1024]{1,0:T(8,128)}, f32[8,1024]{1,0:T(8,128)S(1)}, u32[]{:S(2)}, u32[]{:S(2)}) collective-permute-start(f32[8,1024]{1,0:T(8,128)} %get-tuple-element.129), channel_id=1, source_target_pairs={{4,0},{5,1},{6,2},{7,3},{12,8},{13,9},{14,10},{15,11},{20,16},{21,... | collective-permute-start | bytes 98312 | tf_op jit(solution)/shard_map/ppermute | solution.py:1556
  221.0 19.7 %slice-start = ((s8[4718592]{0:T(1024)(128)(4,1)}), s8[524288]{0:T(1024)(128)(4,1)S(1)}, s32[]{:S(2)}) async-start(s8[4718592]{0:T(1024)(128)(4,1)} %bitcast.67), calls=%async_computation | async-start | bytes 1048576
  226.4 14.4 %slice-start.1 = ((s8[4718592]{0:T(1024)(128)(4,1)}), s8[4194304]{0:T(1024)(128)(4,1)S(1)}, s32[]{:S(2)}) async-start(s8[4718592]{0:T(1024)(128)(4,1)} %bitcast.67), calls=%async_computation.1 | async-start | bytes 8388608
  226.4 14.4 %copy-start.7 = (bf16[1536,304]{1,0:T(8,128)(2,1)S(1)}, bf16[1536,304]{1,0:T(8,128)(2,1)}, u32[]{:S(2)}) copy-start(bf16[1536,304]{1,0:T(8,128)(2,1)} %copy.110) | copy-start | bytes 2801668
  226.4 14.4 %copy-start.42 = (bf16[1024,1024]{1,0:T(8,128)(2,1)S(1)}, bf16[1024,1024]{1,0:T(8,128)(2,1)}, u32[]{:S(2)}) copy-start(bf16[1024,1024]{1,0:T(8,128)(2,1)} %convert_dynamic-update-slice_fusion) | copy-start | bytes 6291460
  226.4 14.4 %copy-start.43 = (bf16[1024,768]{1,0:T(8,128)(2,1)S(1)}, bf16[1024,768]{1,0:T(8,128)(2,1)}, u32[]{:S(2)}) copy-start(bf16[1024,768]{1,0:T(8,128)(2,1)} %get-tuple-element.118) | copy-start | bytes 4718596
  367.6 3.4 copy-start.6
  367.6 5.3 %copy-start.5 = (f32[192,2,768]{2,0,1:T(8,128)S(1)}, f32[192,2,768]{2,0,1:T(8,128)}, u32[]{:S(2)}) copy-start(f32[192,2,768]{2,0,1:T(8,128)} %get-tuple-element.281) | copy-start | bytes 3538948
  370.9 3.9 copy-start.4
  379.6 2.0 copy-start.3
  379.6 2.1 copy-start.13
  379.6 2.1 copy-start.30
  379.6 2.1 copy-start.36
  379.7 17.3 %copy-start.23 = (f32[1536]{0:T(1024)}, f32[1536]{0:T(1024)S(1)}, u32[]{:S(2)}) copy-start(f32[1536]{0:T(1024)S(1)} %slice_reduce_fusion) | copy-start | bytes 18436
  385.3 2.9 copy-start.9
  385.3 2.9 copy-start.10
  388.1 8.2 %copy-start.22 = (f32[3072]{0:T(1024)}, f32[3072]{0:T(1024)S(1)}, u32[]{:S(2)}) copy-start(f32[3072]{0:T(1024)S(1)} %reshape.308) | copy-start | bytes 36868
  388.2 9.4 %copy-start.35 = (f32[3,48]{1,0:T(4,128)}, f32[3,48]{1,0:T(4,128)S(1)}, u32[]{:S(2)}) copy-start(f32[3,48]{1,0:T(4,128)S(1)} %reshape.307) | copy-start | bytes 1732
  388.2 2.9 copy-start.2
  388.2 2.9 copy-start.11
  391.1 5.2 %copy-start.27 = (f32[3072]{0:T(1024)S(1)}, f32[3072]{0:T(1024)}, u32[]{:S(2)}) copy-start(f32[3072]{0:T(1024)} %param.48) | copy-start | bytes 36868
  391.1 5.2 %copy-start.28 = (f32[3072]{0:T(1024)S(1)}, f32[3072]{0:T(1024)}, u32[]{:S(2)}) copy-start(f32[3072]{0:T(1024)} %param.49) | copy-start | bytes 36868
  391.1 5.8 %copy-start.31 = (f32[1536]{0:T(1024)S(1)}, f32[1536]{0:T(1024)}, u32[]{:S(2)}) copy-start(f32[1536]{0:T(1024)} %param.38) | copy-start | bytes 18436
  391.2 5.8 %copy-start.32 = (f32[1536]{0:T(1024)S(1)}, f32[1536]{0:T(1024)}, u32[]{:S(2)}) copy-start(f32[1536]{0:T(1024)} %param.39) | copy-start | bytes 18436
  391.2 6.5 %copy-start.34 = (f32[3,48]{1,0:T(4,128)S(1)}, f32[3,48]{1,0:T(4,128)}, u32[]{:S(2)}) copy-start(f32[3,48]{1,0:T(4,128)} %param.35) | copy-start | bytes 1732
  391.2 6.4 %copy-start.37 = (f32[3,48]{1,0:T(4,128)S(1)}, f32[3,48]{1,0:T(4,128)}, u32[]{:S(2)}) copy-start(f32[3,48]{1,0:T(4,128)} %param.46) | copy-start | bytes 1732
  391.2 6.4 %copy-start.38 = (f32[3,48]{1,0:T(4,128)S(1)}, f32[3,48]{1,0:T(4,128)}, u32[]{:S(2)}) copy-start(f32[3,48]{1,0:T(4,128)} %param.47) | copy-start | bytes 1732
  391.2 7.0 %copy-start.14 = (f32[5,3328]{1,0:T(8,128)S(1)}, f32[5,3328]{1,0:T(8,128)}, u32[]{:S(2)}) copy-start(f32[5,3328]{1,0:T(8,128)} %param.34) | copy-start | bytes 199684
  391.2 7.0 %copy-start.20 = (f32[5,3328]{1,0:T(8,128)S(1)}, f32[5,3328]{1,0:T(8,128)}, u32[]{:S(2)}) copy-start(f32[5,3328]{1,0:T(8,128)} %param.44) | copy-start | bytes 199684
  391.2 7.0 %copy-start.21 = (f32[5,3328]{1,0:T(8,128)S(1)}, f32[5,3328]{1,0:T(8,128)}, u32[]{:S(2)}) copy-start(f32[5,3328]{1,0:T(8,128)} %param.45) | copy-start | bytes 199684

commit v2 on v1

--- a/solution.py
+++ b/solution.py
@@ -6,6 +6,7 @@
 from jax.experimental import pallas as pl
 from jax.experimental.pallas import tpu as pltpu
 from jax.sharding import PartitionSpec as P
+
 
 HEADS = 48
 HEAD_DIM = 64
@@ -38,7 +39,7 @@
     return out
 
 
-def gather_kernel(n_dp, n_ctx, n_z, ring, zc, n_ref, w_ref, nf, wf, halo, *sems):
+def gather_kernel(n_dp, n_ctx, n_z, ring, zc, n_ref, w_ref, seg_ref, nf, wf, halo, pseg, *sems):
     z_send, z_recv, d_send, d_recv, c_send, c_recv, h_sem, l_sem = sems
     z, d, c = lax.axis_index("tensor"), lax.axis_index("dp"), lax.axis_index("ctx")
     pos = pick(d, [ring.index(i) for i in range(n_dp)])
@@ -170,6 +171,10 @@
         device_id_type=MESH,
     )
     edge.start()
+    ids = pltpu.make_async_remote_copy(
+        seg_ref, pseg, h_sem.at[2], h_sem.at[3], device_id={"ctx": c_next}, device_id_type=MESH
+    )
+    ids.start()
     for step in range(1, n_ctx):
         cc = lax.rem(c + n_ctx - step, n_ctx)
         for dist in range(n_dp):
@@ -179,6 +184,7 @@
                 if step < n_ctx - 1:
                     ccopy(cc, dd, h, False).start()
     edge.wait()
+    ids.wait()
     for k in range(zc):
         for dist in range(n_z):
 
@@ -200,7 +206,7 @@
                 ccopy(cc, pick(sp, ring), h, dist == 0 and step == 0).wait_send()
 
 
-def gather_all(dims, normed, weights):
+def gather_all(dims, normed, weights, seg):
     n_dp, n_ctx, n_z, ring = dims
     rows, width = normed.shape
     wr, wc = weights.shape
@@ -212,9 +218,10 @@
             jax.ShapeDtypeStruct((rows * n_z, width), normed.dtype),
             jax.ShapeDtypeStruct((wr * n_dp * n_ctx, wc), weights.dtype),
             jax.ShapeDtypeStruct((16, width), normed.dtype),
+            jax.ShapeDtypeStruct(seg.shape, seg.dtype),
         ),
-        in_specs=[pl.BlockSpec(memory_space=pltpu.VMEM)] * 2,
-        out_specs=tuple([pl.BlockSpec(memory_space=pl.ANY)] * 3),
+        in_specs=[pl.BlockSpec(memory_space=pltpu.VMEM)] * 3,
+        out_specs=tuple([pl.BlockSpec(memory_space=pl.ANY)] * 4),
         scratch_shapes=[
             dma((2, n_z, zc)),
             dma((n_z, zc)),
@@ -222,15 +229,15 @@
             dma((n_dp, 2)),
             dma((n_ctx, n_dp, 2)),
             dma((n_ctx, n_dp, 2)),
-            dma((2,)),
+            dma((4,)),
             dma((2,)),
         ],
         compiler_params=pltpu.CompilerParams(collective_id=0, has_side_effects=True),
         name="gather_all",
-    )(normed, weights)
-
-
-def all_sum_kernel(n_z, x_ref, o_ref, land, send, recv):
+    )(normed, weights, seg)
+
+
+def all_sum_kernel(n_z, x_ref, y_ref, ox_ref, oy_ref, land, send, recv):
     z = lax.axis_index("tensor")
     bar = pltpu.get_barrier_semaphore()
     for k in range(1, n_z):
@@ -239,39 +246,41 @@
         )
     pl.semaphore_wait(bar, n_z - 1)
     copies = []
-    for k in range(1, n_z):
-        copy = pltpu.make_async_remote_copy(
-            x_ref,
-            land.at[k - 1],
-            send.at[k - 1],
-            recv.at[k - 1],
-            device_id={"tensor": lax.rem(z + k, n_z)},
-            device_id_type=MESH,
-        )
-        copy.start()
-        copies.append(copy)
+    for n, ref in enumerate((x_ref, y_ref)):
+        for k in range(1, n_z):
+            copy = pltpu.make_async_remote_copy(
+                ref,
+                land.at[n, k - 1],
+                send.at[n, k - 1],
+                recv.at[n, k - 1],
+                device_id={"tensor": lax.rem(z + k, n_z)},
+                device_id_type=MESH,
+            )
+            copy.start()
+            copies.append(copy)
     for copy in copies:
         copy.wait()
-    total = x_ref[...]
-    for k in range(1, n_z):
-        total = total + land[k - 1]
-    o_ref[...] = total
-
-
-def all_sum(n_z, collective_id, x):
+    for n, (ref, out) in enumerate(((x_ref, ox_ref), (y_ref, oy_ref))):
+        total = ref[...]
+        for k in range(1, n_z):
+            total = total + land[n, k - 1]
+        out[...] = total
+
+
+def all_sum(n_z, collective_id, x, y):
     return pl.pallas_call(
         functools.partial(all_sum_kernel, n_z),
-        out_shape=jax.ShapeDtypeStruct(x.shape, x.dtype),
-        in_specs=[pl.BlockSpec(memory_space=pltpu.VMEM)],
-        out_specs=pl.BlockSpec(memory_space=pltpu.VMEM),
+        out_shape=(jax.ShapeDtypeStruct(x.shape, x.dtype),) * 2,
+        in_specs=[pl.BlockSpec(memory_space=pltpu.VMEM)] * 2,
+        out_specs=(pl.BlockSpec(memory_space=pltpu.VMEM),) * 2,
         scratch_shapes=[
-            pltpu.VMEM((n_z - 1,) + x.shape, x.dtype),
-            pltpu.SemaphoreType.DMA((n_z - 1,)),
-            pltpu.SemaphoreType.DMA((n_z - 1,)),
+            pltpu.VMEM((2, n_z - 1) + x.shape, x.dtype),
+            pltpu.SemaphoreType.DMA((2, n_z - 1)),
+            pltpu.SemaphoreType.DMA((2, n_z - 1)),
         ],
         compiler_params=pltpu.CompilerParams(collective_id=collective_id, has_side_effects=True),
         name="all_sum",
-    )(x)
+    )(x, y)
 
 
 def split2(a):
@@ -319,11 +328,6 @@
     )
 
 
-def halves(a):
-    keep = left_half(a.shape)
-    return jnp.where(keep, a, 0.0), jnp.where(keep, 0.0, a)
-
-
 def column(row):
     return jnp.broadcast_to(row, (LANES, LANES)).T
 
@@ -350,16 +354,72 @@
     return 1.0 / (1.0 + jnp.exp(-x))
 
 
+SEG, BACK1, BACK2, BACK3, BEFORE, LAST, KEEPS, REACHES, STAYS, THROUGH = range(10)
+
+
+class Masks:
+    def __init__(self, rows_ref, nc, chunk):
+        self.rows_ref, self.nc, self.chunk = rows_ref, nc, chunk
+        self.seg = column(self.row(SEG))
+
+    def row(self, kind):
+        return self.rows_ref[pl.ds(kind * self.nc + self.chunk, 1), :]
+
+    def same(self, kind):
+        return jnp.where(self.seg == column(self.row(kind)), 1.0, 0.0)
+
+
+def prep_kernel(x_ref, gain_ref, w_ref, we_ref, ws_ref, n_out, w_out, ws_out, buf, sem):
+    def plane(which):
+        return pltpu.make_async_copy(w_ref.at[:, which, :], buf.at[which], sem.at[which])
+
+    for which in range(2):
+        plane(which).start()
+    x = x_ref[...].astype(f32)
+    scale = lax.rsqrt(jnp.mean(x * x, axis=-1, keepdims=True) + norm_eps)
+    n_out[...] = (x * scale * gain_ref[...]).astype(bf16)
+    width = we_ref.shape[1]
+    w_out[:, 2 * width :] = we_ref[...].astype(bf16)
+    n = ws_ref.shape[0]
+    ws_out[:n] = ws_ref[...].astype(bf16)
+    ws_out[n:] = jnp.zeros((ws_out.shape[0] - n, ws_out.shape[1]), bf16)
+    for which in range(2):
+        plane(which).wait()
+        w_out[:, which * width : (which + 1) * width] = buf[which].astype(bf16)
+
+
+def run_prep(x, gain, w, we, ws):
+    rows, width = we.shape
+    n = ws.shape[0]
+    return pl.pallas_call(
+        prep_kernel,
+        out_shape=(
+            jax.ShapeDtypeStruct(x.shape, bf16),
+            jax.ShapeDtypeStruct((rows, 3 * width), bf16),
+            jax.ShapeDtypeStruct((n + -n % LANES, ws.shape[1]), bf16),
+        ),
+        in_specs=[pl.BlockSpec(memory_space=pltpu.VMEM)] * 2
+        + [pl.BlockSpec(memory_space=pl.ANY)]
+        + [pl.BlockSpec(memory_space=pltpu.VMEM)] * 2,
+        scratch_shapes=[pltpu.VMEM((2, rows, width), f32), pltpu.SemaphoreType.DMA((2,))],
+        name="prep",
+    )(x, gain, w, we, ws)
+
+
 def entry_kernel(
     nc,
+    per_group,
+    at_ref,
     n_ref,
     w_ref,
     ws_ref,
     halo_ref,
-    tok_ref,
-    flag_ref,
-    par_ref,
-    cf_ref,
+    seg_ref,
+    pseg_ref,
+    hp_ref,
+    gg_ref,
+    cfa_ref,
+    cfb_ref,
     gate_ref,
     v_ref,
     u_ref,
@@ -371,6 +431,9 @@
     fin_ref,
     thr_ref,
     vh_ref,
+    rows_ref,
+    par_ref,
+    gains_ref,
     vbuf,
     state,
     total,
@@ -379,18 +442,58 @@
     rows = n_ref.shape[0]
     width = gate_ref.shape[1]
     cols = v_ref.shape[1]
+    group, has_prev = at_ref[0], at_ref[1]
+    lane = lax.broadcasted_iota(jnp.int32, (8, LANES), 1)
+
+    def to_own(a):
+        moved = pltpu.roll(a, lax.rem(LANES - group * per_group, LANES), 1)
+        return jnp.where(lax.broadcasted_iota(jnp.int32, a.shape, 1) < per_group, moved, 0.0)
 
     @pl.when(i == 0)
     def _():
         hv = jnp.concatenate(
-            [dot(halo_ref[...], w_ref[:, width:]), dot(halo_ref[...], ws_ref[:, : 2 * STATE])],
+            [dot(halo_ref[...], w_ref[:, width:]), dot_nt(halo_ref[...], ws_ref[: 2 * STATE])],
             axis=1,
         )
-        hv = hv.astype(bf16).astype(f32) * par_ref[3:4, 0:1]
+        hv = jnp.where(has_prev > 0, hv.astype(bf16).astype(f32), 0.0)
         vbuf[0:8] = hv[8:16]
         vh_ref[...] = hv[8:16]
         state[...] = jnp.zeros_like(state)
         total[...] = jnp.zeros_like(total)
+
+        seg = seg_ref[...].astype(f32)
+        prev = jnp.where(has_prev > 0, pseg_ref[...].astype(f32), -1.0)
+        ahead = jnp.concatenate([prev[nc - 1 : nc], seg[: nc - 1]], axis=0)
+        ends = jnp.broadcast_to(seg[:, LANES - 1 :], (nc, LANES))
+        starts = jnp.broadcast_to(ahead[:, LANES - 1 :], (nc, LANES))
+        first = jnp.broadcast_to(prev[nc - 1 : nc, LANES - 1 :], (nc, LANES))
+        final = jnp.broadcast_to(seg[nc - 1 : nc, LANES - 1 :], (nc, LANES))
+        top = lax.broadcasted_iota(jnp.int32, (nc, LANES), 0) == 0
+        place = lax.broadcasted_iota(jnp.int32, (nc, LANES), 1)
+        kinds = [seg]
+        for k in range(1, CONV):
+            kinds.append(jnp.where(place < k, pltpu.roll(ahead, k, 1), pltpu.roll(seg, k, 1)))
+        kinds += [
+            starts,
+            ends,
+            jnp.where(ends == starts, 1.0, 0.0),
+            jnp.where(top | (starts == first), 1.0, 0.0),
+            jnp.where(ends == final, 1.0, 0.0),
+            jnp.where(final == first, 1.0, 0.0),
+        ]
+        for k, kind in enumerate(kinds):
+            rows_ref[k * nc : (k + 1) * nc] = kind
+        own = to_own(hp_ref[...])
+        par = jnp.where(
+            lax.broadcasted_iota(jnp.int32, (8, LANES), 0) == 1,
+            jnp.where(lane < per_group, -jnp.exp(own), 0.0),
+            own,
+        )
+        par_ref[...] = par
+        for j in range(width // LANES):
+            cs = slice(j * LANES, (j + 1) * LANES)
+            gains_ref[0:1, cs] = expand(par[2:3], j)
+            gains_ref[1:2, cs] = gg_ref[pl.ds(group * (width // LANES) + j, 1), :]
 
     @pl.when(i > 0)
     def _():
@@ -401,22 +504,26 @@
     vi = dot(n, w_ref[:, width:]).astype(bf16)
     v_ref[:, :width] = vi
     vbuf[8 : rows + 8, :width] = vi.astype(f32)
-    sh = dot(n, ws_ref[...])
+    sh = dot_nt(n, ws_ref[...])
     vb = sh[:, : 2 * STATE].astype(bf16)
     v_ref[:, width:] = vb
     vbuf[8 : rows + 8, width:] = vb.astype(f32)
-    raw = sh[:, 2 * STATE :] + par_ref[0:1, :]
+    raw = to_own(sh[:, 2 * STATE :]) + par_ref[0:1, :]
     delta = jnp.maximum(raw, 0.0) + jnp.log1p(jnp.exp(-jnp.abs(raw)))
     del_ref[...] = delta
     sig_ref[...] = sigmoid(raw)
     logdec = par_ref[1:2, :] * delta
 
-    masks = [jnp.broadcast_to(tok_ref[:, k : k + 1], (rows, LANES)) for k in range(3)]
+    chunks = [Masks(rows_ref, nc, i * (rows // CHUNK) + k) for k in range(rows // CHUNK)]
+    masks = [
+        jnp.concatenate([m.same(kind) for m in chunks], axis=0) for kind in (BACK3, BACK2, BACK1)
+    ]
     for j in range(cols // LANES):
         cs = slice(j * LANES, (j + 1) * LANES)
-        u = cf_ref[4:5, cs] + cf_ref[3:4, cs] * vbuf[8 : 8 + rows, cs]
+        cf = cfa_ref[:, cs] if j < width // LANES else cfb_ref[:, j * LANES - width :][:, :LANES]
+        u = cf[4:5] + cf[3:4] * vbuf[8 : 8 + rows, cs]
         for k in range(3):
-            u = u + cf_ref[k : k + 1, cs] * vbuf[5 + k : 5 + k + rows, cs] * masks[k]
+            u = u + cf[k : k + 1] * vbuf[5 + k : 5 + k + rows, cs] * masks[k]
         u_ref[:, cs] = u
         act_ref[:, cs] = u * sigmoid(u)
 
@@ -429,9 +536,9 @@
         cum = dot(tri3, jnp.concatenate(split3(logdec[ts]), axis=0))
         cum_ref[ts] = cum
         last = cum[CHUNK - 1 : CHUNK]
-        weight = jnp.exp(last - cum) * tok_ref[ts, 3:4] * delta[ts]
-        carry = jnp.exp(last) * flag_ref[pl.ds(chunk, 1), :]
-        thr_ref[pl.ds(chunk, 1), :] = jnp.exp(total[0:1]) * flag_ref[pl.ds(nc + chunk, 1), :]
+        weight = jnp.exp(last - cum) * chunks[k].same(LAST) * delta[ts]
+        carry = jnp.exp(last) * chunks[k].row(KEEPS)
+        thr_ref[pl.ds(chunk, 1), :] = jnp.exp(total[0:1]) * chunks[k].row(REACHES)
         total[0:1] = total[0:1] + last
         bt = lhs3(*split2(act_ref[ts, width : width + STATE].T))
         for j in range(width // LANES):
@@ -443,52 +550,67 @@
     @pl.when(i == pl.num_programs(0) - 1)
     def _():
         thr_ref[nc : nc + 8, :] = jnp.broadcast_to(
-            jnp.exp(total[0:1]) * flag_ref[3 * nc : 3 * nc + 1, :], (8, LANES)
+            jnp.exp(total[0:1]) * rows_ref[THROUGH * nc : THROUGH * nc + 1, :], (8, LANES)
         )
         fin_ref[...] = state[...]
 
 
-def run_entry(normed, weights, shared_ext, halo, tok, flags, par, cf, width):
+def run_entry(at, per_group, normed, weights, ws, halo, seg, pseg, hp, gg, conv_filter):
     tokens, d = normed.shape
     rows = 256
     nc = tokens // CHUNK
+    width = weights.shape[1] // 3
     cols = width + 2 * STATE
     one = pl.Buffered(1)
 
     def whole(shape):
-        return pl.BlockSpec(shape, lambda i: (0,) * len(shape), pipeline_mode=one)
+        return pl.BlockSpec(shape, lambda i, at: (0,) * len(shape), pipeline_mode=one)
 
     def by_row(w):
-        return pl.BlockSpec((rows, w), lambda i: (i, 0))
+        return pl.BlockSpec((rows, w), lambda i, at: (i, 0))
 
     def out(shape, dt=f32):
         return jax.ShapeDtypeStruct(shape, dt)
 
+    taps = conv_filter.shape[0]
     return pl.pallas_call(
-        functools.partial(entry_kernel, nc),
-        grid=(tokens // rows,),
-        in_specs=[
-            by_row(d),
-            whole((d, 2 * width)),
-            whole(shared_ext.shape),
-            whole(halo.shape),
-            by_row(tok.shape[1]),
-            whole(flags.shape),
-            whole(par.shape),
-            whole(cf.shape),
-        ],
-        out_specs=(
-            by_row(width),
-            by_row(cols),
-            by_row(cols),
-            by_row(cols),
-            by_row(LANES),
-            by_row(LANES),
-            by_row(LANES),
-            pl.BlockSpec((rows // CHUNK, STATE, width), lambda i: (i, 0, 0)),
-            whole((STATE, width)),
-            whole((nc + 8, LANES)),
-            whole((8, cols)),
+        functools.partial(entry_kernel, nc, per_group),
+        grid_spec=pltpu.PrefetchScalarGridSpec(
+            num_scalar_prefetch=1,
+            grid=(tokens // rows,),
+            in_specs=[
+                by_row(d),
+                whole((d, 2 * width)),
+                whole(ws.shape),
+                whole(halo.shape),
+                whole(seg.shape),
+                whole(pseg.shape),
+                whole(hp.shape),
+                whole(gg.shape),
+                pl.BlockSpec((taps, width), lambda i, at: (0, at[0])),
+                pl.BlockSpec((taps, 2 * STATE), lambda i, at: (0, DI // (2 * STATE))),
+            ],
+            out_specs=(
+                by_row(width),
+                by_row(cols),
+                by_row(cols),
+                by_row(cols),
+                by_row(LANES),
+                by_row(LANES),
+                by_row(LANES),
+                pl.BlockSpec((rows // CHUNK, STATE, width), lambda i, at: (i, 0, 0)),
+                whole((STATE, width)),
+                whole((nc + 8, LANES)),
+                whole((8, cols)),
+                whole((10 * nc, LANES)),
+                whole((8, LANES)),
+                whole((8, width)),
+            ),
+            scratch_shapes=[
+                pltpu.VMEM((rows + 8, cols), f32),
+                pltpu.VMEM((STATE, width), f32),
+                pltpu.VMEM((8, LANES), f32),
+            ],
         ),
         out_shape=(
             out((tokens, width)),
@@ -502,23 +624,20 @@
             out((STATE, width)),
             out((nc + 8, LANES)),
             out((8, cols)),
+            out((10 * nc, LANES)),
+            out((8, LANES)),
+            out((8, width)),
         ),
-        scratch_shapes=[
-            pltpu.VMEM((rows + 8, cols), f32),
-            pltpu.VMEM((STATE, width), f32),
-            pltpu.VMEM((8, LANES), f32),
-        ],
         compiler_params=pltpu.CompilerParams(dimension_semantics=("arbitrary",)),
         name="entry",
-    )(normed, weights, shared_ext, halo, tok, flags, par, cf)
+    )(at, normed, weights, ws, halo, seg, pseg, hp, gg, conv_filter, conv_filter)
 
 
 def mix_kernel(
     act_ref,
     del_ref,
     cum_ref,
-    tok_ref,
-    segr_ref,
+    rows_ref,
     s0_ref,
     sin_ref,
     thr_ref,
@@ -528,6 +647,7 @@
     sq_ref,
 ):
     chunk = pl.program_id(0)
+    masks = Masks(rows_ref, rows_ref.shape[0] // 10, chunk)
     width = gate_ref.shape[1]
     b = act_ref[:, width : width + STATE]
     c = act_ref[:, width + STATE :]
@@ -538,10 +658,9 @@
     cum = cum_ref[...]
     cum_t = cum.T
     r, s = ordered()
-    same = tok_ref[:, 5:6] == segr_ref[pl.ds(chunk, 1), :]
-    bias = jnp.where(same & (r >= s), 0.0, NEG)
+    bias = jnp.where((masks.seg == masks.row(SEG)) & (r >= s), 0.0, NEG)
     delta = del_ref[...]
-    ramp = jnp.exp(cum) * tok_ref[:, 4:5]
+    ramp = jnp.exp(cum) * masks.same(BEFORE)
     thr = thr_ref[pl.ds(chunk, 1), :]
     squares = jnp.zeros((CHUNK, LANES), f32)
     for j in range(width // LANES):
@@ -573,7 +692,7 @@
     sq_ref[pl.ds(chunk, 1), :] = dot_nt(ones, jnp.concatenate(split2(squares), axis=1))[0:1]
 
 
-def run_mix(act, delta, cum, tok, segr, s0, s_in, thr, gate, gains):
+def run_mix(act, delta, cum, table, s0, s_in, thr, gate, gains):
     tokens, cols = act.shape
     width = gate.shape[1]
     nc = tokens // CHUNK
@@ -591,8 +710,7 @@
             by_row(cols),
             by_row(LANES),
             by_row(LANES),
-            by_row(tok.shape[1]),
-            whole(segr.shape),
+            whole(table.shape),
             pl.BlockSpec((1, STATE, width), lambda i: (i, 0, 0)),
             whole(s_in.shape),
             whole(thr.shape),
@@ -606,7 +724,7 @@
         ),
         compiler_params=pltpu.CompilerParams(dimension_semantics=("arbitrary",)),
         name="mix",
-    )(act, delta, cum, tok, segr, s0, s_in, thr, gate, gains)
+    )(act, delta, cum, table, s0, s_in, thr, gate, gains)
 
 
 def exit_kernel(g_ref, mixed_ref, gate_ref, sq_ref, gain_ref, w_ref, gnorm_ref, *out_refs):
@@ -665,26 +783,26 @@
     )(group, mixed, gate, sq, gains, weights)
 
 
+def from_line(refs, groups, group, step):
+    pairs = [(refs[0], step == 0)]
+    for k in range(1, groups):
+        pairs.append((refs[k], (step == k) & (group >= k)))
+        pairs.append((refs[groups - 1 + k], (step == groups - k) & (group < groups - k)))
+    return pairs
+
+
 def pull_exit_kernel(groups, g_ref, *refs):
-    cot_refs, refs = refs[:groups], refs[groups:]
-    w_ref, mixed_ref, gate_ref, gnorm_ref, gain_ref, dgn_ref, dot_ref, gw_ref, acc = refs
+    n_cot = 2 * groups - 1
+    cot_refs, refs = refs[:n_cot], refs[n_cot:]
+    w_ref, mixed_ref, gate_ref, gain_ref, dgn_ref, dot_ref = refs
     i = pl.program_id(0)
     rows, width = mixed_ref.shape
     block = lax.rem(g_ref[0] + groups - i, groups)
-
-    @pl.when(i == 0)
-    def _():
-        acc[...] = jnp.zeros_like(acc)
-
-    for s, cot_ref in enumerate(cot_refs):
-
-        @pl.when(i == s)
+    for cot_ref, here in from_line(cot_refs, groups, g_ref[0], i):
+
+        @pl.when(here)
         def _(cot_ref=cot_ref):
-            cot = cot_ref[...]
-            dgn_ref[...] = dot(cot, w_ref[...])
-            acc[...] = acc[...] + lax.dot_general(
-                cot, gnorm_ref[...], (((0,), (0,)), ((), ())), preferred_element_type=f32
-            )
+            dgn_ref[...] = dot(cot_ref[...], w_ref[...])
 
     part = jnp.zeros((rows, LANES), f32)
     for j in range(width // LANES):
@@ -697,12 +815,55 @@
         row = dot_nt(ones, jnp.concatenate(split2(part[k * CHUNK : (k + 1) * CHUNK]), axis=1))
         dot_ref[pl.ds(block * (rows // CHUNK) + k, 1), :] = row[0:1]
 
+
+def exit_grad_kernel(groups, g_ref, *refs):
+    n_cot = 2 * groups - 1
+    cot_refs, (gnorm_ref, gw_ref, acc) = refs[:n_cot], refs[n_cot:]
+    i = pl.program_id(0)
+
+    @pl.when(i == 0)
+    def _():
+        acc[...] = jnp.zeros_like(acc)
+
+    for cot_ref, here in from_line(cot_refs, groups, g_ref[0], i):
+
+        @pl.when(here)
+        def _(cot_ref=cot_ref):
+            acc[...] = acc[...] + lax.dot_general(
+                cot_ref[...], gnorm_ref[...], (((0,), (0,)), ((), ())), preferred_element_type=f32
+            )
+
     @pl.when(i == groups - 1)
     def _():
         gw_ref[...] = acc[...].astype(bf16)
 
 
-def run_pull_exit(group, groups, cots, weights, mixed, gate, gnorm, gains):
+def run_exit_grad(group, groups, cots, gnorm):
+    _, width = gnorm.shape
+    rows, d = cots[0].shape
+
+    def whole(shape):
+        return pl.BlockSpec(
+            shape, lambda i, g: (0,) * len(shape), pipeline_mode=pl.Buffered(1)
+        )
+
+    return pl.pallas_call(
+        functools.partial(exit_grad_kernel, groups),
+        grid_spec=pltpu.PrefetchScalarGridSpec(
+            num_scalar_prefetch=1,
+            grid=(groups,),
+            in_specs=[whole((rows, d))] * len(cots)
+            + [pl.BlockSpec((rows, width), lambda i, g: (lax.rem(g[0] + groups - i, groups), 0))],
+            out_specs=whole((d, width)),
+            scratch_shapes=[pltpu.VMEM((d, width), f32)],
+        ),
+        out_shape=jax.ShapeDtypeStruct((d, width), bf16),
+        compiler_params=pltpu.CompilerParams(dimension_semantics=("arbitrary",)),
+        name="exit_grad",
+    )(group, *cots, gnorm)
+
+
+def run_pull_exit(group, groups, cots, weights, mixed, gate, gains):
     tokens, width = mixed.shape
     d = weights.shape[0]
     rows = tokens // groups
@@ -721,25 +882,22 @@
         grid_spec=pltpu.PrefetchScalarGridSpec(
             num_scalar_prefetch=1,
             grid=(groups,),
-            in_specs=[whole((rows, d))] * groups
+            in_specs=[whole((rows, d))] * len(cots)
             + [
                 whole((d, width), 2),
                 by_row(width),
                 by_row(width),
-                by_row(width),
                 whole(gains.shape),
             ],
-            out_specs=(by_row(width), whole((nc, LANES)), whole((d, width))),
-            scratch_shapes=[pltpu.VMEM((d, width), f32)],
+            out_specs=(by_row(width), whole((nc, LANES))),
         ),
         out_shape=(
             jax.ShapeDtypeStruct((tokens, width), f32),
             jax.ShapeDtypeStruct((nc, LANES), f32),
-            jax.ShapeDtypeStruct((d, width), bf16),
         ),
         compiler_params=pltpu.CompilerParams(dimension_semantics=("arbitrary",)),
         name="pull_exit",
-    )(group, *cots, weights, mixed, gate, gnorm, gains)
+    )(group, *cots, weights, mixed, gate, gains)
 
 
 def pull_gate_kernel(
@@ -751,9 +909,8 @@
     dot_ref,
     gain_ref,
     cum_ref,
-    tok_ref,
+    rows_ref,
     act_ref,
-    flag_ref,
     dmix_ref,
     dgate_ref,
     g0_ref,
@@ -778,9 +935,10 @@
     inner = column(dot_ref[pl.ds(chunk, 1), :]) / DI * (scale * scale * scale)
     cum = cum_ref[...]
     last = cum[CHUNK - 1 : CHUNK]
-    ramp = jnp.exp(cum) * tok_ref[:, 4:5]
-    carry = jnp.exp(last) * flag_ref[pl.ds(chunk, 1), :]
-    suf_ref[pl.ds(chunk, 1), :] = jnp.exp(total[0:1]) * flag_ref[pl.ds(2 * nc + chunk, 1), :]
+    masks = Masks(rows_ref, nc, chunk)
+    ramp = jnp.exp(cum) * masks.same(BEFORE)
+    carry = jnp.exp(last) * masks.row(KEEPS)
+    suf_ref[pl.ds(chunk, 1), :] = jnp.exp(total[0:1]) * masks.row(STAYS)
     total[0:1] = total[0:1] + last
     ct = lhs3(*split2(act_ref[...].T))
     for j in range(width // LANES):
@@ -803,10 +961,13 @@
     @pl.when(i == nc - 1)
     def _():
         dinc_ref[...] = grad[...]
-        gpart_ref[...] = gacc[...]
-
-
-def run_pull_gate(mixed, gate, dgn, sq, dots, gains, cum, tok, act, flags):
+        for j in range(width // LANES):
+            cs = slice(j * LANES, (j + 1) * LANES)
+            gpart_ref[j : j + 1] = jnp.sum(gacc[:, cs], axis=0, keepdims=True)
+        gpart_ref[width // LANES :] = jnp.zeros((8 - width // LANES, LANES), f32)
+
+
+def run_pull_gate(mixed, gate, dgn, sq, dots, gains, cum, table, act):
     tokens, width = mixed.shape
     nc = tokens // CHUNK
 
@@ -827,9 +988,8 @@
             whole(dots.shape),
             whole(gains.shape),
             by_row(LANES),
-            by_row(tok.shape[1]),
+            whole(table.shape),
             by_row(STATE, (width + STATE) // STATE),
-            whole(flags.shape),
         ],
         out_specs=(
             by_row(width),
@@ -837,7 +997,7 @@
             pl.BlockSpec((1, STATE, width), lambda i: (nc - 1 - i, 0, 0)),
             whole((STATE, width)),
             whole((nc, LANES)),
-            whole((8, width)),
+            whole((8, LANES)),
         ),
         out_shape=(
             jax.ShapeDtypeStruct((tokens, width), f32),
@@ -845,7 +1005,7 @@
             jax.ShapeDtypeStruct((nc, STATE, width), f32),
             jax.ShapeDtypeStruct((STATE, width), f32),
             jax.ShapeDtypeStruct((nc, LANES), f32),
-            jax.ShapeDtypeStruct((8, width), f32),
+            jax.ShapeDtypeStruct((8, LANES), f32),
         ),
         scratch_shapes=[
             pltpu.VMEM((STATE, width), f32),
@@ -854,11 +1014,13 @@
         ],
         compiler_params=pltpu.CompilerParams(dimension_semantics=("arbitrary",)),
         name="pull_gate",
-    )(mixed, gate, dgn, sq, dots, gains, cum, tok, act, flags)
+    )(mixed, gate, dgn, sq, dots, gains, cum, table, act)
 
 
 def pull_mix_kernel(
     nc,
+    per_group,
+    at_ref,
     u_ref,
     act_ref,
     v_ref,
@@ -868,8 +1030,7 @@
     del_ref,
     cum_ref,
     sig_ref,
-    tok_ref,
-    segr_ref,
+    rows_ref,
     s0_ref,
     sin_ref,
     fin_ref,
@@ -879,14 +1040,13 @@
     suf_ref,
     gain_ref,
     par_ref,
-    cf_ref,
+    cfa_ref,
+    cfb_ref,
     dv_ref,
     ddr_ref,
     dvh_ref,
     edge_ref,
-    fpart_ref,
-    hpart_ref,
-    spart_ref,
+    mrow_ref,
     du,
     q1,
     q2,
@@ -926,12 +1086,14 @@
     cum = cum_ref[...]
     cum_t = cum.T
     r, s = ordered()
-    allowed = (tok_ref[:, 5:6] == segr_ref[pl.ds(chunk, 1), :]) & (r <= s)
+    masks = Masks(rows_ref, nc, chunk)
+    allowed = (masks.seg == masks.row(SEG)) & (r <= s)
+    inside, fresh = masks.same(LAST), masks.same(BACK1)
     bias = jnp.where(allowed, 0.0, NEG)
     delta = del_ref[...]
     last = cum[CHUNK - 1 : CHUNK]
-    ramp = jnp.exp(cum) * tok_ref[:, 4:5]
-    tail = jnp.exp(last - cum) * tok_ref[:, 3:4]
+    ramp = jnp.exp(cum) * masks.same(BEFORE)
+    tail = jnp.exp(last - cum) * inside
     thr = thr_ref[pl.ds(chunk, 1), :]
     suf = suf_ref[pl.ds(chunk, 1), :]
     d_scores = jnp.zeros((CHUNK, CHUNK), f32)
@@ -1004,26 +1166,33 @@
     later = jnp.where(allowed, 1.0, 0.0).astype(bf16)
     later3 = jnp.concatenate([later, later, later], axis=1)
     ends = jnp.sum(bound, axis=0, keepdims=True)
-    d_logdec = dot(later3, jnp.concatenate(split3(flow), axis=0)) + ends * tok_ref[:, 3:4]
-    d_logdec = d_logdec * tok_ref[:, 2:3]
+    d_logdec = dot(later3, jnp.concatenate(split3(flow), axis=0)) + ends * inside
+    d_logdec = d_logdec * fresh
     ddr = (d_delta + d_logdec * par_ref[1:2, :]) * sig_ref[...]
-    ddr_ref[...] = ddr.astype(bf16)
+    ddr_ref[...] = pltpu.roll(ddr, at_ref[0] * per_group, 1).astype(bf16)
     hacc[0:8] = hacc[0:8] + fold8(ddr)
     hacc[8:16] = hacc[8:16] + fold8(d_logdec * par_ref[1:2, :] * delta)
 
-    masks = [jnp.broadcast_to(tok_ref[:, k : k + 1], (CHUNK, LANES)) for k in (2, 1, 0)]
+    alike = [fresh, masks.same(BACK2), masks.same(BACK3)]
+
+    def filter_of(j):
+        if j < width // LANES:
+            return cfa_ref[:, j * LANES : (j + 1) * LANES]
+        return cfb_ref[:, j * LANES - width : (j + 1) * LANES - width]
+
     for j in range(cols // LANES):
         cs = slice(j * LANES, (j + 1) * LANES)
+        cf = filter_of(j)
         d = du[:, cs]
         v = v_ref[:, cs].astype(f32)
-        dv = cf_ref[3:4, cs] * d
+        dv = cf[3:4] * d
         facc[32:40, cs] = facc[32:40, cs] + fold8(d)
         facc[24:32, cs] = facc[24:32, cs] + fold8(d * v)
         for n, q in enumerate(shifted, 1):
-            q[8 : 8 + CHUNK, cs] = d * masks[n - 1]
+            q[8 : 8 + CHUNK, cs] = d * alike[n - 1]
             moved = q[8 + n : 8 + n + CHUNK, cs]
             tap = CONV - 1 - n
-            dv = dv + cf_ref[tap : tap + 1, cs] * moved
+            dv = dv + cf[tap : tap + 1] * moved
             at = slice(8 * tap, 8 * tap + 8)
             facc[at, cs] = facc[at, cs] + fold8(moved * v)
         dv_ref[:, cs] = dv.astype(bf16)
@@ -1036,101 +1205,115 @@
     def _():
         for j in range(cols // LANES):
             cs = slice(j * LANES, (j + 1) * LANES)
+            cf = filter_of(j)
             vh = vh_ref[:, cs]
             dvh = jnp.zeros((8, LANES), f32)
             for n, q in enumerate(shifted, 1):
                 moved = q[n : n + 8, cs]
                 tap = CONV - 1 - n
-                dvh = dvh + cf_ref[tap : tap + 1, cs] * moved
+                dvh = dvh + cf[tap : tap + 1] * moved
                 at = slice(8 * tap, 8 * tap + 8)
                 facc[at, cs] = facc[at, cs] + moved * vh
             dvh_ref[:, cs] = dvh
-        fpart_ref[...] = facc[...]
-        hpart_ref[...] = hacc[...]
-        spart_ref[...] = sacc[...]
+        tiles = width // LANES
+        mrow_ref[...] = jnp.zeros_like(mrow_ref)
+        for tap in range(CONV + 1):
+            for j in range(cols // LANES):
+                at = tap * tiles + j if j < tiles else 5 * tiles + 8 + tap * 2 + j - tiles
+                part = facc[8 * tap : 8 * tap + 8, j * LANES : (j + 1) * LANES]
+                mrow_ref[at : at + 1] = jnp.sum(part, axis=0, keepdims=True)
+        skips = jnp.zeros((8, LANES), f32)
+        for j in range(tiles):
+            part = jnp.concatenate(split3(sacc[:, j * LANES : (j + 1) * LANES]), axis=1)
+            to_head = head_columns(j)
+            skips = skips + dot(part, jnp.concatenate([to_head] * 3, axis=0))
+        for k, part in enumerate((hacc[0:8], hacc[8:16], skips)):
+            row = jnp.broadcast_to(jnp.sum(part, axis=0, keepdims=True), (8, LANES))
+            at = 5 * tiles + k
+            mrow_ref[at : at + 1] = pltpu.roll(row, at_ref[0] * per_group, 1)[0:1]
 
 
 def run_pull_mix(
-    u, act, v, vh, dmix, mixed, delta, cum, sig, tok, segr, s0, s_in, fin, thr, g0, g_in, suf,
-    gains, par, cf,
+    at, per_group, u, act, v, vh, dmix, mixed, delta, cum, sig, table, s0, s_in, fin, thr, g0,
+    g_in, suf, gains, par, conv_filter,
 ):
     tokens, cols = u.shape
     width = dmix.shape[1]
     nc = tokens // CHUNK
+    taps = conv_filter.shape[0]
 
     def whole(shape):
         return pl.BlockSpec(
-            shape, lambda i: (0,) * len(shape), pipeline_mode=pl.Buffered(1)
+            shape, lambda i, at: (0,) * len(shape), pipeline_mode=pl.Buffered(1)
         )
 
     def by_row(w):
-        return pl.BlockSpec((CHUNK, w), lambda i: (nc - 1 - i, 0))
+        return pl.BlockSpec((CHUNK, w), lambda i, at: (nc - 1 - i, 0))
 
     def states():
-        return pl.BlockSpec((1, STATE, width), lambda i: (nc - 1 - i, 0, 0))
+        return pl.BlockSpec((1, STATE, width), lambda i, at: (nc - 1 - i, 0, 0))
 
     def out(shape, dt=f32):
         return jax.ShapeDtypeStruct(shape, dt)
 
     return pl.pallas_call(
-        functools.partial(pull_mix_kernel, nc),
-        grid=(nc,),
-        in_specs=[
-            by_row(cols),
-            by_row(cols),
-            by_row(cols),
-            whole(vh.shape),
-            by_row(width),
-            by_row(width),
-            by_row(LANES),
-            by_row(LANES),
-            by_row(LANES),
-            by_row(tok.shape[1]),
-            whole(segr.shape),
-            states(),
-            whole(s_in.shape),
-            whole(fin.shape),
-            whole(thr.shape),
-            states(),
-            whole(g_in.shape),
-            whole(suf.shape),
-            whole(gains.shape),
-            whole(par.shape),
-            whole(cf.shape),
-        ],
-        out_specs=(
-            by_row(cols),
-            by_row(LANES),
-            whole((8, cols)),
-            whole((16, cols)),
-            whole((40, cols)),
-            whole((16, LANES)),
-            whole((8, width)),
+        functools.partial(pull_mix_kernel, nc, per_group),
+        grid_spec=pltpu.PrefetchScalarGridSpec(
+            num_scalar_prefetch=1,
+            grid=(nc,),
+            in_specs=[
+                by_row(cols),
+                by_row(cols),
+                by_row(cols),
+                whole(vh.shape),
+                by_row(width),
+                by_row(width),
+                by_row(LANES),
+                by_row(LANES),
+                by_row(LANES),
+                whole(table.shape),
+                states(),
+                whole(s_in.shape),
+                whole(fin.shape),
+                whole(thr.shape),
+                states(),
+                whole(g_in.shape),
+                whole(suf.shape),
+                whole(gains.shape),
+                whole(par.shape),
+                pl.BlockSpec((taps, width), lambda i, at: (0, at[0])),
+                pl.BlockSpec((taps, 2 * STATE), lambda i, at: (0, DI // (2 * STATE))),
+            ],
+            out_specs=(
+                by_row(cols),
+                by_row(LANES),
+                whole((8, cols)),
+                whole((16, cols)),
+                whole((48, LANES)),
+            ),
+            scratch_shapes=[
+                pltpu.VMEM((CHUNK, cols), f32),
+                pltpu.VMEM((CHUNK + 16, cols), f32),
+                pltpu.VMEM((CHUNK + 16, cols), f32),
+                pltpu.VMEM((CHUNK + 16, cols), f32),
+                pltpu.VMEM((40, cols), f32),
+                pltpu.VMEM((16, LANES), f32),
+                pltpu.VMEM((8, width), f32),
+                pltpu.VMEM((STATE, width), f32),
+            ],
         ),
         out_shape=(
             out((tokens, cols), bf16),
             out((tokens, LANES), bf16),
             out((8, cols)),
             out((16, cols)),
-            out((40, cols)),
-            out((16, LANES)),
-            out((8, width)),
+            out((48, LANES)),
         ),
-        scratch_shapes=[
-            pltpu.VMEM((CHUNK, cols), f32),
-            pltpu.VMEM((CHUNK + 16, cols), f32),
-            pltpu.VMEM((CHUNK + 16, cols), f32),
-            pltpu.VMEM((CHUNK + 16, cols), f32),
-            pltpu.VMEM((40, cols), f32),
-            pltpu.VMEM((16, LANES), f32),
-            pltpu.VMEM((8, width), f32),
-            pltpu.VMEM((STATE, width), f32),
-        ],
         compiler_params=pltpu.CompilerParams(dimension_semantics=("arbitrary",)),
         name="pull_mix",
     )(
-        u, act, v, vh, dmix, mixed, delta, cum, sig, tok, segr, s0, s_in, fin, thr, g0, g_in, suf,
-        gains, par, cf,
+        at, u, act, v, vh, dmix, mixed, delta, cum, sig, table, s0, s_in, fin, thr, g0, g_in, suf,
+        gains, par, conv_filter, conv_filter,
     )
 
 
@@ -1284,9 +1467,8 @@
 
     @pl.when(outer)
     def _():
-        for n in range(3):
-            for k in range(zc):
-                lo_copy(n, k).start()
+        for k in range(zc):
+            lo_copy(0, k).start()
 
     @pl.when(inner)
     def _():
@@ -1369,73 +1551,87 @@
             block = (far_mate, far_z)[n]
             comb[n, k] = (dn_ref[dn_at(block, k)].astype(f32) + lo[n, k].astype(f32)).astype(bf16)
 
+        @pl.when(outer)
+        def _():
+            lo_copy(n, k).wait_send()
+            lo_copy(n + 1, k).start()
+
     def send_combined(n, k):
         @pl.when(inner)
         def _():
             comb_copy(n, k).start()
 
+    def small_sum():
+        for i in range(len(peers)):
+            small_copy(i).wait_recv()
+        total = small_ref[...]
+        for i in range(len(peers)):
+            total = total + sland[i]
+        ssum[...] = total
+        smalls_ref[z] = total
+
+    def shared_split():
+        for k in range(n_z):
+            acc_sh[k] = zsh[k * quarter : (k + 1) * quarter]
+
+    def shared_sum():
+        for k in range(1, n_z):
+            shared_z(k).wait_recv()
+        total = acc_sh[z]
+        for k in range(1, n_z):
+            total = total + zland[k - 1]
+        zsum[...] = total.astype(bf16)
+        shared_ref[mine, z] = total.astype(bf16)
+
+    quarter = wr // n_z
     first(0)
     first(1)
     send_first(0)
-    for i in range(len(peers)):
-        small_copy(i).wait_recv()
-    total = small_ref[...]
-    for i in range(len(peers)):
-        total = total + sland[i]
-    ssum[...] = total
-    smalls_ref[z] = total
     first(2)
+    small_sum()
+    second(0)
     send_first(1)
+    send_second(0)
     for k in range(1, n_z):
         small_z(k, z).start()
     first(3)
+    combine(0, 0)
+    third(0)
+    shared_split()
     send_first(2)
-    second(0)
+    send_combined(0, 0)
+    second(1)
+    for k in range(1, n_z):
+        shared_z(k).start()
+    send_second(1)
     send_first(3)
-    combine(0, 0)
-    send_second(0)
-    second(1)
-    send_combined(0, 0)
     combine(0, 1)
-    send_second(1)
-    third(0)
-    quarter = wr // n_z
-    for k in range(n_z):
-        acc_sh[k] = zsh[k * quarter : (k + 1) * quarter]
     second(2)
     send_combined(0, 1)
+    send_second(2)
+    shared_sum()
+    combine(1, 0)
     for k in range(1, n_z):
-        shared_z(k).start()
-    combine(1, 0)
-    send_second(2)
-    for k in range(1, n_z):
-        shared_z(k).wait_recv()
-    total = acc_sh[z]
-    for k in range(1, n_z):
-        total = total + zland[k - 1]
-    zsum[...] = total
-    shared_ref[mine, z] = total
+        shared_back(k, z).start()
+    third(1)
+    send_combined(1, 0)
     second(3)
-    send_combined(1, 0)
     send_second(3)
     for k in range(1, n_z):
-        shared_back(k, z).start()
+        shared_back(k, z_at(n_z - k)).wait_recv()
     combine(1, 1)
-    third(1)
-    send_combined(1, 1)
-    for k in range(1, n_z):
-        shared_back(k, z_at(n_z - k)).wait_recv()
     for r in range(1, n_dp):
         shared_dp(r, d).start()
     for s in range(1, n_ctx):
         shared_ctx(0, s, c).start()
     third(2)
+    send_combined(1, 1)
+    third(3)
     for r in range(1, n_dp):
         shared_dp(r, at[n_dp - r]).wait_recv()
     for r in range(1, n_dp):
         for s in range(1, n_ctx):
             shared_ctx(r, s, c).start()
-    third(3)
     for k in range(1, n_z):
         small_z(k, z_at(n_z - k)).wait_recv()
     for k in range(zc):
@@ -1469,9 +1665,8 @@
 
     @pl.when(outer)
     def _():
-        for n in range(3):
-            for k in range(zc):
-                lo_copy(n, k).wait_send()
+        for k in range(zc):
+            lo_copy(2, k).wait_send()
 
     @pl.when(inner)
     def _():
@@ -1511,7 +1706,10 @@
     outs = (
         [out(rows, d)]
         + [out(wr, w) for w in widths[1:]]
-        + [out(n_plane, n_z, quarter, widths[0]), out(n_z, *small.shape)]
+        + [
+            jax.ShapeDtypeStruct((n_plane, n_z, quarter, widths[0]), bf16),
+            out(n_z, *small.shape),
+        ]
     )
     scratch = (
         [vmem((n_ctx - 1, n_dp, wr, p.shape[1]), p.dtype) for p in parts]
@@ -1523,7 +1721,7 @@
             vmem((wr, widths[0]), f32),
             vmem((n_z, quarter, widths[0]), f32),
             vmem((n_z - 1, quarter, widths[0]), f32),
-            vmem((quarter, widths[0]), f32),
+            vmem((quarter, widths[0]), bf16),
             vmem((n_plane - 1,) + small.shape, f32),
             vmem(small.shape, f32),
             vmem((3, zc, rows // zc, d), bf16),
@@ -1551,6 +1749,185 @@
     )(d_normed, *parts, small)
 
 
+def update_kernel(
+    tiles, dn_ref, x_ref, cot_ref, ng_ref, *refs
+):
+    refs = list(refs)
+
+    def take(n):
+        return [refs.pop(0) for _ in range(n)]
+
+    parts = take(4)
+    gate_g, inner_g, exit_g, shared_g, smalls = take(5)
+    entry, leave, shared, norm, conv, head, gated = (take(3) for _ in range(7))
+    y_out, ig_out = take(2)
+    n_out, e_out, s_out, c_out, h_out, g_out, l_out = (take(4) for _ in range(7))
+    e_buf, e_new, e_in, e_back = take(4)
+    i = pl.program_id(0)
+
+    def fetch(n, which):
+        return pltpu.make_async_copy(
+            entry[n].at[:, which, :], e_buf.at[n, which], e_in.at[n, which]
+        )
+
+    def store(n, which):
+        return pltpu.make_async_copy(
+            e_new.at[n, which], e_out[n].at[:, which, :], e_back.at[n, which]
+        )
+
+    @pl.when(i == 0)
+    def _():
+        for which in range(2):
+            for n in range(3):
+                fetch(n, which).start()
+
+    for which, grad in ((0, gate_g), (1, inner_g)):
+
+        @pl.when(i == which + 1)
+        def _(which=which, grad=grad):
+            for n in range(3):
+                fetch(n, which).wait()
+            own = [e_buf[n, which] for n in range(3)]
+            new = adamw(own[0], grad[...], own[1], own[2], rate_matrix, decay_matrix)
+            for n in range(4):
+                e_new[n, which] = new[n]
+
+        @pl.when(i == which + 2)
+        def _(which=which):
+            for n in range(4):
+                store(n, which).start()
+
+    @pl.when(i == pl.num_programs(0) - 1)
+    def _():
+        for which in range(2):
+            for n in range(4):
+                store(n, which).wait()
+
+
+    def put(outs, values, at):
+        for ref, value in zip(outs, values, strict=True):
+            ref[at] = value
+
+    at = (slice(None), slice(None))
+    own = [ref[at] for ref in leave]
+    put(l_out, adamw(own[0], exit_g[...], own[1], own[2], rate_matrix, decay_matrix), at)
+    n = shared[0].shape[0]
+    g = shared_g[...].astype(f32).T[:n]
+    own = [ref[at] for ref in shared]
+    put(s_out, adamw(own[0], g, own[1], own[2], rate_matrix, decay_matrix), at)
+
+    @pl.when(i < 4)
+    def _():
+        x = x_ref[...].astype(f32)
+        y = x
+        for part in parts:
+            y = y + part[...].astype(f32)
+        y_out[...] = y.astype(bf16)
+        scale = lax.rsqrt(jnp.mean(x * x, axis=-1, keepdims=True) + norm_eps)
+        d_scaled = dn_ref[...] * ng_ref[...]
+        inner = jnp.mean(d_scaled * x, axis=-1, keepdims=True) * (scale * scale * scale)
+        value = cot_ref[...].astype(f32) + scale * d_scaled - x * inner
+        across = value.shape[1] // LANES
+        for k in range(across):
+            at = (pl.ds(k, value.shape[0], stride=across), slice(None))
+            ig_out[at] = value[:, k * LANES : (k + 1) * LANES]
+
+    @pl.when(i == 0)
+    def _():
+        n_z = smalls.shape[0]
+
+        def summed(lo, hi):
+            out = smalls[0, lo:hi]
+            for z in range(1, n_z):
+                out = out + smalls[z, lo:hi]
+            return out
+
+        for z in range(n_z):
+            g_out[0][z * tiles : (z + 1) * tiles] = smalls[z, :tiles]
+            for tap in range(CONV + 1):
+                for k in range(tiles):
+                    at = 8 + tap * tiles + k
+                    to = (z * tiles + k) * LANES
+                    c_out[0][tap : tap + 1, to : to + LANES] = smalls[z, at : at + 1]
+        bc = summed(16 + 5 * tiles, 26 + 5 * tiles)
+        for tap in range(CONV + 1):
+            for k in range(2):
+                to = (n_z * tiles + k) * LANES
+                c_out[0][tap : tap + 1, to : to + LANES] = bc[2 * tap + k : 2 * tap + k + 1]
+        heads = summed(8 + 5 * tiles, 11 + 5 * tiles)
+        h_out[0][...] = heads[:, : head[0].shape[1]]
+        n_out[0][...] = summed(56, 56 + norm[0].shape[0])
+        for outs, old in ((n_out, norm), (c_out, conv), (h_out, head), (g_out, gated)):
+            g = outs[0][...]
+            new = adamw(old[0][...], g, old[1][...], old[2][...], rate_vector, 0.0)
+            put(outs, new, at_all)
+
+
+at_all = (slice(None), slice(None))
+
+
+def run_update(dn, x, cot, ng, parts, grads, smalls, entry, leave, shared, norm, conv, head, gated):
+    steps = 6
+    tiles = leave[0].shape[1] // LANES
+    rows = leave[0].shape[0] // steps
+    d = dn.shape[1]
+    quarter = dn.shape[0] // 4
+    across = d // LANES
+
+    def clip(i):
+        return jnp.minimum(i, 3)
+
+    def whole(a):
+        return pl.BlockSpec(a.shape, lambda i: (0,) * a.ndim)
+
+    def by_row(a, n):
+        return pl.BlockSpec((n, a.shape[1]), lambda i: (i, 0))
+
+    token = pl.BlockSpec((quarter, d), lambda i: (clip(i), 0))
+    columns = pl.BlockSpec((shared[0].shape[0], d // steps), lambda i: (0, i))
+    e_spec = pl.BlockSpec(memory_space=pl.ANY)
+    l_spec = by_row(leave[0], rows)
+    groups = (
+        (norm, whole(norm[0])),
+        (entry, e_spec),
+        (shared, columns),
+        (conv, whole(conv[0])),
+        (head, whole(head[0])),
+        (gated, whole(gated[0])),
+        (leave, l_spec),
+    )
+    return pl.pallas_call(
+        functools.partial(update_kernel, tiles),
+        grid=(steps,),
+        in_specs=[token, token, token, whole(ng)]
+        + [token] * 4
+        + [whole(grads[0])] * 2
+        + [l_spec, pl.BlockSpec((d // steps, grads[3].shape[1]), lambda i: (i, 0)), whole(smalls)]
+        + [e_spec] * 3
+        + [l_spec] * 3
+        + [columns] * 3
+        + [whole(norm[0])] * 3
+        + [whole(conv[0])] * 3
+        + [whole(head[0])] * 3
+        + [whole(gated[0])] * 3,
+        out_specs=(token, pl.BlockSpec((quarter * across, LANES), lambda i: (clip(i), 0)))
+        + tuple(spec for _, spec in groups for _ in range(4)),
+        out_shape=(
+            jax.ShapeDtypeStruct(x.shape, bf16),
+            jax.ShapeDtypeStruct((x.shape[0] * across, LANES), f32),
+        )
+        + tuple(jax.ShapeDtypeStruct(a[0].shape, f32) for a, _ in groups for _ in range(4)),
+        scratch_shapes=[
+            pltpu.VMEM((3, 2) + leave[0].shape, f32),
+            pltpu.VMEM((4, 2) + leave[0].shape, f32),
+            pltpu.SemaphoreType.DMA((3, 2)),
+            pltpu.SemaphoreType.DMA((4, 2)),
+        ],
+        compiler_params=pltpu.CompilerParams(dimension_semantics=("arbitrary",)),
+        name="update",
+    )(dn, x, cot, ng, *parts, *grads, smalls, *entry, *leave, *shared, *norm, *conv, *head, *gated)
+
+
 def shift(block, axis, by):
     n = lax.axis_size(axis)
     return lax.ppermute(block, axis, [(i, i + by) for i in range(n) if 0 <= i + by < n])
@@ -1572,10 +1949,6 @@
 
 def per_lane(row):
     return jnp.repeat(row, HEAD_DIM, axis=-1)
-
-
-def pad_lanes(a):
-    return jnp.pad(a, ((0, 0),) * (a.ndim - 1) + ((0, LANES - a.shape[-1]),))
 
 
 def state_scan(through, final, axis, reverse):
@@ -1624,177 +1997,103 @@
     groups = lax.axis_size("tensor")
     per_group = HEADS // groups
     width = DI // groups
-    rows = block_in.shape[0]
+    rows, _, d = block_in.shape
     tokens = rows * groups
     nc = tokens // CHUNK
-    inputs = block_in[:, 0].astype(f32)
-    cot = cotangent[:, 0]
-    scale_in = lax.rsqrt(jnp.mean(inputs * inputs, axis=-1, keepdims=True) + norm_eps)
-    normed_own = (inputs * scale_in * norm_gain).astype(bf16)
-    w_own = jnp.concatenate(
-        [inward_weight[:, 0], inward_weight[:, 1], exit_weight], axis=1
-    ).astype(bf16)
-
-    seg = segments[0]
-    prev = shift(seg[-8:], "ctx", 1)
-    prev = jnp.where(lax.axis_index("ctx") > 0, prev, -1)
-    seg_pad = jnp.concatenate([prev[-3:], seg])
-    same = [(seg_pad[k : k + tokens] == seg).astype(f32) for k in range(3)]
-    chunks = seg.reshape(nc, CHUNK)
-    lasts = chunks[:, -1]
-    before = jnp.concatenate([prev[-1:], lasts[:-1]])
-    keep = (chunks == lasts[:, None]).astype(f32).reshape(-1)
-    inflow = (chunks == before[:, None]).astype(f32).reshape(-1)
-    zero = jnp.zeros_like(keep)
-    tok = jnp.stack(same + [keep, inflow, seg.astype(f32), zero, zero], axis=1)
-    segr = chunks.astype(f32)
-    reach = (before == prev[-1]).at[0].set(True)
-    flag = jnp.concatenate(
-        [
-            lasts == before,
-            reach,
-            lasts == lasts[-1],
-            jnp.broadcast_to(lasts[-1] == prev[-1], (nc,)),
-        ]
-    ).astype(f32)
-    flags = jnp.broadcast_to(flag[:, None], (4 * nc, LANES))
-
-    head_own = lax.dynamic_slice_in_dim(head_params, group * per_group, per_group, 1)
-    has_prev = jnp.broadcast_to((lax.axis_index("ctx") > 0).astype(f32), (1, LANES))
-    par = jnp.concatenate(
-        [
-            pad_lanes(head_own[0:1]),
-            pad_lanes(-jnp.exp(head_own[1:2])),
-            jnp.zeros((1, LANES), f32),
-            has_prev,
-            jnp.zeros((4, LANES), f32),
-        ]
+    x, cot = block_in[:, 0], cotangent[:, 0]
+    at = jnp.stack([group, (lax.axis_index("ctx") > 0).astype(jnp.int32)]).astype(jnp.int32)
+
+    seg = segments.reshape(nc, CHUNK)
+    hp = jnp.pad(head_params, ((0, 5), (0, LANES - HEADS)))
+    gg = gated_gain.reshape(-1, LANES)
+    normed_own, w_own, ws = run_prep(
+        x, norm_gain[None], inward_weight, exit_weight, shared_weight.T
     )
-    gain_own = lax.dynamic_slice_in_dim(gated_gain, group * width, width)
-    gains = jnp.concatenate(
-        [per_lane(head_own[2:3]), gain_own[None], jnp.zeros((6, width), f32)]
-    )
-    cf = jnp.concatenate(
-        [
-            lax.dynamic_slice_in_dim(conv_filter[:, :DI], group * width, width, 1),
-            conv_filter[:, DI:],
-        ],
-        axis=1,
-    )
-    cf = jnp.pad(cf, ((0, 3), (0, 0)))
-    delta_w = lax.dynamic_slice_in_dim(shared_weight[:, 2 * STATE :], group * per_group, per_group, 1)
-    shared_ext = jnp.concatenate(
-        [shared_weight[:, : 2 * STATE], pad_lanes(delta_w)], axis=1
-    ).astype(bf16)
-
-    shared_bf = jnp.pad(
-        shared_weight, ((0, 0), (0, -shared_weight.shape[1] % LANES))
-    ).astype(bf16)
-
-    normed, weights, halo = gather_all(dims, normed_own, w_own)
-
-    cot_out = lax.optimization_barrier((cot, halo))[0]
-    cots = [cot] + [turn(cot_out, "tensor", k) for k in range(1, groups)]
-
-    gate, v, u, act, delta, cum, sig, s0, fin, thr, vh = run_entry(
-        normed, weights, shared_ext, halo, tok, flags, par, cf, width
+    normed, weights, halo, pseg = gather_all(dims, normed_own, w_own, seg)
+
+    first = lax.optimization_barrier((cot, halo))[0]
+    lower, upper = [first], [first]
+    for _ in range(1, groups):
+        lower.append(shift(lower[-1], "tensor", 1))
+        upper.append(shift(upper[-1], "tensor", -1))
+    cots = [cot] + lower[1:] + upper[1:]
+
+    gate, v, u, act, delta, cum, sig, s0, fin, thr, vh, table, par, gains = run_entry(
+        at, per_group, normed, weights, ws, halo, seg, pseg, hp, gg, conv_filter
     )
     through = per_lane(thr[nc : nc + 1, :per_group])
     s_in = state_scan(through, fin, "ctx", False)
-    mixed, sq = run_mix(act, delta, cum, tok, segr, s0, s_in, thr, gate, gains)
-    sq = all_sum(groups, 1, sq)
-    group_at = group.astype(jnp.int32)[None]
+    mixed, sq = run_mix(act, delta, cum, table, s0, s_in, thr, gate, gains)
+    group_at = at[:1]
+    dgn, dots = run_pull_exit(group_at, groups, cots, weights, mixed, gate, gains)
+    sq, dots = all_sum(groups, 1, sq, dots)
     gnorm, *out_parts = run_exit(group_at, groups, mixed, gate, sq, gains, weights)
-    total = inputs + out_parts[0].astype(f32)
-    for k in range(1, groups):
-        total = total + turn(out_parts[k], "tensor", k).astype(f32)
-    block_output = total.astype(bf16)[:, None]
-
-    dgn, dots, exit_part = run_pull_exit(
-        group_at, groups, cots, weights, mixed, gate, gnorm, gains
-    )
-    dots = all_sum(groups, 2, dots)
+    out_parts = [out_parts[0]] + [turn(out_parts[k], "tensor", k) for k in range(1, groups)]
+    exit_part = run_exit_grad(group_at, groups, cots, gnorm)
     dmix, d_gate, g0, d_inc, suf, gpart = run_pull_gate(
-        mixed, gate, dgn, sq, dots, gains, cum, tok, act, flags
+        mixed, gate, dgn, sq, dots, gains, cum, table, act
     )
     g_in = state_scan(through, d_inc, "ctx", True)
-    d_v, d_raw, d_vh, edge, fpart, hpart, spart = run_pull_mix(
-        u, act, v, vh, dmix, mixed, delta, cum, sig, tok, segr, s0, s_in, fin, thr, g0, g_in, suf,
-        gains, par, cf,
+    d_v, d_raw, d_vh, edge, mrows = run_pull_mix(
+        at, per_group, u, act, v, vh, dmix, mixed, delta, cum, sig, table, s0, s_in, fin, thr, g0,
+        g_in, suf, gains, par, conv_filter,
     )
     from_next = shift(d_vh, "ctx", -1)
     edge = edge.at[8:].add(from_next).astype(bf16)
     d_v = lax.dynamic_update_slice_in_dim(d_v, edge, tokens - 16, 0)
 
-    d_raw = lax.dynamic_update_slice_in_dim(
-        jnp.zeros((tokens, LANES), bf16), d_raw[:, :per_group], group * per_group, 1
-    )
     d_all = jnp.concatenate([d_gate, d_v, d_raw], axis=1)
-    w_all = jnp.concatenate([weights[:, : 2 * width], shared_bf], axis=1)
-    back = lax.dot_general(d_all, w_all, NT, preferred_element_type=bf16)
+    back = (
+        lax.dot_general(d_all[:, : 2 * width], weights[:, : 2 * width], NT, preferred_element_type=f32)
+        + jnp.dot(d_all[:, 2 * width :], ws, preferred_element_type=f32)
+    ).astype(bf16)
     w_part = lax.dot_general(
         normed, d_all, (((0,), (0,)), ((), ())), preferred_element_type=f32
     )
+    w_all = jnp.concatenate([weights[:, : 2 * width], ws.T], axis=1)
     norm_part = jnp.sum(w_part * w_all.astype(f32), axis=1) / norm_gain
     shared_part = w_part[:, 2 * width :]
     w_part = w_part.astype(bf16)
     small = jnp.concatenate(
-        [
-            jnp.sum(gpart, axis=0),
-            jnp.sum(fpart[:, :width].reshape(CONV + 1, 8, width), axis=1).reshape(-1),
-            pad_lanes(
-                jnp.concatenate(
-                    [
-                        jnp.sum(hpart.reshape(2, 8, LANES), axis=1)[:, :per_group],
-                        jnp.sum(spart, axis=0).reshape(1, per_group, HEAD_DIM).sum(-1),
-                    ]
-                )
-            ).reshape(-1),
-            jnp.sum(fpart[:, width:].reshape(CONV + 1, 8, 2 * STATE), axis=1).reshape(-1),
-            norm_part,
-        ]
+        [gpart, mrows, jnp.pad(norm_part, (0, 16 * LANES - d)).reshape(16, LANES)]
     )
-    n_small = small.shape[0]
-    small = jnp.pad(small, (0, -n_small % (8 * LANES))).reshape(-1, LANES)
     d_normed, exit_grad, grad_gate, grad_inner, shared_sum, smalls = scatter_all(
         dims,
         back,
         [shared_part, exit_part, w_part[:, :width], w_part[:, width : 2 * width]],
         small,
     )
-    entry_grad = jnp.stack([grad_gate, grad_inner], axis=1)
-    shared_grad = shared_sum.reshape(w_part.shape[0], -1)[:, : 2 * STATE + HEADS]
-    d_scaled = d_normed * norm_gain
-    input_grad = (
-        cot.astype(f32)
-        + scale_in * d_scaled
-        - inputs * scale_in**3 * jnp.mean(d_scaled * inputs, axis=-1, keepdims=True)
-    )[:, None]
-    smalls = smalls.reshape(groups, -1)
-    sizes = [width, (CONV + 1) * width, 3 * LANES, (CONV + 1) * 2 * STATE, norm_gain.shape[0]]
-    ends = [sum(sizes[: k + 1]) for k in range(5)]
-    gated_grad, f_own, heads, f_shared, norm_grad = (
-        smalls[:, e - s : e] for s, e in zip(sizes, ends, strict=True)
+
+    def rows_of(a):
+        return a.reshape(-1, LANES)
+
+    out, d_in, *sets = run_update(
+        d_normed,
+        x,
+        cot,
+        norm_gain[None],
+        out_parts,
+        [grad_gate, grad_inner, exit_grad, shared_sum.reshape(d, -1)],
+        smalls,
+        [inward_weight, entry_first, entry_second],
+        [exit_weight, exit_first, exit_second],
+        [a.T for a in (shared_weight, shared_first, shared_second)],
+        [rows_of(a) for a in (norm_gain, norm_first, norm_second)],
+        [conv_filter, filter_first, filter_second],
+        [head_params, head_first, head_second],
+        [rows_of(a) for a in (gated_gain, gated_first, gated_second)],
     )
-    gated_grad = gated_grad.reshape(DI)
-    f_own = f_own.reshape(groups, CONV + 1, width).transpose(1, 0, 2).reshape(CONV + 1, DI)
-    filter_grad = jnp.concatenate(
-        [f_own, jnp.sum(f_shared, axis=0).reshape(CONV + 1, 2 * STATE)], axis=1
-    )
-    head_grad = (
-        heads.reshape(groups, 3, LANES)[:, :, :per_group].transpose(1, 0, 2).reshape(3, HEADS)
-    )
-    norm_grad = jnp.sum(norm_grad, axis=0)
+    n_set, e_set, s_set, c_set, h_set, g_set, l_set = (sets[4 * k : 4 * k + 4] for k in range(7))
     return (
-        block_output,
-        input_grad,
-        *adamw(norm_gain, norm_grad, norm_first, norm_second, rate_vector, 0.0),
-        *adamw(inward_weight, entry_grad, entry_first, entry_second, rate_matrix, decay_matrix),
-        *adamw(shared_weight, shared_grad, shared_first, shared_second, rate_matrix, decay_matrix),
-        *adamw(conv_filter, filter_grad, filter_first, filter_second, rate_vector, 0.0),
-        *adamw(head_params, head_grad, head_first, head_second, rate_vector, 0.0),
-        *adamw(gated_gain, gated_grad, gated_first, gated_second, rate_vector, 0.0),
-        *adamw(exit_weight, exit_grad, exit_first, exit_second, rate_matrix, decay_matrix),
+        out[:, None],
+        d_in.reshape(rows, 1, d),
+        *(a.reshape(-1) for a in n_set),
+        *e_set,
+        *(a.T for a in s_set),
+        *c_set,
+        *h_set,
+        *(a.reshape(-1) for a in g_set),
+        *l_set,
     )
 
 

time: 407 us -> 369 us (0.907); the launches traced: 400 us -> 367 us
  other arithmetic: 40.6 us -> 1.22 us
  waiting for transfers between devices: 0.03 us -> 35.5 us
  local copies, waits for them, and re-layouts: 49.7 us -> 15.6 us
  starting transfers between devices: 14.3 us -> 23.5 us
    ppermute x4 -> x9, waiting for transfers between devices: 0.01 us -> 35.4 us  [shift(): lax.ppermute(block, axis, [(i, i + by) for i in range(n) if 0 <= i + by <...]
    pallas_call x1, Pallas kernels: 104 us -> 77.6 us  [scatter_all(): pl.pallas_call(functools.partial(scatter_kernel, n_dp, n_ctx, n_z, ring,...]
    pallas_call x4 -> x6, Pallas kernels: 62.3 us -> 88 us  [the longest x1 28.6 us: run_pull_mix(): pl.pallas_call(functools.partial(pull_mix_kernel, nc, per_group), grid_sp...]
    unnamed x105 -> x38, local copies, waits for them, and re-layouts: 22 us -> 1.57 us
    sub x7 -> x0, other arithmetic: 15.5 us -> none  [adamw(): weight - rate * (first_hat / (jnp.sqrt(second_hat) + adam_eps) + decay *...]
    ppermute x4 -> x9, starting transfers between devices: 6.6 us -> 19.1 us  [shift(): lax.ppermute(block, axis, [(i, i + by) for i in range(n) if 0 <= i + by <...]
    slice x16 -> x1, local copies, waits for them, and re-layouts: 10.7 us -> 4.81 us  [local(): weights[:, :2 * width]]
    reduce_sum x10 -> x0, other arithmetic: 5.45 us -> none  [the longest x1 1.85 us: local(): jnp.mean(d_scaled * inputs, axis=-1, keepdims=True)]
  transfers between devices with their start and end apart: 10 -> 12, of which waited for: 0 -> 4; matrix products, arithmetic and copies ran while one was open for 22% -> 10% of each run, Pallas kernels for 45% -> 35%
where the time goes in v2:
time: 369 us; the launch traced here: 367 us
  Pallas kernels  267 us (72%)
  waiting for transfers between devices  35.5 us (10%)
  matrix products  23.8 us (6%)
  starting transfers between devices  23.5 us (6%)
  local copies, waits for them, and re-layouts  15.6 us (4%)
    pallas_call x1, Pallas kernels, scatter_all(): pl.pallas_call(functools.partial(scatter_kernel, n_dp, n_ctx, n_z, ring,...  77.6 us
    pallas_call x1, Pallas kernels, gather_all(): pl.pallas_call(functools.partial(gather_kernel, n_dp, n_ctx, n_z, ring, z...  59.1 us
    ppermute x9, waiting for transfers between devices, shift(): lax.ppermute(block, axis, [(i, i + by) for i in range(n) if 0 <= i + by <...  35.4 us
    pallas_call x1, Pallas kernels, run_pull_mix(): pl.pallas_call(functools.partial(pull_mix_kernel, nc, per_group), grid_sp...  28.6 us
    pallas_call x1, Pallas kernels, run_entry(): pl.pallas_call(functools.partial(entry_kernel, nc, per_group), grid_spec=...  21.6 us
    ppermute x9, starting transfers between devices, shift(): lax.ppermute(block, axis, [(i, i + by) for i in range(n) if 0 <= i + by <...  19.1 us
    pallas_call x1, Pallas kernels, run_update(): pl.pallas_call(functools.partial(update_kernel, tiles), grid=(steps,), in...  15.7 us
    dot_general x1, matrix products, local(): lax.dot_general(normed, d_all, (((0,), (0,)), ((), ())), preferred_elemen...  12.8 us
  transfers between devices with their start and end apart: 12, of which 4 were waited for; matrix products, arithmetic and copies ran while one was open for 10% of the time, Pallas kernels for 35%

profile of v2, /device:TPU:0, one launch (start us, length us, event | category | flops | bytes accessed | tf_op | source)
XLA Modules:
  0.0 367.4 jit_solution(945440265140280563)
XLA Ops:
  0.7 0.0 copy-start.1
  0.7 0.0 copy-start.15
  0.7 1.4 broadcast_in_dim.7.gain_ref.ng_ref
  2.1 4.8 %prep.1 = (bf16[256,1536]{1,0:T(8,128)(2,1)}, bf16[192,2304]{1,0:T(8,128)(2,1)}, bf16[384,1536]{1,0:T(8,128)(2,1)}) custom-call(bf16[256,1536]{1,0:T(8,128)(2,1)} %bitcast.43, f32[1,1536]{1,0:T(1,128)} %broadcast_in_dim.7.gain_ref.ng_ref, f32[192,2,768]{2,1,0:T(2,128)} %refs_9_.1, f32[192,768]{1,0:T(8,128)} %refs_12_.1, f32[304,1536]{1,0:T(8,128)} %bitcast.34), custom_call_target="tpu_custom_call" | custom-call | tf_op jit(solution)/shard_map/prep/pallas_call | solution.py:394
  6.9 59.1 %gather_all.1 = (bf16[1024,1536]{1,0:T(8,128)(2,1)}, bf16[1536,2304]{1,0:T(8,128)(2,1)}, bf16[16,1536]{1,0:T(8,128)(2,1)}, s32[8,128]{1,0:T(8,128)}) custom-call(bf16[256,1536]{1,0:T(8,128)(2,1)} %get-tuple-element.122.n_ref, bf16[192,2304]{1,0:T(8,128)(2,1)} %get-tuple-element.123.w_ref, s32[8,128]{1,0:T(8,128)} %bitcast.52), custom_call_target="tpu_custom_call" | custom-call | tf_op jit(solution)/shard_map/gather_all/pallas_call | solution.py:215
  66.0 1.3 collective-permute-start.1
  67.3 1.3 collective-permute-start.4
  68.6 16.2 %collective-permute-done.1.refs_1_ = bf16[256,1536]{1,0:T(8,128)(2,1)S(1)} collective-permute-done((bf16[256,1536]{1,0:T(8,128)(2,1)S(1)}, bf16[256,1536]{1,0:T(8,128)(2,1)S(1)}, u32[]{:S(2)}, u32[]{:S(2)}) %collective-permute-start.1) | collective-permute-done | bytes 786464 | tf_op jit(solution)/shard_map/ppermute | solution.py:1933
  84.8 4.4 %collective-permute-start.2 = (bf16[256,1536]{1,0:T(8,128)(2,1)S(1)}, bf16[256,1536]{1,0:T(8,128)(2,1)S(1)}, u32[]{:S(2)}, u32[]{:S(2)}) collective-permute-start(bf16[256,1536]{1,0:T(8,128)(2,1)S(1)} %collective-permute-done.1.refs_1_), channel_id=1, source_target_pairs={{0,1},{1,2},{2,3},{4,5},{5,6},{6,7},{8,9},{9,10},{10,11},{12,13},{... | collective-permute-start | bytes 2359304 | tf_op jit(solution)/shard_map/ppermute | solution.py:1933
  89.3 0.0 collective-permute-done.4.refs_4_
  89.3 0.0 copy-start.3
  89.3 1.3 collective-permute-start.5
  90.6 15.3 %collective-permute-done.2.refs_2_ = bf16[256,1536]{1,0:T(8,128)(2,1)S(1)} collective-permute-done((bf16[256,1536]{1,0:T(8,128)(2,1)S(1)}, bf16[256,1536]{1,0:T(8,128)(2,1)S(1)}, u32[]{:S(2)}, u32[]{:S(2)}) %collective-permute-start.2) | collective-permute-done | bytes 786464 | tf_op jit(solution)/shard_map/ppermute | solution.py:1933
  105.9 5.3 %collective-permute-start.3 = (bf16[256,1536]{1,0:T(8,128)(2,1)S(1)}, bf16[256,1536]{1,0:T(8,128)(2,1)}, u32[]{:S(2)}, u32[]{:S(2)}) collective-permute-start(bf16[256,1536]{1,0:T(8,128)(2,1)S(1)} %collective-permute-done.2.refs_2_), channel_id=1, source_target_pairs={{0,1},{1,2},{2,3},{4,5},{5,6},{6,7},{8,9},{9,10},{10,11},{12,13},{... | collective-permute-start | bytes 2359304 | tf_op jit(solution)/shard_map/ppermute | solution.py:1933
  111.2 0.0 collective-permute-done.5.refs_5_
  111.2 1.3 collective-permute-start.6
  112.5 0.0 copy-done.15
  112.5 0.6 pad.10.hp_ref
  113.1 0.6 pad_add_fusion.at_ref
  113.7 21.6 %entry.1 = (f32[1024,768]{1,0:T(8,128)}, bf16[1024,1024]{1,0:T(8,128)(2,1)}, f32[1024,1024]{1,0:T(8,128)}, f32[1024,1024]{1,0:T(8,128)}, f32[1024,128]{1,0:T(8,1...) custom-call(s32[2]{0:T(128)} %pad_add_fusion.at_ref, ...), custom_call_target="tpu_custom_call" | custom-call | tf_op jit(solution)/shard_map/entry/pallas_call | solution.py:576
  135.3 0.0 copy-done.2
  135.3 0.0 copy-done.3
  135.3 0.0 copy-done.4
  135.3 0.0 copy-done.5
  135.3 1.3 collective-permute-start
  136.6 1.5 collective-permute-done.sin_ref
  138.1 0.7 copy-done.8
  138.9 12.3 %mix.1 = (f32[1024,768]{1,0:T(8,128)}, f32[8,128]{1,0:T(8,128)}) custom-call(f32[1024,1024]{1,0:T(8,128)} %get-tuple-element.129.act_ref, f32[1024,128]{1,0:T(8,128)} %get-tuple-element.130.del_ref, f32[1024,128]{1,0:T(8,128)} %get-tuple-element.131.cum_ref, f32[80,128]{1,0:T(8,128)} %get-tuple-element.132.rows_ref, ...), custom_call_target="tpu_custom_call" | custom-call | tf_op jit(solution)/shard_map/mix/pallas_call | solution.py:706
  151.1 0.0 collective-permute-done.3.refs_3_
  151.1 0.0 collective-permute-done.6.refs_6_
  151.2 9.7 %pull_exit.1 = (f32[1024,768]{1,0:T(8,128)}, f32[8,128]{1,0:T(8,128)}) custom-call(s32[1]{0:T(128)} %bitcast.g_ref, bf16[256,1536]{1,0:T(8,128)(2,1)} %bitcast.36, bf16[256,1536]{1,0:T(8,128)(2,1)} %copy-done.2, bf16[256,1536]{1,0:T(8,128)(2,1)} %copy-done.4, bf16[256,1536]{1,0:T(8,128)(2,1)} %collective-permute-done.3.refs_3_, bf16[256,1536]{1,0:T(8,128)(2,1)} %copy-done.3, ...), custom_call_target="tpu_custom_call" | custom-call | tf_op jit(solution)/shard_map/pull_exit/pallas_call | solution.py:880
  160.8 8.9 %all_sum.1 = (f32[8,128]{1,0:T(8,128)}, f32[8,128]{1,0:T(8,128)}) custom-call(f32[8,128]{1,0:T(8,128)} %get-tuple-element.141.x_ref, f32[8,128]{1,0:T(8,128)} %get-tuple-element.142.y_ref), custom_call_target="tpu_custom_call" | custom-call | tf_op jit(solution)/shard_map/all_sum/pallas_call | solution.py:271
  169.7 11.2 %pull_gate.1 = (f32[1024,768]{1,0:T(8,128)}, bf16[1024,768]{1,0:T(8,128)(2,1)}, f32[8,128,768]{2,1,0:T(8,128)}, f32[128,768]{1,0:T(8,128)}, f32[8,128]{1,0:T(8,128)}, /*index=5*/f32[8,128]{1,0:T(8,128)}) custom-call(f32[1024,768]{1,0:T(8,128)} %get-tuple-element.138.refs_8_.mixed_ref, f32[1024,768]{1,0:T(8,128)} %get-tuple-element.136.gate_ref.refs_9_, ...), custom_call_target="tpu_custom_call" | custom-call | tf_op jit(solution)/shard_map/pull_gate/pallas_call | solution.py:980
  180.9 1.5 collective-permute-start.7
  182.4 2.3 collective-permute-done.7.gin_ref
  184.8 0.7 copy-done.10
  185.5 28.6 %pull_mix.1 = (bf16[1024,1024]{1,0:T(8,128)(2,1)}, bf16[1024,128]{1,0:T(8,128)(2,1)}, f32[8,1024]{1,0:T(8,128)}, f32[16,1024]{1,0:T(8,128)}, f32[48,128]{1,0:T(8,128)}) custom-call(s32[2]{0:T(128)} %pad_add_fusion.at_ref, f32[1024,1024]{1,0:T(8,128)} %get-tuple-element.146.u_ref, f32[1024,1024]{1,0:T(8,128)} %get-tuple-element.129.act_ref, ...), custom_call_target="tpu_custom_call" | custom-call | tf_op jit(solution)/shard_map/pull_mix/pallas_call | solution.py:1259
  214.1 0.0 copy-start
  214.1 1.4 collective-permute-start.8
  215.6 4.8 %slice.42 = bf16[1536,1536]{1,0:T(8,128)(2,1)} slice(bf16[1536,2304]{1,0:T(8,128)(2,1)} %get-tuple-element.125.w_ref.refs_7_), slice={[0:1536], [0:1536]} | slice | bytes 9437184 | tf_op jit(solution)/shard_map/slice | solution.py:2047
  220.4 1.4 copy.54
  221.8 8.7 %exit.1 = (bf16[1024,768]{1,0:T(8,128)(2,1)}, bf16[256,1536]{1,0:T(8,128)(2,1)}, bf16[256,1536]{1,0:T(8,128)(2,1)}, bf16[256,1536]{1,0:T(8,128)(2,1)}, bf16[256,1536]{1,0:T(8,128)(2,1)}) custom-call(s32[1]{0:T(128)} %bitcast.g_ref, f32[1024,768]{1,0:T(8,128)} %get-tuple-element.138.refs_8_.mixed_ref, f32[1024,768]{1,0:T(8,128)} %get-tuple-element.136.gate_ref.refs_9_, ...), custom_call_target="tpu_custom_call" | custom-call | tf_op jit(solution)/shard_map/exit/pallas_call | solution.py:765
  230.5 2.4 collective-permute-start.10
  232.9 1.4 collective-permute-start.11
  234.3 0.6 collective-permute-start.9
  234.9 8.4 %exit_grad.1.refs_2_ = bf16[1536,768]{1,0:T(8,128)(2,1)} custom-call(s32[1]{0:T(128)} %bitcast.g_ref, bf16[256,1536]{1,0:T(8,128)(2,1)} %bitcast.37, bf16[256,1536]{1,0:T(8,128)(2,1)} %copy-done.2, bf16[256,1536]{1,0:T(8,128)(2,1)} %copy-done.4, bf16[256,1536]{1,0:T(8,128)(2,1)} %collective-permute-done.3.refs_3_, bf16[256,1536]{1,0:T(8,128)(2,1)} %copy-done.3, ...), custom_call_target="tpu_custom_call" | custom-call | tf_op jit(solution)/shard_map/exit_grad/pallas_call | solution.py:850
  243.3 0.0 collective-permute-done.8
  243.4 0.0 copy-done.7
  243.4 0.0 copy-start.9
  243.4 0.0 copy-start.11
  243.4 7.6 %fusion.6 = f32[1024,1536]{1,0:T(8,128)S(1)} fusion(bf16[1024,1024]{1,0:T(8,128)(2,1)S(1)} %convert_dynamic-update-slice_fusion, bf16[1024,768]{1,0:T(8,128)(2,1)} %get-tuple-element.145, bf16[1536,2304]{1,0:T(8,128)(2,1)} %get-tuple-element.125.w_ref.refs_7_), kind=kOutput, calls=%fused_computation.9 | convolution fusion | flops 4838129664 | bytes 14680064 | tf_op jit(solution)/shard_map/dot_general | solution.py:2047
  251.0 0.0 copy-start.13
  251.0 12.8 %multiply_reduce_fusion = (f32[1536]{0:T(1024)S(1)}, bf16[1536,1920]{1,0:T(8,128)(2,1)}, f32[1536,1920]{1,0:T(8,128)}) fusion(bf16[1536,384]{1,0:T(8,128)(2,1)S(1)} %bitcast.48, bf16[1536,1536]{1,0:T(8,128)(2,1)} %slice.42, bf16[1024,1536]{1,0:T(8,128)(2,1)S(1)} %copy-done.6, bf16[1024,128]{1,0:T(8,128)(2,1)S(1)} %copy-done.11, ...), kind=kOutput, calls=%fused_computation | convolution fusion | flops 6072236544 | bytes 30676992 | tf_op jit(solution)/shard_map/dot_general | solution.py:2050
  263.9 0.0 slice-start
  263.9 3.4 slice.47.refs_1_
  267.3 3.4 add_convert_fusion.refs_0_
  270.7 0.0 copy-done.14
  270.7 0.6 pad_maximum_fusion.4.refs_5_
  271.3 2.4 fusion.13
  273.8 77.6 %scatter_all.1 = (f32[256,1536]{1,0:T(8,128)}, f32[192,768]{1,0:T(8,128)}, f32[192,768]{1,0:T(8,128)}, f32[192,768]{1,0:T(8,128)}, bf16[8,4,48,384]{3,2,1,0:T(8,128)(2,1)}, /*index=5*/f32[4,72,128]{2,1,0:T(8,128)}) custom-call(bf16[1024,1536]{1,0:T(8,128)(2,1)} %add_convert_fusion.refs_0_, f32[1536,384]{1,0:T(8,128)} %slice.47.refs_1_, ...), custom_call_target="tpu_custom_call" | custom-call | tf_op jit(solution)/shard_map/scatter_all/pallas_call | solution.py:1741
  351.4 0.0 collective-permute-done.10.refs_2_
  351.4 0.0 collective-permute-done.11.refs_3_
  351.5 0.0 collective-permute-done.9.refs_1_
  351.5 15.7 %update.1 = (bf16[256,1536]{1,0:T(8,128)(2,1)}, f32[3072,128]{1,0:T(8,128)}, f32[12,128]{1,0:T(8,128)}, f32[12,128]{1,0:T(8,128)}, f32[12,128]{1,0:T(8,128)}, /*...) custom-call(f32[256,1536]{1,0:T(8,128)} %get-tuple-element.162.dn_re, ...), custom_call_target="tpu_custom_call" | custom-call | tf_op jit(solution)/shard_map/update/pallas_call | solution.py:1899
  (26 shorter events, 0.1 us)
Async XLA Ops:
  0.7 65.3 %copy-start.1 = (bf16[256,1,1536]{2,0,1:T(8,128)(2,1)S(1)}, bf16[256,1,1536]{2,0,1:T(8,128)(2,1)}, u32[]{:S(2)}) copy-start(bf16[256,1,1536]{2,0,1:T(8,128)(2,1)} %param.27) | copy-start | bytes 2359300
  0.7 111.8 %copy-start.15 = (f32[3,48]{1,0:T(4,128)S(1)}, f32[3,48]{1,0:T(4,128)}, u32[]{:S(2)}) copy-start(f32[3,48]{1,0:T(4,128)} %refs_24_.1) | copy-start | bytes 1732
  66.0 18.9 %collective-permute-start.1 = (bf16[256,1536]{1,0:T(8,128)(2,1)S(1)}, bf16[256,1536]{1,0:T(8,128)(2,1)S(1)}, u32[]{:S(2)}, u32[]{:S(2)}) collective-permute-start(bf16[256,1536]{1,0:T(8,128)(2,1)S(1)} %bitcast.39), channel_id=1, source_target_pairs={{0,1},{1,2},{2,3},{4,5},{5,6},{6,7},{8,9},{9,10},{10,11},{12,13},{... | collective-permute-start | bytes 2359304 | tf_op jit(solution)/shard_map/ppermute | solution.py:1933
  67.3 22.0 %collective-permute-start.4 = (bf16[256,1536]{1,0:T(8,128)(2,1)S(1)}, bf16[256,1536]{1,0:T(8,128)(2,1)S(1)}, u32[]{:S(2)}, u32[]{:S(2)}) collective-permute-start(bf16[256,1536]{1,0:T(8,128)(2,1)S(1)} %bitcast.40), channel_id=1, source_target_pairs={{1,0},{2,1},{3,2},{5,4},{6,5},{7,6},{9,8},{10,9},{11,10},{13,12},{... | collective-permute-start | bytes 2359304 | tf_op jit(solution)/shard_map/ppermute | solution.py:1933
  84.8 50.4 %copy-start.2 = (bf16[256,1536]{1,0:T(8,128)(2,1)}, bf16[256,1536]{1,0:T(8,128)(2,1)S(1)}, u32[]{:S(2)}) copy-start(bf16[256,1536]{1,0:T(8,128)(2,1)S(1)} %collective-permute-done.1.refs_1_) | copy-start | bytes 2359300
  84.8 21.1 %collective-permute-start.2 = (bf16[256,1536]{1,0:T(8,128)(2,1)S(1)}, bf16[256,1536]{1,0:T(8,128)(2,1)S(1)}, u32[]{:S(2)}, u32[]{:S(2)}) collective-permute-start(bf16[256,1536]{1,0:T(8,128)(2,1)S(1)} %collective-permute-done.1.refs_1_), channel_id=1, source_target_pairs={{0,1},{1,2},{2,3},{4,5},{5,6},{6,7},{8,9},{9,10},{10,11},{12,13},{... | collective-permute-start | bytes 2359304 | tf_op jit(solution)/shard_map/ppermute | solution.py:1933
  89.3 46.0 %copy-start.3 = (bf16[256,1536]{1,0:T(8,128)(2,1)}, bf16[256,1536]{1,0:T(8,128)(2,1)S(1)}, u32[]{:S(2)}) copy-start(bf16[256,1536]{1,0:T(8,128)(2,1)S(1)} %collective-permute-done.4.refs_4_) | copy-start | bytes 2359300
  89.3 21.9 %collective-permute-start.5 = (bf16[256,1536]{1,0:T(8,128)(2,1)S(1)}, bf16[256,1536]{1,0:T(8,128)(2,1)S(1)}, u32[]{:S(2)}, u32[]{:S(2)}) collective-permute-start(bf16[256,1536]{1,0:T(8,128)(2,1)S(1)} %collective-permute-done.4.refs_4_), channel_id=1, source_target_pairs={{1,0},{2,1},{3,2},{5,4},{6,5},{7,6},{9,8},{10,9},{11,10},{13,12},{... | collective-permute-start | bytes 2359304 | tf_op jit(solution)/shard_map/ppermute | solution.py:1933
  105.9 29.3 %copy-start.4 = (bf16[256,1536]{1,0:T(8,128)(2,1)}, bf16[256,1536]{1,0:T(8,128)(2,1)S(1)}, u32[]{:S(2)}) copy-start(bf16[256,1536]{1,0:T(8,128)(2,1)S(1)} %collective-permute-done.2.refs_2_) | copy-start | bytes 2359300
  105.9 45.2 %collective-permute-start.3 = (bf16[256,1536]{1,0:T(8,128)(2,1)S(1)}, bf16[256,1536]{1,0:T(8,128)(2,1)}, u32[]{:S(2)}, u32[]{:S(2)}) collective-permute-start(bf16[256,1536]{1,0:T(8,128)(2,1)S(1)} %collective-permute-done.2.refs_2_), channel_id=1, source_target_pairs={{0,1},{1,2},{2,3},{4,5},{5,6},{6,7},{8,9},{9,10},{10,11},{12,13},{... | collective-permute-start | bytes 2359304 | tf_op jit(solution)/shard_map/ppermute | solution.py:1933
  111.2 24.1 %copy-start.5 = (bf16[256,1536]{1,0:T(8,128)(2,1)}, bf16[256,1536]{1,0:T(8,128)(2,1)S(1)}, u32[]{:S(2)}) copy-start(bf16[256,1536]{1,0:T(8,128)(2,1)S(1)} %collective-permute-done.5.refs_5_) | copy-start | bytes 2359300
  111.2 39.9 %collective-permute-start.6 = (bf16[256,1536]{1,0:T(8,128)(2,1)S(1)}, bf16[256,1536]{1,0:T(8,128)(2,1)}, u32[]{:S(2)}, u32[]{:S(2)}) collective-permute-start(bf16[256,1536]{1,0:T(8,128)(2,1)S(1)} %collective-permute-done.5.refs_5_), channel_id=1, source_target_pairs={{1,0},{2,1},{3,2},{5,4},{6,5},{7,6},{9,8},{10,9},{11,10},{13,12},{... | collective-permute-start | bytes 2359304 | tf_op jit(solution)/shard_map/ppermute | solution.py:1933
  135.3 2.8 collective-permute-start
  138.1 0.7 copy-start.8
  180.9 3.8 %collective-permute-start.7 = (f32[128,768]{1,0:T(8,128)}, f32[128,768]{1,0:T(8,128)S(1)}, u32[]{:S(2)}, u32[]{:S(2)}) collective-permute-start(f32[128,768]{1,0:T(8,128)} %get-tuple-element.152), channel_id=1, source_target_pairs={{4,0},{5,1},{6,2},{7,3},{12,8},{13,9},{14,10},{15,11},{20,16},{21,... | collective-permute-start | bytes 1179656 | tf_op jit(solution)/shard_map/ppermute | solution.py:1933
  184.8 0.7 copy-start.10
  214.1 6.3 %copy-start = (bf16[384,1536]{1,0:T(8,128)(2,1)S(1)}, bf16[384,1536]{1,0:T(8,128)(2,1)}, u32[]{:S(2)}) copy-start(bf16[384,1536]{1,0:T(8,128)(2,1)} %get-tuple-element.126.ws_ref) | copy-start | bytes 3538948
  214.1 29.2 %collective-permute-start.8 = (f32[8,1024]{1,0:T(8,128)}, f32[8,1024]{1,0:T(8,128)S(1)}, u32[]{:S(2)}, u32[]{:S(2)}) collective-permute-start(f32[8,1024]{1,0:T(8,128)} %get-tuple-element.157), channel_id=1, source_target_pairs={{4,0},{5,1},{6,2},{7,3},{12,8},{13,9},{14,10},{15,11},{20,16},{21,... | collective-permute-start | bytes 98312 | tf_op jit(solution)/shard_map/ppermute | solution.py:1933
  230.5 121.0 %collective-permute-start.10 = (bf16[256,1536]{1,0:T(8,128)(2,1)}, bf16[256,1536]{1,0:T(8,128)(2,1)}, u32[]{:S(2)}, u32[]{:S(2)}) collective-permute-start(bf16[256,1536]{1,0:T(8,128)(2,1)} %get-tuple-element.165), channel_id=1, source_target_pairs={{0,2},{1,3},{2,0},{3,1},{4,6},{5,7},{6,4},{7,5},{8,10},{9,11},{10,... | collective-permute-start | bytes 2359304 | tf_op jit(solution)/shard_map/ppermute | solution.py:1938
  232.9 118.6 %collective-permute-start.11 = (bf16[256,1536]{1,0:T(8,128)(2,1)}, bf16[256,1536]{1,0:T(8,128)(2,1)}, u32[]{:S(2)}, u32[]{:S(2)}) collective-permute-start(bf16[256,1536]{1,0:T(8,128)(2,1)} %get-tuple-element.166), channel_id=1, source_target_pairs={{0,3},{1,0},{2,1},{3,2},{4,7},{5,4},{6,5},{7,6},{8,11},{9,8},{10,9... | collective-permute-start | bytes 2359304 | tf_op jit(solution)/shard_map/ppermute | solution.py:1938
  234.3 117.2 %collective-permute-start.9 = (bf16[256,1536]{1,0:T(8,128)(2,1)}, bf16[256,1536]{1,0:T(8,128)(2,1)}, u32[]{:S(2)}, u32[]{:S(2)}) collective-permute-start(bf16[256,1536]{1,0:T(8,128)(2,1)} %get-tuple-element.164), channel_id=1, source_target_pairs={{0,1},{1,2},{2,3},{3,0},{4,5},{5,6},{6,7},{7,4},{8,9},{9,10},{10,1... | collective-permute-start | bytes 2359304 | tf_op jit(solution)/shard_map/ppermute | solution.py:1938
  234.9 8.4 %copy-start.12 = (f32[16,1024]{1,0:T(8,128)S(1)}, f32[16,1024]{1,0:T(8,128)}, u32[]{:S(2)}) copy-start(f32[16,1024]{1,0:T(8,128)} %get-tuple-element.156) | copy-start | bytes 196612
  234.9 8.4 %copy-start.7 = (bf16[1024,1024]{1,0:T(8,128)(2,1)S(1)}, bf16[1024,1024]{1,0:T(8,128)(2,1)}, u32[]{:S(2)}) copy-start(bf16[1024,1024]{1,0:T(8,128)(2,1)} %get-tuple-element.155) | copy-start | bytes 6291460
  243.4 7.6 %copy-start.6 = (bf16[1024,1536]{1,0:T(8,128)(2,1)S(1)}, bf16[1024,1536]{1,0:T(8,128)(2,1)}, u32[]{:S(2)}) copy-start(bf16[1024,1536]{1,0:T(8,128)(2,1)} %get-tuple-element.124.n_ref) | copy-start | bytes 9437188
  243.4 7.6 %copy-start.9 = (bf16[384,1536]{0,1:T(8,128)(2,1)S(1)}, bf16[384,1536]{0,1:T(8,128)(2,1)}, u32[]{:S(2)}) copy-start(bf16[384,1536]{0,1:T(8,128)(2,1)} %copy.54) | copy-start | bytes 3538948
  243.4 7.6 %copy-start.11 = (bf16[1024,128]{1,0:T(8,128)(2,1)S(1)}, bf16[1024,128]{1,0:T(8,128)(2,1)}, u32[]{:S(2)}) copy-start(bf16[1024,128]{1,0:T(8,128)(2,1)} %get-tuple-element.158) | copy-start | bytes 786436
  251.0 12.9 %copy-start.13 = (f32[1536]{0:T(1024)S(1)}, f32[1536]{0:T(1024)}, u32[]{:S(2)}) copy-start(f32[1536]{0:T(1024)} %param.29) | copy-start | bytes 18436
  263.9 7.4 %slice-start = ((s8[5898240]{0:T(1024)(128)(4,1)}), s8[4194304]{0:T(1024)(128)(4,1)S(1)}, s32[]{:S(2)}) async-start(s8[5898240]{0:T(1024)(128)(4,1)} %bitcast.41), calls=%async_computation | async-start | bytes 8388608
  267.3 3.4 copy-start.14
  267.3 3.4 copy-start.16
  267.3 4.1 %slice-start.1 = ((s8[5898240]{0:T(1024)(128)(4,1)}), s8[1703936]{0:T(1024)(128)(4,1)S(1)}, s32[]{:S(2)}) async-start(s8[5898240]{0:T(1024)(128)(4,1)} %bitcast.41), calls=%async_computation.1 | async-start | bytes 3407872
